TPU v7x, 128 devices: a whole 4x4x4 slice. The times are simulated.
128 devices in a mesh: img: 4 (over z), row: 4 (over x_hi, core), col: 8 (over x_lo, y).
Axes of the slice: x: 4 (x_hi: 2, x_lo: 2; x = x_hi * 2 + x_lo), y: 4, z: 4, core: 2. Of those that a mesh axis runs over, the one named last changes fastest.
Arguments:
- edges: int32 [4, 2048, 4096], P('img', 'row', 'col'), parts along dimension 0, may hold values from 0 to 15, as said below
- labels: int32 [4, 2048, 4096], P('img', 'row', 'col'), parts along dimension 0, may hold values from 0 to 2, as said below
- prior: float32 [4, 2048, 4096], P('img', 'row', 'col'), parts along dimension 0, may hold values from 0.05 to 1
- data_weight: float32 [4, 2048, 4096], P('img', 'row', 'col'), parts along dimension 0, may hold values from 0.05 to 1
Outputs:
- labeling: float32 [4, 2048, 4096], P('img', 'row', 'col'), parts along dimension 0
- residual: float32 [4, 2048, 4096], P('img', 'row', 'col'), parts along dimension 0
There are 4 independent parts, one for each index of `img`. A program takes and returns all parts, laid end to end along the dimension named above; each array names one. Nothing has to cross between parts.
Inputs may be any that keep to these rules, and one draw needn't show every extreme that they name: `edges`: bit 1 of a pixel's code marks an edge to the next column, bit 2 to the previous column, bit 4 to the next row, bit 8 to the previous row; both ends of an edge carry it, and no edge leaves the image. `labels`: 0 marks a pixel to be labeled, 1 a foreground seed, 2 a background seed.
All inputs are finite; a program needn't handle non-finite values.
Results may differ from a plain program's by a relative error of at most 0.0002.
Values sent between devices are 32-bit elements; how exact they have to be, the bound alone decides.
No kernel may reach another device: no remote copies, remote signals or barrier semaphores. Data moves between devices by JAX's collectives and lax.ppermute only.
A program may use at most 64 MiB of HBM per device.

v0:
```python
import jax
import jax.numpy as jnp
from jax import lax
from jax.sharding import PartitionSpec as P

ITERS = 8


def with_halo(array, sides, width):
    edges = {}
    for axis, dim in sides:
        count, length = (lax.axis_size(axis), array.shape[dim])
        up = [(i, (i + 1) % count) for i in range(count - 1)]
        last = lax.slice_in_dim(array, length - width, length, axis=dim)
        first = lax.slice_in_dim(array, 0, width, axis=dim)
        edges[dim] = (
            lax.ppermute(last, axis, up),
            lax.ppermute(first, axis, [(b, a) for a, b in up]),
        )
    done = []
    for _, dim in sides:
        low, high = edges[dim]
        around = [(width, width) if d in done else (0, 0) for d in range(array.ndim)]
        array = jnp.concatenate([jnp.pad(low, around), array, jnp.pad(high, around)], axis=dim)
        done.append(dim)
    return array


def from_everyone(array, axis):
    count = lax.axis_size(axis)
    return lax.all_to_all(
        jnp.broadcast_to(array[None], (count, *array.shape)), axis, 0, 0, tiled=True
    )


def of_everyone(array, axis):
    return from_everyone(array, axis).sum(axis=0)


def together(arrays, axis):
    flat, at, finished = (jnp.concatenate([a.reshape(-1) for a in arrays]), 0, [])
    so_far = of_everyone(flat, axis)
    for a in arrays:
        finished.append(so_far[at : at + a.size].reshape(a.shape))
        at += a.size
    return tuple(finished)


def neighbours(field, right, left, down, upper):
    padded = with_halo(field, (("row", 1), ("col", 2)), 1)
    return (
        right * padded[:, 1:-1, 2:]
        + left * padded[:, 1:-1, :-2]
        + down * padded[:, 2:, 1:-1]
        + upper * padded[:, :-2, 1:-1]
    )


def paired_sums(residual, image_v):
    return together(
        (jnp.sum(residual * residual, axis=(1, 2)), jnp.sum(residual * image_v, axis=(1, 2))),
        ("row", "col"),
    )


def per_device(edges, labels, prior, data_weight):
    right = (edges % 2).astype(jnp.float32)
    left = (edges // 2 % 2).astype(jnp.float32)
    down = (edges // 4 % 2).astype(jnp.float32)
    upper = (edges // 8 % 2).astype(jnp.float32)
    degree = right + left + down + upper
    free = (labels == 0).astype(jnp.float32)
    anchor = (labels == 1).astype(jnp.float32)
    diag_term = degree + data_weight

    def operate(field):
        return free * (diag_term * field - neighbours(field, right, left, down, upper))

    rhs = free * (data_weight * prior + neighbours(anchor, right, left, down, upper))
    solution = jnp.zeros_like(rhs)
    residual = rhs
    image_v = operate(residual)
    norm_now, product = paired_sums(residual, image_v)
    alpha = norm_now / product
    direction = residual
    along = image_v
    for step in range(ITERS):
        solution = solution + alpha[:, None, None] * direction
        residual = residual - alpha[:, None, None] * along
        if step + 1 < ITERS:
            image_v = operate(residual)
            norm_next, product = paired_sums(residual, image_v)
            ratio = norm_next / norm_now
            alpha = norm_next / (product - ratio * norm_next / alpha)
            direction = residual + ratio[:, None, None] * direction
            along = image_v + ratio[:, None, None] * along
            norm_now = norm_next
    return (anchor + solution, residual)


def solution(mesh):
    return jax.shard_map(
        per_device,
        mesh=mesh,
        in_specs=(
            P("img", "row", "col"),
            P("img", "row", "col"),
            P("img", "row", "col"),
            P("img", "row", "col"),
        ),
        out_specs=(P("img", "row", "col"), P("img", "row", "col")),
        check_vma=False,
    )
```

profile of v0, /device:TPU:1, one launch (start us, length us, event | category | flops | bytes accessed | tf_op | source)
XLA Modules:
  0.0 404.3 jit_solution(9970603584264286101)
XLA Ops:
  2.2 3.4 collective-permute-start.1
  5.6 4.7 %collective-permute-start = (f32[1,1,512]{2,1,0:T(1,128)S(1)}, f32[1,1,512]{2,1,0:T(1,128)S(1)}, u32[]{:S(2)}, u32[]{:S(2)}) collective-permute-start(f32[1,1,512]{2,1,0:T(1,128)S(1)} %get-tuple-element.69), channel_id=1, source_target_pairs={{0,8},{8,16},{16,24},{1,9},{9,17},{17,25},{2,10},{10,18},{18,26},{... | collective-permute-start | bytes 6152 | tf_op jit(solution)/shard_map/ppermute | solution.py:17
  11.7 4.0 collective-permute-start.3
  15.8 2.8 collective-permute-done.2
  18.6 1.8 collective-permute-done.3
  20.3 5.7 %fusion.100 = (f32[1,512,512]{2,1,0:T(8,128)S(1)}, pred[1,512,512]{2,1,0:T(8,128)(4,1)S(1)}) fusion(f32[1,512,512]{2,1,0:T(8,128)S(1)} %compare_convert_fusion, f32[1,1,512]{2,1,0:T(1,128)S(1)} %collective-permute-done, f32[1,1,512]{2,1,0:T(1,128)S(1)} %collective-permute-done.1, f32[1,512,1]{2,1,0:T(8,128)S(1)} %collective-permute-done.3, ...), kind=kLoop, calls=%fused_computation.185 | loop fusion | flops 26476544 | bytes 6561792 | tf_op jit(solution)/shard_map/mul | solution.py:79
  26.2 1.9 collective-permute-start.5
  28.2 5.1 %collective-permute-start.4 = (f32[1,1,512]{2,1,0:T(1,128)S(1)}, f32[1,1,512]{2,1,0:T(1,128)S(1)}, u32[]{:S(2)}, u32[]{:S(2)}) collective-permute-start(f32[1,1,512]{2,1,0:T(1,128)S(1)} %get-tuple-element.65), channel_id=1, source_target_pairs={{0,8},{8,16},{16,24},{1,9},{9,17},{17,25},{2,10},{10,18},{18,26},{... | collective-permute-start | bytes 6152 | tf_op jit(solution)/shard_map/ppermute | solution.py:17
  34.6 4.5 %collective-permute-start.7 = (f32[1,512,1]{2,1,0:T(8,128)S(1)}, f32[1,512,1]{2,1,0:T(8,128)S(1)}, u32[]{:S(2)}, u32[]{:S(2)}) collective-permute-start(f32[1,512,1]{2,1,0:T(8,128)S(1)} %get-tuple-element.63), channel_id=1, source_target_pairs={{0,1},{1,2},{2,3},{3,4},{4,5},{5,6},{6,7},{8,9},{9,10},{10,11},{11... | collective-permute-start | bytes 6152 | tf_op jit(solution)/shard_map/ppermute | solution.py:17
  39.1 2.0 collective-permute-done.6
  41.2 1.8 collective-permute-done.7
  42.9 6.3 %multiply_reduce_fusion.15 = (f32[]{:T(128)}, f32[]{:T(128)}, f32[1,512,512]{2,1,0:T(8,128)}) fusion(f32[1,512,512]{2,1,0:T(8,128)S(1)} %get-tuple-element.32, pred[1,512,512]{2,1,0:T(8,128)(4,1)S(1)} %get-tuple-element.33, f32[1,1,512]{2,1,0:T(1,128)S(1)} %collective-permute-done.4, f32[1,1,512]{2,1,0:T(1,128)S(1)} %collective-permute-done.5, ...), kind=kLoop, calls=%fused_computation.233 | loop fusion | flops 28311552 | bytes 4464648 | tf_op jit(solution)/shard_map/reduce_sum | solution.py:61
  50.5 17.3 %all_to_all.48 = f32[32,1,2]{2,1,0:T(1,128)S(1)} all-to-all(f32[32,1,2]{2,1,0:T(1,128)S(1)} %broadcast_in_dim.16), channel_id=1, replica_groups=mesh['img'=4,'row'=4,'col'=8] {'row','col'}, dimensions={0} | all-to-all | bytes 512 | tf_op jit(solution)/shard_map/all_to_all | solution.py:31
  69.8 1.8 multiply_subtract_fusion.7
  71.7 2.6 collective-permute-start.9
  74.3 4.5 %collective-permute-start.8 = (f32[1,1,512]{2,1,0:T(1,128)S(1)}, f32[1,1,512]{2,1,0:T(1,128)S(1)}, u32[]{:S(2)}, u32[]{:S(2)}) collective-permute-start(f32[1,1,512]{2,1,0:T(1,128)S(1)} %get-tuple-element.61), channel_id=1, source_target_pairs={{0,8},{8,16},{16,24},{1,9},{9,17},{17,25},{2,10},{10,18},{18,26},{... | collective-permute-start | bytes 6152 | tf_op jit(solution)/shard_map/ppermute | solution.py:17
  80.1 4.0 collective-permute-start.11
  84.2 3.0 collective-permute-done.10
  88.9 6.3 %multiply_reduce_fusion.13 = (f32[]{:T(128)}, f32[]{:T(128)}, f32[1,512,512]{2,1,0:T(8,128)}) fusion(f32[1,512,512]{2,1,0:T(8,128)S(1)} %multiply_subtract_fusion.7, pred[1,512,512]{2,1,0:T(8,128)(4,1)S(1)} %get-tuple-element.33, f32[1,1,512]{2,1,0:T(1,128)S(1)} %collective-permute-done.8, f32[1,1,512]{2,1,0:T(1,128)S(1)} %collective-permute-done.9, ...), kind=kLoop, calls=%fused_computation.229 | loop fusion | flops 28311552 | bytes 4464648 | tf_op jit(solution)/shard_map/reduce_sum | solution.py:61
  96.5 13.2 %all_to_all.49 = f32[32,1,2]{2,1,0:T(1,128)S(1)} all-to-all(f32[32,1,2]{2,1,0:T(1,128)S(1)} %broadcast_in_dim.17), channel_id=1, replica_groups=mesh['img'=4,'row'=4,'col'=8] {'row','col'}, dimensions={0} | all-to-all | bytes 512 | tf_op jit(solution)/shard_map/all_to_all | solution.py:31
  114.6 1.9 multiply_subtract_fusion.6
  116.6 2.6 collective-permute-start.13
  119.2 4.5 %collective-permute-start.12 = (f32[1,1,512]{2,1,0:T(1,128)S(1)}, f32[1,1,512]{2,1,0:T(1,128)S(1)}, u32[]{:S(2)}, u32[]{:S(2)}) collective-permute-start(f32[1,1,512]{2,1,0:T(1,128)S(1)} %get-tuple-element.57), channel_id=1, source_target_pairs={{0,8},{8,16},{16,24},{1,9},{9,17},{17,25},{2,10},{10,18},{18,26},{... | collective-permute-start | bytes 6152 | tf_op jit(solution)/shard_map/ppermute | solution.py:17
  125.0 4.3 %collective-permute-start.15 = (f32[1,512,1]{2,1,0:T(8,128)S(1)}, f32[1,512,1]{2,1,0:T(8,128)S(1)}, u32[]{:S(2)}, u32[]{:S(2)}) collective-permute-start(f32[1,512,1]{2,1,0:T(8,128)S(1)} %get-tuple-element.55), channel_id=1, source_target_pairs={{0,1},{1,2},{2,3},{3,4},{4,5},{5,6},{6,7},{8,9},{9,10},{10,11},{11... | collective-permute-start | bytes 6152 | tf_op jit(solution)/shard_map/ppermute | solution.py:17
  129.3 2.7 collective-permute-done.14
  133.8 6.3 %multiply_reduce_fusion.11 = (f32[]{:T(128)}, f32[]{:T(128)}, f32[1,512,512]{2,1,0:T(8,128)}) fusion(f32[1,512,512]{2,1,0:T(8,128)S(1)} %multiply_subtract_fusion.6, pred[1,512,512]{2,1,0:T(8,128)(4,1)S(1)} %get-tuple-element.33, f32[1,1,512]{2,1,0:T(1,128)S(1)} %collective-permute-done.12, f32[1,1,512]{2,1,0:T(1,128)S(1)} %collective-permute-done.13, ...), kind=kLoop, calls=%fused_computation.225 | loop fusion | flops 28311552 | bytes 4464648 | tf_op jit(solution)/shard_map/reduce_sum | solution.py:61
  141.6 13.2 %all_to_all.50 = f32[32,1,2]{2,1,0:T(1,128)S(1)} all-to-all(f32[32,1,2]{2,1,0:T(1,128)S(1)} %broadcast_in_dim.18), channel_id=1, replica_groups=mesh['img'=4,'row'=4,'col'=8] {'row','col'}, dimensions={0} | all-to-all | bytes 512 | tf_op jit(solution)/shard_map/all_to_all | solution.py:31
  159.1 3.6 multiply_subtract_fusion.5
  162.9 2.6 collective-permute-start.17
  165.5 4.5 %collective-permute-start.16 = (f32[1,1,512]{2,1,0:T(1,128)S(1)}, f32[1,1,512]{2,1,0:T(1,128)S(1)}, u32[]{:S(2)}, u32[]{:S(2)}) collective-permute-start(f32[1,1,512]{2,1,0:T(1,128)S(1)} %get-tuple-element.53), channel_id=1, source_target_pairs={{0,8},{8,16},{16,24},{1,9},{9,17},{17,25},{2,10},{10,18},{18,26},{... | collective-permute-start | bytes 6152 | tf_op jit(solution)/shard_map/ppermute | solution.py:17
  171.3 4.0 collective-permute-start.19
  175.4 3.0 collective-permute-done.18
  180.1 6.3 %multiply_reduce_fusion.9 = (f32[]{:T(128)}, f32[]{:T(128)}, f32[1,512,512]{2,1,0:T(8,128)}) fusion(f32[1,512,512]{2,1,0:T(8,128)S(1)} %get-tuple-element.27, pred[1,512,512]{2,1,0:T(8,128)(4,1)S(1)} %get-tuple-element.33, f32[1,1,512]{2,1,0:T(1,128)S(1)} %collective-permute-done.16, f32[1,1,512]{2,1,0:T(1,128)S(1)} %collective-permute-done.17, ...), kind=kLoop, calls=%fused_computation.221 | loop fusion | flops 28311552 | bytes 4464648 | tf_op jit(solution)/shard_map/reduce_sum | solution.py:61
  187.6 13.2 %all_to_all.51 = f32[32,1,2]{2,1,0:T(1,128)S(1)} all-to-all(f32[32,1,2]{2,1,0:T(1,128)S(1)} %broadcast_in_dim.19), channel_id=1, replica_groups=mesh['img'=4,'row'=4,'col'=8] {'row','col'}, dimensions={0} | all-to-all | bytes 512 | tf_op jit(solution)/shard_map/all_to_all | solution.py:31
  205.3 2.2 multiply_subtract_fusion.4
  207.7 2.6 collective-permute-start.21
  210.3 4.5 %collective-permute-start.20 = (f32[1,1,512]{2,1,0:T(1,128)S(1)}, f32[1,1,512]{2,1,0:T(1,128)S(1)}, u32[]{:S(2)}, u32[]{:S(2)}) collective-permute-start(f32[1,1,512]{2,1,0:T(1,128)S(1)} %get-tuple-element.49), channel_id=1, source_target_pairs={{0,8},{8,16},{16,24},{1,9},{9,17},{17,25},{2,10},{10,18},{18,26},{... | collective-permute-start | bytes 6152 | tf_op jit(solution)/shard_map/ppermute | solution.py:17
  216.1 4.0 collective-permute-start.23
  220.1 3.0 collective-permute-done.22
  224.9 6.3 %multiply_reduce_fusion.7 = (f32[]{:T(128)}, f32[]{:T(128)}, f32[1,512,512]{2,1,0:T(8,128)}) fusion(f32[1,512,512]{2,1,0:T(8,128)S(1)} %multiply_subtract_fusion.4, pred[1,512,512]{2,1,0:T(8,128)(4,1)S(1)} %get-tuple-element.33, f32[1,1,512]{2,1,0:T(1,128)S(1)} %collective-permute-done.20, f32[1,1,512]{2,1,0:T(1,128)S(1)} %collective-permute-done.21, ...), kind=kLoop, calls=%fused_computation.217 | loop fusion | flops 28311552 | bytes 4464648 | tf_op jit(solution)/shard_map/reduce_sum | solution.py:61
  232.4 13.2 %all_to_all.52 = f32[32,1,2]{2,1,0:T(1,128)S(1)} all-to-all(f32[32,1,2]{2,1,0:T(1,128)S(1)} %broadcast_in_dim.20), channel_id=1, replica_groups=mesh['img'=4,'row'=4,'col'=8] {'row','col'}, dimensions={0} | all-to-all | bytes 512 | tf_op jit(solution)/shard_map/all_to_all | solution.py:31
  249.9 3.6 multiply_subtract_fusion.3
  253.7 2.6 collective-permute-start.25
  256.3 4.5 %collective-permute-start.24 = (f32[1,1,512]{2,1,0:T(1,128)S(1)}, f32[1,1,512]{2,1,0:T(1,128)S(1)}, u32[]{:S(2)}, u32[]{:S(2)}) collective-permute-start(f32[1,1,512]{2,1,0:T(1,128)S(1)} %get-tuple-element.45), channel_id=1, source_target_pairs={{0,8},{8,16},{16,24},{1,9},{9,17},{17,25},{2,10},{10,18},{18,26},{... | collective-permute-start | bytes 6152 | tf_op jit(solution)/shard_map/ppermute | solution.py:17
  260.8 10.7 %collective-permute-start.26 = (f32[1,512,1]{2,1,0:T(8,128)S(1)}, f32[1,512,1]{2,1,0:T(8,128)S(1)}, u32[]{:S(2)}, u32[]{:S(2)}) collective-permute-start(f32[1,512,1]{2,1,0:T(8,128)S(1)} %get-tuple-element.42), channel_id=1, source_target_pairs={{1,0},{2,1},{3,2},{4,3},{5,4},{6,5},{7,6},{9,8},{10,9},{11,10},{12... | collective-permute-start | bytes 6152 | tf_op jit(solution)/shard_map/ppermute | solution.py:18
  271.5 4.0 collective-permute-start.27
  275.6 3.0 collective-permute-done.26
  280.3 6.3 %multiply_reduce_fusion.5 = (f32[]{:T(128)}, f32[]{:T(128)}, f32[1,512,512]{2,1,0:T(8,128)}) fusion(f32[1,512,512]{2,1,0:T(8,128)S(1)} %get-tuple-element.23, pred[1,512,512]{2,1,0:T(8,128)(4,1)S(1)} %get-tuple-element.33, f32[1,1,512]{2,1,0:T(1,128)S(1)} %collective-permute-done.24, f32[1,1,512]{2,1,0:T(1,128)S(1)} %collective-permute-done.25, ...), kind=kLoop, calls=%fused_computation.213 | loop fusion | flops 28311552 | bytes 4464648 | tf_op jit(solution)/shard_map/reduce_sum | solution.py:61
  288.0 13.2 %all_to_all.53 = f32[32,1,2]{2,1,0:T(1,128)S(1)} all-to-all(f32[32,1,2]{2,1,0:T(1,128)S(1)} %broadcast_in_dim.21), channel_id=1, replica_groups=mesh['img'=4,'row'=4,'col'=8] {'row','col'}, dimensions={0} | all-to-all | bytes 512 | tf_op jit(solution)/shard_map/all_to_all | solution.py:31
  305.7 2.2 multiply_subtract_fusion.2
  308.1 2.6 collective-permute-start.29
  310.7 4.5 %collective-permute-start.28 = (f32[1,1,512]{2,1,0:T(1,128)S(1)}, f32[1,1,512]{2,1,0:T(1,128)S(1)}, u32[]{:S(2)}, u32[]{:S(2)}) collective-permute-start(f32[1,1,512]{2,1,0:T(1,128)S(1)} %get-tuple-element.41), channel_id=1, source_target_pairs={{0,8},{8,16},{16,24},{1,9},{9,17},{17,25},{2,10},{10,18},{18,26},{... | collective-permute-start | bytes 6152 | tf_op jit(solution)/shard_map/ppermute | solution.py:17
  316.5 4.0 collective-permute-start.31
  320.5 3.0 collective-permute-done.30
  325.3 6.3 %multiply_reduce_fusion.3 = (f32[]{:T(128)}, f32[]{:T(128)}, f32[1,512,512]{2,1,0:T(8,128)}) fusion(f32[1,512,512]{2,1,0:T(8,128)S(1)} %multiply_subtract_fusion.2, pred[1,512,512]{2,1,0:T(8,128)(4,1)S(1)} %get-tuple-element.33, f32[1,1,512]{2,1,0:T(1,128)S(1)} %collective-permute-done.28, f32[1,1,512]{2,1,0:T(1,128)S(1)} %collective-permute-done.29, ...), kind=kLoop, calls=%fused_computation.209 | loop fusion | flops 28311552 | bytes 4464648 | tf_op jit(solution)/shard_map/reduce_sum | solution.py:61
  332.8 13.2 %all_to_all.54 = f32[32,1,2]{2,1,0:T(1,128)S(1)} all-to-all(f32[32,1,2]{2,1,0:T(1,128)S(1)} %broadcast_in_dim.22), channel_id=1, replica_groups=mesh['img'=4,'row'=4,'col'=8] {'row','col'}, dimensions={0} | all-to-all | bytes 512 | tf_op jit(solution)/shard_map/all_to_all | solution.py:31
  350.7 3.7 multiply_subtract_fusion.1
  354.6 2.6 collective-permute-start.33
  357.2 4.5 %collective-permute-start.32 = (f32[1,1,512]{2,1,0:T(1,128)S(1)}, f32[1,1,512]{2,1,0:T(1,128)S(1)}, u32[]{:S(2)}, u32[]{:S(2)}) collective-permute-start(f32[1,1,512]{2,1,0:T(1,128)S(1)} %get-tuple-element.37), channel_id=1, source_target_pairs={{0,8},{8,16},{16,24},{1,9},{9,17},{17,25},{2,10},{10,18},{18,26},{... | collective-permute-start | bytes 6152 | tf_op jit(solution)/shard_map/ppermute | solution.py:17
  362.9 4.0 collective-permute-start.35
  367.0 3.0 collective-permute-done.34
  371.7 6.3 %multiply_reduce_fusion.1 = (f32[]{:T(128)}, f32[]{:T(128)}, f32[1,512,512]{2,1,0:T(8,128)}) fusion(f32[1,512,512]{2,1,0:T(8,128)S(1)} %get-tuple-element.19, pred[1,512,512]{2,1,0:T(8,128)(4,1)S(1)} %get-tuple-element.33, f32[1,1,512]{2,1,0:T(1,128)S(1)} %collective-permute-done.32, f32[1,1,512]{2,1,0:T(1,128)S(1)} %collective-permute-done.33, ...), kind=kLoop, calls=%fused_computation.205 | loop fusion | flops 28311552 | bytes 4464648 | tf_op jit(solution)/shard_map/reduce_sum | solution.py:61
  379.4 13.2 %all_to_all.55 = f32[32,1,2]{2,1,0:T(1,128)S(1)} all-to-all(f32[32,1,2]{2,1,0:T(1,128)S(1)} %broadcast_in_dim.23), channel_id=1, replica_groups=mesh['img'=4,'row'=4,'col'=8] {'row','col'}, dimensions={0} | all-to-all | bytes 512 | tf_op jit(solution)/shard_map/all_to_all | solution.py:31
  397.0 5.7 %add_add_fusion = f32[1,512,512]{2,1,0:T(8,128)} fusion(f32[1,512,512]{2,1,0:T(8,128)} %copy-done.7, f32[1,512,512]{2,1,0:T(8,128)} %copy-done.6, f32[1,512,512]{2,1,0:T(8,128)} %copy-done.5, f32[1,512,512]{2,1,0:T(8,128)} %copy-done.4, f32[1,512,512]{2,1,0:T(8,128)} %copy-done.3, f32[1,512,512]{2,1,0:T(8,128)} %copy-done.2, ...), kind=kLoop, calls=%fused_computation.203 | loop fusion | flops 8388608 | bytes 10485820 | tf_op jit(solution)/shard_map/add | solution.py:98
  (111 shorter events, 42.7 us)
Async XLA Ops:
  0.6 19.7 %copy-start.1 = (s32[1,512,512]{2,1,0:T(8,128)S(1)}, s32[1,512,512]{2,1,0:T(8,128)}, u32[]{:S(2)}) copy-start(s32[1,512,512]{2,1,0:T(8,128)} %param.4) | copy-start | bytes 3145732
  0.6 19.7 %copy-start.10 = (s32[1,512,512]{2,1,0:T(8,128)S(1)}, s32[1,512,512]{2,1,0:T(8,128)}, u32[]{:S(2)}) copy-start(s32[1,512,512]{2,1,0:T(8,128)} %param.5) | copy-start | bytes 3145732
  2.1 18.2 %copy-start = (f32[1,512,512]{2,1,0:T(8,128)S(1)}, f32[1,512,512]{2,1,0:T(8,128)}, u32[]{:S(2)}) copy-start(f32[1,512,512]{2,1,0:T(8,128)} %param.7) | copy-start | bytes 3145732
  2.2 13.6 %collective-permute-start.1 = (f32[1,1,512]{2,1,0:T(1,128)S(1)}, f32[1,1,512]{2,1,0:T(1,128)S(1)}, u32[]{:S(2)}, u32[]{:S(2)}) collective-permute-start(f32[1,1,512]{2,1,0:T(1,128)S(1)} %get-tuple-element.68), channel_id=1, source_target_pairs={{8,0},{16,8},{24,16},{9,1},{17,9},{25,17},{10,2},{18,10},{26,18},{... | collective-permute-start | bytes 6152 | tf_op jit(solution)/shard_map/ppermute | solution.py:18
  5.6 10.1 %collective-permute-start = (f32[1,1,512]{2,1,0:T(1,128)S(1)}, f32[1,1,512]{2,1,0:T(1,128)S(1)}, u32[]{:S(2)}, u32[]{:S(2)}) collective-permute-start(f32[1,1,512]{2,1,0:T(1,128)S(1)} %get-tuple-element.69), channel_id=1, source_target_pairs={{0,8},{8,16},{16,24},{1,9},{9,17},{17,25},{2,10},{10,18},{18,26},{... | collective-permute-start | bytes 6152 | tf_op jit(solution)/shard_map/ppermute | solution.py:17
  10.4 8.1 %collective-permute-start.2 = (f32[1,512,1]{2,1,0:T(8,128)S(1)}, f32[1,512,1]{2,1,0:T(8,128)S(1)}, u32[]{:S(2)}, u32[]{:S(2)}) collective-permute-start(f32[1,512,1]{2,1,0:T(8,128)S(1)} %get-tuple-element.66), channel_id=1, source_target_pairs={{1,0},{2,1},{3,2},{4,3},{5,4},{6,5},{7,6},{9,8},{10,9},{11,10},{12... | collective-permute-start | bytes 6152 | tf_op jit(solution)/shard_map/ppermute | solution.py:18
  11.7 8.6 %collective-permute-start.3 = (f32[1,512,1]{2,1,0:T(8,128)S(1)}, f32[1,512,1]{2,1,0:T(8,128)S(1)}, u32[]{:S(2)}, u32[]{:S(2)}) collective-permute-start(f32[1,512,1]{2,1,0:T(8,128)S(1)} %get-tuple-element.67), channel_id=1, source_target_pairs={{0,1},{1,2},{2,3},{3,4},{4,5},{5,6},{6,7},{8,9},{9,10},{10,11},{11... | collective-permute-start | bytes 6152 | tf_op jit(solution)/shard_map/ppermute | solution.py:17
  26.1 23.1 %copy-start.9 = (f32[1,512,512]{2,1,0:T(8,128)}, f32[1,512,512]{2,1,0:T(8,128)S(1)}, u32[]{:S(2)}) copy-start(f32[1,512,512]{2,1,0:T(8,128)S(1)} %get-tuple-element.32) | copy-start | bytes 3145732
  26.2 12.9 %collective-permute-start.5 = (f32[1,1,512]{2,1,0:T(1,128)S(1)}, f32[1,1,512]{2,1,0:T(1,128)S(1)}, u32[]{:S(2)}, u32[]{:S(2)}) collective-permute-start(f32[1,1,512]{2,1,0:T(1,128)S(1)} %get-tuple-element.64), channel_id=1, source_target_pairs={{8,0},{16,8},{24,16},{9,1},{17,9},{25,17},{10,2},{18,10},{26,18},{... | collective-permute-start | bytes 6152 | tf_op jit(solution)/shard_map/ppermute | solution.py:18
  28.2 10.9 %collective-permute-start.4 = (f32[1,1,512]{2,1,0:T(1,128)S(1)}, f32[1,1,512]{2,1,0:T(1,128)S(1)}, u32[]{:S(2)}, u32[]{:S(2)}) collective-permute-start(f32[1,1,512]{2,1,0:T(1,128)S(1)} %get-tuple-element.65), channel_id=1, source_target_pairs={{0,8},{8,16},{16,24},{1,9},{9,17},{17,25},{2,10},{10,18},{18,26},{... | collective-permute-start | bytes 6152 | tf_op jit(solution)/shard_map/ppermute | solution.py:17
  33.3 7.8 %collective-permute-start.6 = (f32[1,512,1]{2,1,0:T(8,128)S(1)}, f32[1,512,1]{2,1,0:T(8,128)S(1)}, u32[]{:S(2)}, u32[]{:S(2)}) collective-permute-start(f32[1,512,1]{2,1,0:T(8,128)S(1)} %get-tuple-element.62), channel_id=1, source_target_pairs={{1,0},{2,1},{3,2},{4,3},{5,4},{6,5},{7,6},{9,8},{10,9},{11,10},{12... | collective-permute-start | bytes 6152 | tf_op jit(solution)/shard_map/ppermute | solution.py:18
  34.6 8.3 %collective-permute-start.7 = (f32[1,512,1]{2,1,0:T(8,128)S(1)}, f32[1,512,1]{2,1,0:T(8,128)S(1)}, u32[]{:S(2)}, u32[]{:S(2)}) collective-permute-start(f32[1,512,1]{2,1,0:T(8,128)S(1)} %get-tuple-element.63), channel_id=1, source_target_pairs={{0,1},{1,2},{2,3},{3,4},{4,5},{5,6},{6,7},{8,9},{9,10},{10,11},{11... | collective-permute-start | bytes 6152 | tf_op jit(solution)/shard_map/ppermute | solution.py:17
  71.7 12.4 %collective-permute-start.9 = (f32[1,1,512]{2,1,0:T(1,128)S(1)}, f32[1,1,512]{2,1,0:T(1,128)S(1)}, u32[]{:S(2)}, u32[]{:S(2)}) collective-permute-start(f32[1,1,512]{2,1,0:T(1,128)S(1)} %get-tuple-element.60), channel_id=1, source_target_pairs={{8,0},{16,8},{24,16},{9,1},{17,9},{25,17},{10,2},{18,10},{26,18},{... | collective-permute-start | bytes 6152 | tf_op jit(solution)/shard_map/ppermute | solution.py:18
  74.3 9.8 %collective-permute-start.8 = (f32[1,1,512]{2,1,0:T(1,128)S(1)}, f32[1,1,512]{2,1,0:T(1,128)S(1)}, u32[]{:S(2)}, u32[]{:S(2)}) collective-permute-start(f32[1,1,512]{2,1,0:T(1,128)S(1)} %get-tuple-element.61), channel_id=1, source_target_pairs={{0,8},{8,16},{16,24},{1,9},{9,17},{17,25},{2,10},{10,18},{18,26},{... | collective-permute-start | bytes 6152 | tf_op jit(solution)/shard_map/ppermute | solution.py:17
  78.8 8.3 %collective-permute-start.10 = (f32[1,512,1]{2,1,0:T(8,128)S(1)}, f32[1,512,1]{2,1,0:T(8,128)S(1)}, u32[]{:S(2)}, u32[]{:S(2)}) collective-permute-start(f32[1,512,1]{2,1,0:T(8,128)S(1)} %get-tuple-element.58), channel_id=1, source_target_pairs={{1,0},{2,1},{3,2},{4,3},{5,4},{6,5},{7,6},{9,8},{10,9},{11,10},{12... | collective-permute-start | bytes 6152 | tf_op jit(solution)/shard_map/ppermute | solution.py:18
  80.1 8.8 %collective-permute-start.11 = (f32[1,512,1]{2,1,0:T(8,128)S(1)}, f32[1,512,1]{2,1,0:T(8,128)S(1)}, u32[]{:S(2)}, u32[]{:S(2)}) collective-permute-start(f32[1,512,1]{2,1,0:T(8,128)S(1)} %get-tuple-element.59), channel_id=1, source_target_pairs={{0,1},{1,2},{2,3},{3,4},{4,5},{5,6},{6,7},{8,9},{9,10},{10,11},{11... | collective-permute-start | bytes 6152 | tf_op jit(solution)/shard_map/ppermute | solution.py:17
  116.5 23.7 %copy-start.2 = (f32[1,512,512]{2,1,0:T(8,128)}, f32[1,512,512]{2,1,0:T(8,128)S(1)}, u32[]{:S(2)}) copy-start(f32[1,512,512]{2,1,0:T(8,128)S(1)} %multiply_subtract_fusion.6) | copy-start | bytes 3145732
  116.6 12.7 %collective-permute-start.13 = (f32[1,1,512]{2,1,0:T(1,128)S(1)}, f32[1,1,512]{2,1,0:T(1,128)S(1)}, u32[]{:S(2)}, u32[]{:S(2)}) collective-permute-start(f32[1,1,512]{2,1,0:T(1,128)S(1)} %get-tuple-element.56), channel_id=1, source_target_pairs={{8,0},{16,8},{24,16},{9,1},{17,9},{25,17},{10,2},{18,10},{26,18},{... | collective-permute-start | bytes 6152 | tf_op jit(solution)/shard_map/ppermute | solution.py:18
  119.2 10.1 %collective-permute-start.12 = (f32[1,1,512]{2,1,0:T(1,128)S(1)}, f32[1,1,512]{2,1,0:T(1,128)S(1)}, u32[]{:S(2)}, u32[]{:S(2)}) collective-permute-start(f32[1,1,512]{2,1,0:T(1,128)S(1)} %get-tuple-element.57), channel_id=1, source_target_pairs={{0,8},{8,16},{16,24},{1,9},{9,17},{17,25},{2,10},{10,18},{18,26},{... | collective-permute-start | bytes 6152 | tf_op jit(solution)/shard_map/ppermute | solution.py:17
  123.7 8.3 %collective-permute-start.14 = (f32[1,512,1]{2,1,0:T(8,128)S(1)}, f32[1,512,1]{2,1,0:T(8,128)S(1)}, u32[]{:S(2)}, u32[]{:S(2)}) collective-permute-start(f32[1,512,1]{2,1,0:T(8,128)S(1)} %get-tuple-element.54), channel_id=1, source_target_pairs={{1,0},{2,1},{3,2},{4,3},{5,4},{6,5},{7,6},{9,8},{10,9},{11,10},{12... | collective-permute-start | bytes 6152 | tf_op jit(solution)/shard_map/ppermute | solution.py:18
  125.0 8.8 %collective-permute-start.15 = (f32[1,512,1]{2,1,0:T(8,128)S(1)}, f32[1,512,1]{2,1,0:T(8,128)S(1)}, u32[]{:S(2)}, u32[]{:S(2)}) collective-permute-start(f32[1,512,1]{2,1,0:T(8,128)S(1)} %get-tuple-element.55), channel_id=1, source_target_pairs={{0,1},{1,2},{2,3},{3,4},{4,5},{5,6},{6,7},{8,9},{9,10},{10,11},{11... | collective-permute-start | bytes 6152 | tf_op jit(solution)/shard_map/ppermute | solution.py:17
  162.8 23.6 %copy-start.3 = (f32[1,512,512]{2,1,0:T(8,128)}, f32[1,512,512]{2,1,0:T(8,128)S(1)}, u32[]{:S(2)}) copy-start(f32[1,512,512]{2,1,0:T(8,128)S(1)} %get-tuple-element.27) | copy-start | bytes 3145732
  162.9 12.4 %collective-permute-start.17 = (f32[1,1,512]{2,1,0:T(1,128)S(1)}, f32[1,1,512]{2,1,0:T(1,128)S(1)}, u32[]{:S(2)}, u32[]{:S(2)}) collective-permute-start(f32[1,1,512]{2,1,0:T(1,128)S(1)} %get-tuple-element.52), channel_id=1, source_target_pairs={{8,0},{16,8},{24,16},{9,1},{17,9},{25,17},{10,2},{18,10},{26,18},{... | collective-permute-start | bytes 6152 | tf_op jit(solution)/shard_map/ppermute | solution.py:18
  165.5 9.8 %collective-permute-start.16 = (f32[1,1,512]{2,1,0:T(1,128)S(1)}, f32[1,1,512]{2,1,0:T(1,128)S(1)}, u32[]{:S(2)}, u32[]{:S(2)}) collective-permute-start(f32[1,1,512]{2,1,0:T(1,128)S(1)} %get-tuple-element.53), channel_id=1, source_target_pairs={{0,8},{8,16},{16,24},{1,9},{9,17},{17,25},{2,10},{10,18},{18,26},{... | collective-permute-start | bytes 6152 | tf_op jit(solution)/shard_map/ppermute | solution.py:17
  170.0 8.3 %collective-permute-start.18 = (f32[1,512,1]{2,1,0:T(8,128)S(1)}, f32[1,512,1]{2,1,0:T(8,128)S(1)}, u32[]{:S(2)}, u32[]{:S(2)}) collective-permute-start(f32[1,512,1]{2,1,0:T(8,128)S(1)} %get-tuple-element.50), channel_id=1, source_target_pairs={{1,0},{2,1},{3,2},{4,3},{5,4},{6,5},{7,6},{9,8},{10,9},{11,10},{12... | collective-permute-start | bytes 6152 | tf_op jit(solution)/shard_map/ppermute | solution.py:18
  171.3 8.8 %collective-permute-start.19 = (f32[1,512,1]{2,1,0:T(8,128)S(1)}, f32[1,512,1]{2,1,0:T(8,128)S(1)}, u32[]{:S(2)}, u32[]{:S(2)}) collective-permute-start(f32[1,512,1]{2,1,0:T(8,128)S(1)} %get-tuple-element.51), channel_id=1, source_target_pairs={{0,1},{1,2},{2,3},{3,4},{4,5},{5,6},{6,7},{8,9},{9,10},{10,11},{11... | collective-permute-start | bytes 6152 | tf_op jit(solution)/shard_map/ppermute | solution.py:17
  207.5 23.6 %copy-start.4 = (f32[1,512,512]{2,1,0:T(8,128)}, f32[1,512,512]{2,1,0:T(8,128)S(1)}, u32[]{:S(2)}) copy-start(f32[1,512,512]{2,1,0:T(8,128)S(1)} %multiply_subtract_fusion.4) | copy-start | bytes 3145732
  207.7 12.4 %collective-permute-start.21 = (f32[1,1,512]{2,1,0:T(1,128)S(1)}, f32[1,1,512]{2,1,0:T(1,128)S(1)}, u32[]{:S(2)}, u32[]{:S(2)}) collective-permute-start(f32[1,1,512]{2,1,0:T(1,128)S(1)} %get-tuple-element.48), channel_id=1, source_target_pairs={{8,0},{16,8},{24,16},{9,1},{17,9},{25,17},{10,2},{18,10},{26,18},{... | collective-permute-start | bytes 6152 | tf_op jit(solution)/shard_map/ppermute | solution.py:18
  210.3 9.8 %collective-permute-start.20 = (f32[1,1,512]{2,1,0:T(1,128)S(1)}, f32[1,1,512]{2,1,0:T(1,128)S(1)}, u32[]{:S(2)}, u32[]{:S(2)}) collective-permute-start(f32[1,1,512]{2,1,0:T(1,128)S(1)} %get-tuple-element.49), channel_id=1, source_target_pairs={{0,8},{8,16},{16,24},{1,9},{9,17},{17,25},{2,10},{10,18},{18,26},{... | collective-permute-start | bytes 6152 | tf_op jit(solution)/shard_map/ppermute | solution.py:17
  214.8 8.3 %collective-permute-start.22 = (f32[1,512,1]{2,1,0:T(8,128)S(1)}, f32[1,512,1]{2,1,0:T(8,128)S(1)}, u32[]{:S(2)}, u32[]{:S(2)}) collective-permute-start(f32[1,512,1]{2,1,0:T(8,128)S(1)} %get-tuple-element.46), channel_id=1, source_target_pairs={{1,0},{2,1},{3,2},{4,3},{5,4},{6,5},{7,6},{9,8},{10,9},{11,10},{12... | collective-permute-start | bytes 6152 | tf_op jit(solution)/shard_map/ppermute | solution.py:18
  216.1 8.8 %collective-permute-start.23 = (f32[1,512,1]{2,1,0:T(8,128)S(1)}, f32[1,512,1]{2,1,0:T(8,128)S(1)}, u32[]{:S(2)}, u32[]{:S(2)}) collective-permute-start(f32[1,512,1]{2,1,0:T(8,128)S(1)} %get-tuple-element.47), channel_id=1, source_target_pairs={{0,1},{1,2},{2,3},{3,4},{4,5},{5,6},{6,7},{8,9},{9,10},{10,11},{11... | collective-permute-start | bytes 6152 | tf_op jit(solution)/shard_map/ppermute | solution.py:17
  253.6 33.1 %copy-start.5 = (f32[1,512,512]{2,1,0:T(8,128)}, f32[1,512,512]{2,1,0:T(8,128)S(1)}, u32[]{:S(2)}) copy-start(f32[1,512,512]{2,1,0:T(8,128)S(1)} %get-tuple-element.23) | copy-start | bytes 3145732
  253.7 21.8 %collective-permute-start.25 = (f32[1,1,512]{2,1,0:T(1,128)S(1)}, f32[1,1,512]{2,1,0:T(1,128)S(1)}, u32[]{:S(2)}, u32[]{:S(2)}) collective-permute-start(f32[1,1,512]{2,1,0:T(1,128)S(1)} %get-tuple-element.44), channel_id=1, source_target_pairs={{8,0},{16,8},{24,16},{9,1},{17,9},{25,17},{10,2},{18,10},{26,18},{... | collective-permute-start | bytes 6152 | tf_op jit(solution)/shard_map/ppermute | solution.py:18
  256.3 19.2 %collective-permute-start.24 = (f32[1,1,512]{2,1,0:T(1,128)S(1)}, f32[1,1,512]{2,1,0:T(1,128)S(1)}, u32[]{:S(2)}, u32[]{:S(2)}) collective-permute-start(f32[1,1,512]{2,1,0:T(1,128)S(1)} %get-tuple-element.45), channel_id=1, source_target_pairs={{0,8},{8,16},{16,24},{1,9},{9,17},{17,25},{2,10},{10,18},{18,26},{... | collective-permute-start | bytes 6152 | tf_op jit(solution)/shard_map/ppermute | solution.py:17
  260.8 17.8 %collective-permute-start.26 = (f32[1,512,1]{2,1,0:T(8,128)S(1)}, f32[1,512,1]{2,1,0:T(8,128)S(1)}, u32[]{:S(2)}, u32[]{:S(2)}) collective-permute-start(f32[1,512,1]{2,1,0:T(8,128)S(1)} %get-tuple-element.42), channel_id=1, source_target_pairs={{1,0},{2,1},{3,2},{4,3},{5,4},{6,5},{7,6},{9,8},{10,9},{11,10},{12... | collective-permute-start | bytes 6152 | tf_op jit(solution)/shard_map/ppermute | solution.py:18
  271.5 8.8 %collective-permute-start.27 = (f32[1,512,1]{2,1,0:T(8,128)S(1)}, f32[1,512,1]{2,1,0:T(8,128)S(1)}, u32[]{:S(2)}, u32[]{:S(2)}) collective-permute-start(f32[1,512,1]{2,1,0:T(8,128)S(1)} %get-tuple-element.43), channel_id=1, source_target_pairs={{0,1},{1,2},{2,3},{3,4},{4,5},{5,6},{6,7},{8,9},{9,10},{10,11},{11... | collective-permute-start | bytes 6152 | tf_op jit(solution)/shard_map/ppermute | solution.py:17
  307.9 23.6 %copy-start.6 = (f32[1,512,512]{2,1,0:T(8,128)}, f32[1,512,512]{2,1,0:T(8,128)S(1)}, u32[]{:S(2)}) copy-start(f32[1,512,512]{2,1,0:T(8,128)S(1)} %multiply_subtract_fusion.2) | copy-start | bytes 3145732
  308.1 12.4 %collective-permute-start.29 = (f32[1,1,512]{2,1,0:T(1,128)S(1)}, f32[1,1,512]{2,1,0:T(1,128)S(1)}, u32[]{:S(2)}, u32[]{:S(2)}) collective-permute-start(f32[1,1,512]{2,1,0:T(1,128)S(1)} %get-tuple-element.40), channel_id=1, source_target_pairs={{8,0},{16,8},{24,16},{9,1},{17,9},{25,17},{10,2},{18,10},{26,18},{... | collective-permute-start | bytes 6152 | tf_op jit(solution)/shard_map/ppermute | solution.py:18
  310.7 9.8 %collective-permute-start.28 = (f32[1,1,512]{2,1,0:T(1,128)S(1)}, f32[1,1,512]{2,1,0:T(1,128)S(1)}, u32[]{:S(2)}, u32[]{:S(2)}) collective-permute-start(f32[1,1,512]{2,1,0:T(1,128)S(1)} %get-tuple-element.41), channel_id=1, source_target_pairs={{0,8},{8,16},{16,24},{1,9},{9,17},{17,25},{2,10},{10,18},{18,26},{... | collective-permute-start | bytes 6152 | tf_op jit(solution)/shard_map/ppermute | solution.py:17
  315.2 8.3 %collective-permute-start.30 = (f32[1,512,1]{2,1,0:T(8,128)S(1)}, f32[1,512,1]{2,1,0:T(8,128)S(1)}, u32[]{:S(2)}, u32[]{:S(2)}) collective-permute-start(f32[1,512,1]{2,1,0:T(8,128)S(1)} %get-tuple-element.38), channel_id=1, source_target_pairs={{1,0},{2,1},{3,2},{4,3},{5,4},{6,5},{7,6},{9,8},{10,9},{11,10},{12... | collective-permute-start | bytes 6152 | tf_op jit(solution)/shard_map/ppermute | solution.py:18
  316.5 8.8 %collective-permute-start.31 = (f32[1,512,1]{2,1,0:T(8,128)S(1)}, f32[1,512,1]{2,1,0:T(8,128)S(1)}, u32[]{:S(2)}, u32[]{:S(2)}) collective-permute-start(f32[1,512,1]{2,1,0:T(8,128)S(1)} %get-tuple-element.39), channel_id=1, source_target_pairs={{0,1},{1,2},{2,3},{3,4},{4,5},{5,6},{6,7},{8,9},{9,10},{10,11},{11... | collective-permute-start | bytes 6152 | tf_op jit(solution)/shard_map/ppermute | solution.py:17
  354.4 23.6 %copy-start.7 = (f32[1,512,512]{2,1,0:T(8,128)}, f32[1,512,512]{2,1,0:T(8,128)S(1)}, u32[]{:S(2)}) copy-start(f32[1,512,512]{2,1,0:T(8,128)S(1)} %get-tuple-element.19) | copy-start | bytes 3145732
  354.6 12.4 %collective-permute-start.33 = (f32[1,1,512]{2,1,0:T(1,128)S(1)}, f32[1,1,512]{2,1,0:T(1,128)S(1)}, u32[]{:S(2)}, u32[]{:S(2)}) collective-permute-start(f32[1,1,512]{2,1,0:T(1,128)S(1)} %get-tuple-element.36), channel_id=1, source_target_pairs={{8,0},{16,8},{24,16},{9,1},{17,9},{25,17},{10,2},{18,10},{26,18},{... | collective-permute-start | bytes 6152 | tf_op jit(solution)/shard_map/ppermute | solution.py:18
  357.2 9.8 %collective-permute-start.32 = (f32[1,1,512]{2,1,0:T(1,128)S(1)}, f32[1,1,512]{2,1,0:T(1,128)S(1)}, u32[]{:S(2)}, u32[]{:S(2)}) collective-permute-start(f32[1,1,512]{2,1,0:T(1,128)S(1)} %get-tuple-element.37), channel_id=1, source_target_pairs={{0,8},{8,16},{16,24},{1,9},{9,17},{17,25},{2,10},{10,18},{18,26},{... | collective-permute-start | bytes 6152 | tf_op jit(solution)/shard_map/ppermute | solution.py:17
  361.6 8.3 %collective-permute-start.34 = (f32[1,512,1]{2,1,0:T(8,128)S(1)}, f32[1,512,1]{2,1,0:T(8,128)S(1)}, u32[]{:S(2)}, u32[]{:S(2)}) collective-permute-start(f32[1,512,1]{2,1,0:T(8,128)S(1)} %get-tuple-element.34), channel_id=1, source_target_pairs={{1,0},{2,1},{3,2},{4,3},{5,4},{6,5},{7,6},{9,8},{10,9},{11,10},{12... | collective-permute-start | bytes 6152 | tf_op jit(solution)/shard_map/ppermute | solution.py:18
  362.9 8.8 %collective-permute-start.35 = (f32[1,512,1]{2,1,0:T(8,128)S(1)}, f32[1,512,1]{2,1,0:T(8,128)S(1)}, u32[]{:S(2)}, u32[]{:S(2)}) collective-permute-start(f32[1,512,1]{2,1,0:T(8,128)S(1)} %get-tuple-element.35), channel_id=1, source_target_pairs={{0,1},{1,2},{2,3},{3,4},{4,5},{5,6},{6,7},{8,9},{9,10},{10,11},{11... | collective-permute-start | bytes 6152 | tf_op jit(solution)/shard_map/ppermute | solution.py:17
  397.0 5.8 %copy-start.8 = (f32[1,512,512]{2,1,0:T(8,128)S(1)}, f32[1,512,512]{2,1,0:T(8,128)}, u32[]{:S(2)}) copy-start(f32[1,512,512]{2,1,0:T(8,128)} %copy-done.7) | copy-start | bytes 3145732
  397.0 5.8 %copy-start.11 = (f32[1,512,512]{2,1,0:T(8,128)S(1)}, f32[1,512,512]{2,1,0:T(8,128)}, u32[]{:S(2)}) copy-start(f32[1,512,512]{2,1,0:T(8,128)} %get-tuple-element.20) | copy-start | bytes 3145732
  397.0 5.8 %copy-start.12 = (f32[1,512,512]{2,1,0:T(8,128)S(1)}, f32[1,512,512]{2,1,0:T(8,128)}, u32[]{:S(2)}) copy-start(f32[1,512,512]{2,1,0:T(8,128)} %get-tuple-element.18) | copy-start | bytes 3145732
where the time goes:
time: 410 us; the launch traced here: 404 us
  starting transfers between devices  122 us (30%)
  blocking collectives  110 us (27%)
  other arithmetic  94.7 us (23%)
  waiting for transfers between devices  41.4 us (10%)
  between operations  29.8 us (7%)
  local copies, waits for them, and re-layouts  6.29 us (2%)
    all_to_all x8, blocking collectives, from_everyone(): lax.all_to_all(jnp.broadcast_to(array[None], (count, *array.shape)), axis...  110 us
    ppermute x18, starting transfers between devices, with_halo(): lax.ppermute(last, axis, up)  77.9 us
    reduce_sum x8, other arithmetic, paired_sums(): jnp.sum(residual * residual, axis=(1, 2))  50.4 us
    ppermute x18, starting transfers between devices, with_halo(): lax.ppermute(first, axis, [(b, a) for a, b in up])  44.6 us
    ppermute x18, waiting for transfers between devices, with_halo(): lax.ppermute(first, axis, [(b, a) for a, b in up])  25.6 us
    sub x8, other arithmetic, per_device(): residual = residual - alpha[:, None, None] * along  20.4 us
    ppermute x18, waiting for transfers between devices, with_halo(): lax.ppermute(last, axis, up)  15.8 us
    concatenate x8, other arithmetic, together(): jnp.concatenate([a.reshape(-1) for a in arrays])  10.5 us
  transfers between devices with their start and end apart: 36, of which 18 were waited for; matrix products, arithmetic and copies ran while one was open for 0% of the time, Pallas kernels for 0%

commit v1 on v0

v1 whole, which is shorter than its diff:
```python
import functools
import jax
import jax.numpy as jnp
from jax import lax
from jax.experimental import pallas as pl
from jax.experimental.pallas import tpu as pltpu
from jax.sharding import PartitionSpec as P

ITERS = 8
HALO = 8
LANES = 128
LOW, HIGH = 0.05, 7.5
CENTRE, RADIUS = (HIGH + LOW) / 2, (HIGH - LOW) / 2
AMPLIFICATION = 24.0
VMEM = pl.BlockSpec(memory_space=pltpu.VMEM)
ANY = pl.BlockSpec(memory_space=pl.ANY)


def with_halo(array, sides, width):
    edges = {}
    for axis, dim in sides:
        count, length = (lax.axis_size(axis), array.shape[dim])
        up = [(i, (i + 1) % count) for i in range(count - 1)]
        last = lax.slice_in_dim(array, length - width, length, axis=dim)
        first = lax.slice_in_dim(array, 0, width, axis=dim)
        edges[dim] = (
            lax.ppermute(last, axis, up),
            lax.ppermute(first, axis, [(b, a) for a, b in up]),
        )
    done = []
    for _, dim in sides:
        low, high = edges[dim]
        around = [(width, width) if d in done else (0, 0) for d in range(array.ndim)]
        array = jnp.concatenate([jnp.pad(low, around), array, jnp.pad(high, around)], axis=dim)
        done.append(dim)
    return array


def total(value, axis):
    count = lax.axis_size(axis)
    flat = value.reshape(1, 1, 1)
    every = lax.all_to_all(jnp.broadcast_to(flat, (count, 1, 1)), axis, 0, 0, tiled=True)
    return every.sum()


def neighbours(field, right, left, down, upper):
    padded = with_halo(field, (("row", 1), ("col", 2)), 1)
    return (
        right * padded[:, 1:-1, 2:]
        + left * padded[:, 1:-1, :-2]
        + down * padded[:, 2:, 1:-1]
        + upper * padded[:, :-2, 1:-1]
    )


def plain(edges, labels, prior, data_weight):
    right = (edges % 2).astype(jnp.float32)
    left = (edges // 2 % 2).astype(jnp.float32)
    down = (edges // 4 % 2).astype(jnp.float32)
    upper = (edges // 8 % 2).astype(jnp.float32)
    degree = right + left + down + upper
    free = (labels == 0).astype(jnp.float32)
    anchor = (labels == 1).astype(jnp.float32)
    diag_term = degree + data_weight

    def nearby(field):
        return neighbours(field, right, left, down, upper)

    rhs = free * (data_weight * prior + nearby(anchor))

    def step(_, carry):
        result, residual, direction, norm_now = carry
        image_v = free * (diag_term * direction - nearby(direction))
        alpha = norm_now / total(jnp.sum(direction * image_v), ("row", "col"))
        result = result + alpha * direction
        residual = residual - alpha * image_v
        norm_next = total(jnp.sum(residual * residual), ("row", "col"))
        direction = residual + (norm_next / norm_now) * direction
        return result, residual, direction, norm_next

    start = (jnp.zeros_like(rhs), rhs, rhs, total(jnp.sum(rhs * rhs), ("row", "col")))
    result, residual, _, _ = lax.fori_loop(0, ITERS, step, start)
    return anchor + result, residual


def lane_ids(rows):
    return lax.broadcasted_iota(jnp.int32, (rows, LANES), 1)


def col_pack(*refs):
    first, last, to_left, to_right = refs[:4], refs[4:8], refs[8], refs[9]
    rows = first[0].shape[1]
    width = HALO + 1
    lane = lane_ids(rows)
    for side, out, base in ((first, to_left, 0), (last, to_right, LANES - width)):
        packed = None
        for a, ref in enumerate(side):
            x = ref[0].astype(jnp.float32)
            x = pltpu.roll(x, (a * width - base) % LANES, 1) if (a * width - base) % LANES else x
            packed = x if packed is None else jnp.where(lane < a * width, packed, x)
        out[...] = jnp.swapaxes(packed, 0, 1)[: out.shape[0]]


def side_tiles(from_right, from_left, rows_at, count):
    width = HALO + 1
    pad = jnp.zeros((LANES - from_right.shape[0], count), jnp.float32)
    r = jnp.swapaxes(jnp.concatenate([from_right[:, pl.ds(rows_at, count)], pad], 0), 0, 1)
    l = jnp.swapaxes(jnp.concatenate([from_left[:, pl.ds(rows_at, count)], pad], 0), 0, 1)
    lane = lane_ids(count)
    tiles = []
    for a in range(4):
        right = pltpu.roll(r, (-a * width) % LANES, 1) if a else r
        left = pltpu.roll(l, (LANES - width - a * width) % LANES, 1)
        outside = 2.0 if a == 1 else 0.0
        x = jnp.where(lane < width, right, jnp.where(lane >= LANES - width, left, outside))
        tiles.append(x)
    return tiles


def row_pack(*refs):
    top, bottom = refs[:4], refs[4:8]
    from_right, from_left, to_upper, to_lower = refs[8:]
    rows = from_right.shape[1]
    inner = top[0].shape[2]
    for side, out, at, narrow in (
        (top, to_upper, 0, 0),
        (bottom, to_lower, rows - LANES, HALO),
    ):
        tiles = side_tiles(from_right, from_left, at, LANES)
        shift = 0 if at == 0 else LANES - 2 * HALO
        for a, row, lo, n in ((0, 0, narrow, 8), (2, 8, narrow, 8), (3, 16, narrow, 8), (1, 24, 0, 16)):
            out[row : row + n, :inner] = side[a][0, lo : lo + n, :].astype(jnp.float32)
            out[row : row + n, inner:] = tiles[a][shift + lo : shift + lo + n]


def shifted(tiles, lane, by):
    count = len(tiles)
    turned = [pltpu.roll(t, by % LANES, 1) for t in tiles]
    if by > 0:
        return [jnp.where(lane == 0, turned[j - 1], turned[j]) for j in range(count)]
    return [jnp.where(lane == LANES - 1, turned[(j + 1) % count], turned[j]) for j in range(count)]


def basis(
    edges, labels, prior, weight, from_right, from_left, from_lower, from_upper,
    field, sums, code_s, lab_s, prior_s, weight_s, er_s, ed_s, eu_s, diag_s, sem,
):
    rows, cols = edges.shape[1], edges.shape[2]
    inner = cols // LANES
    tiles = inner + 1
    top = 2 * HALO
    copies = []
    for a, (src, dst) in enumerate(((edges, code_s), (labels, lab_s), (prior, prior_s), (weight, weight_s))):
        for j in range(inner):
            copy = pltpu.make_async_copy(
                src.at[0, :, pl.ds(j * LANES, LANES)],
                dst.at[j, pl.ds(top, rows), :],
                sem.at[a * inner + j],
            )
            copy.start()
            copies.append(copy)
    order = (code_s, lab_s, prior_s, weight_s)
    for at in range(0, rows, LANES):
        side = side_tiles(from_right, from_left, at, LANES)
        for a, dst in enumerate(order):
            dst[inner, top + at : top + at + LANES, :] = side[a].astype(dst.dtype)
    for a, row, n in ((0, 0, 8), (2, 8, 8), (3, 16, 8), (1, 24, 16)):
        dst = order[a]
        for j in range(tiles):
            lanes = slice(j * LANES, (j + 1) * LANES)
            dst[j, top - n : top, :] = from_upper[row : row + n, lanes].astype(dst.dtype)
            dst[j, top + rows : top + rows + n, :] = from_lower[row : row + n, lanes].astype(dst.dtype)
    zero = jnp.zeros((HALO, LANES), jnp.float32)
    for k in range(ITERS):
        for j in range(tiles):
            field[k, j, 0:HALO, :] = zero
            field[k, j, top + rows + HALO : top + rows + 2 * HALO, :] = zero
    for copy in copies:
        copy.wait()

    lane = lane_ids(8)
    scale = 2.0 / RADIUS

    def decode(i, _):
        s = pl.multiple_of(HALO + 8 * i, 8)
        here = pl.ds(s, 8)
        lab = [lab_s[j, here, :] for j in range(tiles)]
        lab_r = shifted(lab, lane, -1)
        lab_l = shifted(lab, lane, 1)
        for j in range(tiles):
            code = code_s[j, here, :]
            r = (code & 1).astype(jnp.float32)
            l = ((code >> 1) & 1).astype(jnp.float32)
            d = ((code >> 2) & 1).astype(jnp.float32)
            u = ((code >> 3) & 1).astype(jnp.float32)
            lab_d = lab_s[j, pl.ds(s + 1, 8), :]
            lab_u = lab_s[j, pl.ds(s - 1, 8), :]
            w = weight_s[j, here, :]
            free = lab[j] == 0
            one = jnp.where(free, scale, 0.0)
            er_s[j, here, :] = jnp.where(lab_r[j] == 0, one, 0.0) * r
            ed_s[j, here, :] = one * d
            eu_s[j, here, :] = one * u
            diag_s[j, here, :] = scale * ((r + l + d + u) + w - CENTRE)
            near = (
                jnp.where(lab_r[j] == 1, r, 0.0)
                + jnp.where(lab_l[j] == 1, l, 0.0)
                + jnp.where(lab_d == 1, d, 0.0)
                + jnp.where(lab_u == 1, u, 0.0)
            )
            rhs = jnp.where(free, w * prior_s[j, here, :] + near, 0.0)
            field[0, j, here, :] = rhs
        return 0

    lax.fori_loop(0, (rows + 2 * HALO) // 8, decode, 0)

    def advance(k, s):
        here = pl.ds(s, 8)
        v = [field[k, j, here, :] for j in range(tiles)]
        er = [er_s[j, here, :] for j in range(tiles)]
        v_r = shifted(v, lane, -1)
        g = shifted([er[j] * v[j] for j in range(tiles)], lane, 1)
        new = []
        for j in range(tiles):
            x = diag_s[j, here, :] * v[j] - (er[j] * v_r[j] + g[j])
            x = x - (
                ed_s[j, here, :] * field[k, j, pl.ds(s + 1, 8), :]
                + eu_s[j, here, :] * field[k, j, pl.ds(s - 1, 8), :]
            )
            x = 0.5 * x if k == 0 else x - field[k - 1, j, here, :]
            field[k + 1, j, here, :] = x
            new.append(x)
        return v, new

    parts = []
    for k in range(ITERS):
        last = k == ITERS - 1

        def body(i, carry, k=k, last=last):
            s = pl.multiple_of(top + 8 * i, 8)
            v, new = advance(k, s)
            pairs = [(v, v), (v, new)] + ([(new, new)] if last else [])
            out = []
            for acc, (a, b) in zip(carry, pairs):
                t = [a[j] * b[j] for j in range(inner)]
                while len(t) > 1:
                    t = [t[q] + t[q + 1] for q in range(0, len(t) - 1, 2)] + ([t[-1]] if len(t) % 2 else [])
                out.append(acc + t[0])
            return tuple(out)

        if not last:
            advance(k, HALO)
            advance(k, top + rows)
        acc = tuple(jnp.zeros((8, LANES), jnp.float32) for _ in range(3 if last else 2))
        parts.extend(lax.fori_loop(0, rows // 8, body, acc))

    out = jnp.zeros((1, LANES), jnp.float32)
    for n, acc in enumerate(parts):
        one = jnp.sum(jnp.sum(acc, axis=0, keepdims=True), axis=1, keepdims=True)
        out = jnp.where(lane_ids(1) == n, one, out)
    sums[...] = jnp.broadcast_to(out[None], sums.shape)


def coefficients(dots):
    n = ITERS
    inv = 1.0 / dots[0]
    moment = [jnp.ones_like(dots[0]), dots[1] * inv]
    for k in range(1, n + 1):
        moment.append(2.0 * (dots[2 * k] * inv) - moment[0])
        if k < n:
            moment.append(2.0 * (dots[2 * k + 1] * inv) - moment[1])
    gram = [[0.5 * (moment[i + j] + moment[abs(i - j)]) for j in range(n + 1)] for i in range(n + 1)]

    def image(p):
        q = [CENTRE * x for x in p] + [jnp.zeros_like(p[0])]
        for i, x in enumerate(p):
            if i == 0:
                q[1] = q[1] + RADIUS * x
            else:
                q[i + 1] = q[i + 1] + (RADIUS / 2) * x
                q[i - 1] = q[i - 1] + (RADIUS / 2) * x
        return q

    def product(a, b):
        sums = None
        for i, x in enumerate(a):
            t = gram[i][0] * b[0]
            for j in range(1, len(b)):
                t = t + gram[i][j] * b[j]
            sums = x * t if sums is None else sums + x * t
        return sums

    zero = jnp.zeros_like(inv)
    x, r, p = [], [moment[0]], [moment[0]]
    now = moment[0]
    for _ in range(n):
        q = image(p)
        alpha = now / product(p, q)
        x = [(x[i] if i < len(x) else zero) + alpha * p[i] for i in range(len(p))]
        r = [(r[i] if i < len(r) else zero) - alpha * q[i] for i in range(len(q))]
        following = product(r, r)
        beta = following / now
        p = [r[i] + (beta * p[i] if i < len(p) else zero) for i in range(len(r))]
        now = following
    size = zero
    for i in range(n + 1):
        size = size + jnp.abs(r[i]) * jnp.sqrt(jnp.maximum(gram[i][i], 0.0))
    good = (size * size <= (AMPLIFICATION * AMPLIFICATION) * now) & (now > 0.0)
    return x, r, good


def combine(every, labels, field, labeling, residual, flag):
    rows, cols = labels.shape[1], labels.shape[2]
    inner = cols // LANES
    top = 2 * HALO
    g = jnp.sum(every[:, 0, :], axis=0, keepdims=True)
    dots = [jnp.broadcast_to(g[:, n : n + 1], (8, LANES)) for n in range(2 * ITERS + 1)]
    x, r, good = coefficients(dots)
    flag[...] = good.astype(jnp.int32)

    def body(i, _):
        s = pl.multiple_of(8 * i, 8)
        for j in range(inner):
            lanes = slice(j * LANES, (j + 1) * LANES)
            sol = jnp.where(labels[0, pl.ds(s, 8), lanes] == 1, 1.0, 0.0)
            res = None
            for k in range(ITERS + 1):
                t = field[k, j, pl.ds(s + top, 8), :]
                res = r[k] * t if res is None else res + r[k] * t
                if k < ITERS:
                    sol = sol + x[k] * t
            labeling[0, pl.ds(s, 8), lanes] = sol
            residual[0, pl.ds(s, 8), lanes] = res
        return 0

    lax.fori_loop(0, rows // 8, body, 0)


def fixed(shape, at):
    return pl.BlockSpec(shape, lambda *_: at)


def per_device(edges, labels, prior, data_weight):
    arrays = (edges, labels, prior, data_weight)
    _, rows, cols = edges.shape
    f32 = jnp.float32
    tiles = cols // LANES + 1
    deep = rows + 4 * HALO

    to_left, to_right = pl.pallas_call(
        col_pack,
        grid=(1,),
        in_specs=[fixed((1, rows, LANES), (0, 0, 0))] * 4
        + [fixed((1, rows, LANES), (0, 0, cols // LANES - 1))] * 4,
        out_specs=[fixed((40, rows), (0, 0))] * 2,
        out_shape=[jax.ShapeDtypeStruct((40, rows), f32)] * 2,
    )(*arrays, *arrays)
    count = lax.axis_size("col")
    up = [(i, i + 1) for i in range(count - 1)]
    back = [(b, a) for a, b in up]
    from_right = lax.ppermute(to_left, "col", back)
    from_left = lax.ppermute(to_right, "col", up)

    to_upper, to_lower = pl.pallas_call(
        row_pack,
        grid=(1,),
        in_specs=[fixed((1, 2 * HALO, cols), (0, 0, 0))] * 4
        + [fixed((1, 2 * HALO, cols), (0, rows // (2 * HALO) - 1, 0))] * 4
        + [fixed((40, rows), (0, 0))] * 2,
        out_specs=[fixed((40, tiles * LANES), (0, 0))] * 2,
        out_shape=[jax.ShapeDtypeStruct((40, tiles * LANES), f32)] * 2,
    )(*arrays, *arrays, from_right, from_left)
    count = lax.axis_size("row")
    up = [(i, i + 1) for i in range(count - 1)]
    back = [(b, a) for a, b in up]
    from_lower = lax.ppermute(to_upper, "row", back)
    from_upper = lax.ppermute(to_lower, "row", up)

    group = lax.axis_size(("row", "col"))
    grid_s = lambda dtype: pltpu.VMEM((tiles, deep, LANES), dtype)
    field, sums = pl.pallas_call(
        basis,
        in_specs=[ANY] * 4 + [VMEM] * 4,
        out_specs=[VMEM, VMEM],
        out_shape=[
            jax.ShapeDtypeStruct((ITERS + 1, tiles, deep, LANES), f32),
            jax.ShapeDtypeStruct((group, 1, LANES), f32),
        ],
        scratch_shapes=[grid_s(jnp.int32), grid_s(jnp.int32)]
        + [grid_s(f32)] * 6
        + [pltpu.SemaphoreType.DMA((4 * (tiles - 1),))],
        compiler_params=pltpu.CompilerParams(vmem_limit_bytes=32 * 1024 * 1024),
    )(*arrays, from_right, from_left, from_lower, from_upper)

    every = lax.all_to_all(sums, ("row", "col"), 0, 0, tiled=True)

    labeling, residual, flag = pl.pallas_call(
        combine,
        in_specs=[VMEM] * 3,
        out_specs=[VMEM] * 3,
        out_shape=[jax.ShapeDtypeStruct(edges.shape, f32)] * 2
        + [jax.ShapeDtypeStruct((8, LANES), jnp.int32)],
        compiler_params=pltpu.CompilerParams(vmem_limit_bytes=32 * 1024 * 1024),
    )(every, labels, field)

    def again(carry):
        return (jnp.int32(1), *plain(edges, labels, prior, data_weight))

    _, labeling, residual = lax.while_loop(
        lambda carry: carry[0] == 0, again, (flag[0, 0], labeling, residual)
    )
    return labeling, residual


def solution(mesh):
    spec = P("img", "row", "col")
    return jax.shard_map(
        per_device, mesh=mesh, in_specs=(spec,) * 4, out_specs=(spec,) * 2, check_vma=False
    )
```

time: 410 us -> 115 us (0.28); the launches traced: 404 us -> 114 us
  starting transfers between devices: 122 us -> 14.3 us
  other arithmetic: 94.7 us -> 0 us
  blocking collectives: 110 us -> 17.7 us
  Pallas kernels: 0 us -> 74.1 us
  waiting for transfers between devices: 41.4 us -> 3.75 us
  between operations: 29.8 us -> 0.84 us
    ppermute x36 -> x4, starting transfers between devices: 122 us -> 14.3 us  [the longest x1 4.66 us: per_device(): from_upper = lax.ppermute(to_lower, 'row', up)]
    all_to_all x8 -> x1, blocking collectives: 110 us -> 17.7 us  [per_device(): every = lax.all_to_all(sums, ('row', 'col'), 0, 0, tiled=True)]
    pallas_call x0 -> x4, Pallas kernels: none -> 74.1 us  [the longest x1 64.5 us: per_device(): pl.pallas_call(basis, in_specs=[ANY] * 4 + [VMEM] * 4, out_specs=[VMEM, V...]
    reduce_sum x16 -> x0, other arithmetic: 50.8 us -> none  [the longest x8 50.4 us: paired_sums(): jnp.sum(residual * residual, axis=(1, 2))]
    ppermute x36 -> x4, waiting for transfers between devices: 41.4 us -> 3.75 us  [the longest x1 1.68 us: per_device(): from_left = lax.ppermute(to_right, 'col', up)]
    sub x8 -> x0, other arithmetic: 20.4 us -> none  [per_device(): residual = residual - alpha[:, None, None] * along]
    concatenate x8 -> x0, other arithmetic: 10.5 us -> none  [together(): jnp.concatenate([a.reshape(-1) for a in arrays])]
    add x1 -> x0, other arithmetic: 5.75 us -> none  [per_device(): return (anchor + solution, residual)]
  transfers between devices with their start and end apart: 36 -> 4, of which waited for: 18 -> 4; matrix products, arithmetic and copies ran while one was open for 0% -> 0% of each run, Pallas kernels for 0% -> 0%
where the time goes in v1:
time: 115 us; the launch traced here: 114 us
  Pallas kernels  74.1 us (64%)
  blocking collectives  17.7 us (15%)
  starting transfers between devices  14.3 us (12%)
  waiting for transfers between devices  3.75 us (3%)
  local copies, waits for them, and re-layouts  2.91 us (3%)
    pallas_call x1, Pallas kernels, per_device(): pl.pallas_call(basis, in_specs=[ANY] * 4 + [VMEM] * 4, out_specs=[VMEM, V...  64.5 us
    all_to_all x1, blocking collectives, per_device(): every = lax.all_to_all(sums, ('row', 'col'), 0, 0, tiled=True)  17.7 us
    pallas_call x1, Pallas kernels, per_device(): pl.pallas_call(combine, in_specs=[VMEM] * 3, out_specs=[VMEM] * 3, out_sh...  4.78 us
    ppermute x1, starting transfers between devices, per_device(): from_upper = lax.ppermute(to_lower, 'row', up)  4.66 us
    ppermute x1, starting transfers between devices, per_device(): from_left = lax.ppermute(to_right, 'col', up)  4.65 us
    ppermute x1, starting transfers between devices, per_device(): from_lower = lax.ppermute(to_upper, 'row', back)  3.75 us
    pallas_call x1, Pallas kernels, per_device(): pl.pallas_call(col_pack, grid=(1,), in_specs=[fixed((1, rows, LANES), (0,...  2.85 us
    unnamed x8, local copies, waits for them, and re-layouts  2.39 us
  transfers between devices with their start and end apart: 4, of which 4 were waited for; matrix products, arithmetic and copies ran while one was open for 0% of the time, Pallas kernels for 0%

profile of v1, /device:TPU:1, one launch (start us, length us, event | category | flops | bytes accessed | tf_op | source)
XLA Modules:
  0.0 114.4 jit_solution(4885619168881265379)
XLA Ops:
  0.6 2.9 %shard_map.59 = (f32[40,512]{1,0:T(8,128)}, f32[40,512]{1,0:T(8,128)}) custom-call(s32[1,512,512]{2,1,0:T(8,128)} %edges.1, s32[1,512,512]{2,1,0:T(8,128)} %labels.3, f32[1,512,512]{2,1,0:T(8,128)} %prior.1, f32[1,512,512]{2,1,0:T(8,128)} %weight.1, s32[1,512,512]{2,1,0:T(8,128)} %edges.1, s32[1,512,512]{2,1,0:T(8,128)} %labels.3, f32[1,512,512]{2,1,0:T(8,128)} %prior.1, ...), custom_call_target="tpu_custom_call" | custom-call | tf_op jit(solution)/shard_map/pallas_call | solution.py:350
  3.5 1.3 %collective-permute-start.8 = (f32[40,512]{1,0:T(8,128)}, f32[40,512]{1,0:T(8,128)S(1)}, u32[]{:S(2)}, u32[]{:S(2)}) collective-permute-start(f32[40,512]{1,0:T(8,128)} %get-tuple-element.211), channel_id=1, source_target_pairs={{1,0},{2,1},{3,2},{4,3},{5,4},{6,5},{7,6},{9,8},{10,9},{11,10},{12... | collective-permute-start | bytes 245768 | tf_op jit(solution)/shard_map/ppermute | solution.py:361
  4.8 4.7 %collective-permute-start.9 = (f32[40,512]{1,0:T(8,128)}, f32[40,512]{1,0:T(8,128)S(1)}, u32[]{:S(2)}, u32[]{:S(2)}) collective-permute-start(f32[40,512]{1,0:T(8,128)} %get-tuple-element.212), channel_id=1, source_target_pairs={{0,1},{1,2},{2,3},{3,4},{4,5},{5,6},{6,7},{8,9},{9,10},{10,11},{11... | collective-permute-start | bytes 245768 | tf_op jit(solution)/shard_map/ppermute | solution.py:362
  9.4 0.1 collective-permute-done.8.refs_8_.from_right
  9.5 0.0 copy-start
  9.5 1.7 %collective-permute-done.9.refs_9_.from_left = f32[40,512]{1,0:T(8,128)S(1)} collective-permute-done((f32[40,512]{1,0:T(8,128)}, f32[40,512]{1,0:T(8,128)S(1)}, u32[]{:S(2)}, u32[]{:S(2)}) %collective-permute-start.9) | collective-permute-done | bytes 81952 | tf_op jit(solution)/shard_map/ppermute | solution.py:362
  11.2 0.0 copy-done
  11.2 0.0 copy-start.2
  11.2 0.6 copy-done.2
  11.8 2.0 %shard_map.60 = (f32[40,640]{1,0:T(8,128)}, f32[40,640]{1,0:T(8,128)}) custom-call(s32[1,512,512]{2,1,0:T(8,128)} %edges.1, s32[1,512,512]{2,1,0:T(8,128)} %labels.3, f32[1,512,512]{2,1,0:T(8,128)} %prior.1, f32[1,512,512]{2,1,0:T(8,128)} %weight.1, s32[1,512,512]{2,1,0:T(8,128)} %edges.1, s32[1,512,512]{2,1,0:T(8,128)} %labels.3, f32[1,512,512]{2,1,0:T(8,128)} %prior.1, ...), custom_call_target="tpu_custom_call" | custom-call | tf_op jit(solution)/shard_map/pallas_call | solution.py:364
  13.8 3.8 %collective-permute-start.10 = (f32[40,640]{1,0:T(8,128)}, f32[40,640]{1,0:T(8,128)S(1)}, u32[]{:S(2)}, u32[]{:S(2)}) collective-permute-start(f32[40,640]{1,0:T(8,128)} %get-tuple-element.213), channel_id=1, source_target_pairs={{8,0},{16,8},{24,16},{9,1},{17,9},{25,17},{10,2},{18,10},{26,18},{... | collective-permute-start | bytes 307208 | tf_op jit(solution)/shard_map/ppermute | solution.py:376
  17.5 4.7 %collective-permute-start.11 = (f32[40,640]{1,0:T(8,128)}, f32[40,640]{1,0:T(8,128)S(1)}, u32[]{:S(2)}, u32[]{:S(2)}) collective-permute-start(f32[40,640]{1,0:T(8,128)} %get-tuple-element.214), channel_id=1, source_target_pairs={{0,8},{8,16},{16,24},{1,9},{9,17},{17,25},{2,10},{10,18},{18,26},{... | collective-permute-start | bytes 307208 | tf_op jit(solution)/shard_map/ppermute | solution.py:377
  22.2 0.6 collective-permute-done.10.from_lower
  22.8 1.4 %collective-permute-done.11.from_upper = f32[40,640]{1,0:T(8,128)S(1)} collective-permute-done((f32[40,640]{1,0:T(8,128)}, f32[40,640]{1,0:T(8,128)S(1)}, u32[]{:S(2)}, u32[]{:S(2)}) %collective-permute-start.11) | collective-permute-done | bytes 102432 | tf_op jit(solution)/shard_map/ppermute | solution.py:377
  24.2 0.0 copy-start.1
  24.2 0.9 copy-done.1
  25.1 0.0 copy-start.3
  25.1 0.9 copy-done.3
  26.0 64.5 %shard_map.61 = (f32[9,5,544,128]{3,2,1,0:T(8,128)S(1)}, f32[32,1,128]{2,1,0:T(1,128)S(1)}) custom-call(s32[1,512,512]{2,1,0:T(8,128)} %edges.1, s32[1,512,512]{2,1,0:T(8,128)} %labels.3, f32[1,512,512]{2,1,0:T(8,128)} %prior.1, f32[1,512,512]{2,1,0:T(8,128)} %weight.1, f32[40,512]{1,0:T(8,128)S(1)} %copy-done.1, f32[40,512]{1,0:T(8,128)S(1)} %copy-done.3, ...), custom_call_target="tpu_custom_call" | custom-call | tf_op jit(solution)/shard_map/pallas_call | solution.py:381
  90.5 17.7 %all_to_all.31.every = f32[32,1,128]{2,1,0:T(1,128)S(1)} all-to-all(f32[32,1,128]{2,1,0:T(1,128)S(1)} %get-tuple-element.215), channel_id=1, replica_groups=mesh['img'=4,'row'=4,'col'=8] {'row','col'}, dimensions={0} | all-to-all | bytes 32768 | tf_op jit(solution)/shard_map/all_to_all | solution.py:395
  108.2 4.8 %shard_map.62 = (f32[1,512,512]{2,1,0:T(8,128)}, f32[1,512,512]{2,1,0:T(8,128)}, s32[8,128]{1,0:T(8,128)S(1)}) custom-call(f32[32,1,128]{2,1,0:T(1,128)S(1)} %all_to_all.31.every, s32[1,512,512]{2,1,0:T(8,128)} %labels.3, f32[9,5,544,128]{3,2,1,0:T(8,128)S(1)} %get-tuple-element.216.field), custom_call_target="tpu_custom_call" | custom-call | tf_op jit(solution)/shard_map/pallas_call | solution.py:397
  113.0 0.5 slice.91
  113.5 0.8 while.30
Async XLA Ops:
  3.5 6.0 %collective-permute-start.8 = (f32[40,512]{1,0:T(8,128)}, f32[40,512]{1,0:T(8,128)S(1)}, u32[]{:S(2)}, u32[]{:S(2)}) collective-permute-start(f32[40,512]{1,0:T(8,128)} %get-tuple-element.211), channel_id=1, source_target_pairs={{1,0},{2,1},{3,2},{4,3},{5,4},{6,5},{7,6},{9,8},{10,9},{11,10},{12... | collective-permute-start | bytes 245768 | tf_op jit(solution)/shard_map/ppermute | solution.py:361
  4.8 6.4 %collective-permute-start.9 = (f32[40,512]{1,0:T(8,128)}, f32[40,512]{1,0:T(8,128)S(1)}, u32[]{:S(2)}, u32[]{:S(2)}) collective-permute-start(f32[40,512]{1,0:T(8,128)} %get-tuple-element.212), channel_id=1, source_target_pairs={{0,1},{1,2},{2,3},{3,4},{4,5},{5,6},{6,7},{8,9},{9,10},{10,11},{11... | collective-permute-start | bytes 245768 | tf_op jit(solution)/shard_map/ppermute | solution.py:362
  9.5 1.7 %copy-start = (f32[40,512]{1,0:T(8,128)}, f32[40,512]{1,0:T(8,128)S(1)}, u32[]{:S(2)}) copy-start(f32[40,512]{1,0:T(8,128)S(1)} %collective-permute-done.8.refs_8_.from_right) | copy-start | bytes 245764
  11.2 0.6 copy-start.2
  13.8 9.0 %collective-permute-start.10 = (f32[40,640]{1,0:T(8,128)}, f32[40,640]{1,0:T(8,128)S(1)}, u32[]{:S(2)}, u32[]{:S(2)}) collective-permute-start(f32[40,640]{1,0:T(8,128)} %get-tuple-element.213), channel_id=1, source_target_pairs={{8,0},{16,8},{24,16},{9,1},{17,9},{25,17},{10,2},{18,10},{26,18},{... | collective-permute-start | bytes 307208 | tf_op jit(solution)/shard_map/ppermute | solution.py:376
  17.5 6.6 %collective-permute-start.11 = (f32[40,640]{1,0:T(8,128)}, f32[40,640]{1,0:T(8,128)S(1)}, u32[]{:S(2)}, u32[]{:S(2)}) collective-permute-start(f32[40,640]{1,0:T(8,128)} %get-tuple-element.214), channel_id=1, source_target_pairs={{0,8},{8,16},{16,24},{1,9},{9,17},{17,25},{2,10},{10,18},{18,26},{... | collective-permute-start | bytes 307208 | tf_op jit(solution)/shard_map/ppermute | solution.py:377
  24.2 0.9 copy-start.1
  25.1 0.9 copy-start.3

commit v2 on v1

--- a/solution.py
+++ b/solution.py
@@ -143,8 +143,10 @@
 
 def basis(
     edges, labels, prior, weight, from_right, from_left, from_lower, from_upper,
-    field, sums, code_s, lab_s, prior_s, weight_s, er_s, ed_s, eu_s, diag_s, sem,
+    *refs,
 ):
+    field, sums = refs[: ITERS + 1], refs[ITERS + 1]
+    code_s, lab_s, prior_s, weight_s, er_s, ed_s, eu_s, diag_s, sem = refs[ITERS + 2 :]
     rows, cols = edges.shape[1], edges.shape[2]
     inner = cols // LANES
     tiles = inner + 1
@@ -173,8 +175,8 @@
     zero = jnp.zeros((HALO, LANES), jnp.float32)
     for k in range(ITERS):
         for j in range(tiles):
-            field[k, j, 0:HALO, :] = zero
-            field[k, j, top + rows + HALO : top + rows + 2 * HALO, :] = zero
+            field[k][j, 0:HALO, :] = zero
+            field[k][j, top + rows + HALO : top + rows + 2 * HALO, :] = zero
     for copy in copies:
         copy.wait()
 
@@ -209,14 +211,14 @@
                 + jnp.where(lab_u == 1, u, 0.0)
             )
             rhs = jnp.where(free, w * prior_s[j, here, :] + near, 0.0)
-            field[0, j, here, :] = rhs
+            field[0][j, here, :] = rhs
         return 0
 
-    lax.fori_loop(0, (rows + 2 * HALO) // 8, decode, 0)
+    lax.fori_loop(0, (rows + 2 * HALO) // 8, decode, 0, unroll=6)
 
     def advance(k, s):
         here = pl.ds(s, 8)
-        v = [field[k, j, here, :] for j in range(tiles)]
+        v = [field[k][j, here, :] for j in range(tiles)]
         er = [er_s[j, here, :] for j in range(tiles)]
         v_r = shifted(v, lane, -1)
         g = shifted([er[j] * v[j] for j in range(tiles)], lane, 1)
@@ -224,11 +226,11 @@
         for j in range(tiles):
             x = diag_s[j, here, :] * v[j] - (er[j] * v_r[j] + g[j])
             x = x - (
-                ed_s[j, here, :] * field[k, j, pl.ds(s + 1, 8), :]
-                + eu_s[j, here, :] * field[k, j, pl.ds(s - 1, 8), :]
+                ed_s[j, here, :] * field[k][j, pl.ds(s + 1, 8), :]
+                + eu_s[j, here, :] * field[k][j, pl.ds(s - 1, 8), :]
             )
-            x = 0.5 * x if k == 0 else x - field[k - 1, j, here, :]
-            field[k + 1, j, here, :] = x
+            x = 0.5 * x if k == 0 else x - field[k - 1][j, here, :]
+            field[k + 1][j, here, :] = x
             new.append(x)
         return v, new
 
@@ -252,7 +254,7 @@
             advance(k, HALO)
             advance(k, top + rows)
         acc = tuple(jnp.zeros((8, LANES), jnp.float32) for _ in range(3 if last else 2))
-        parts.extend(lax.fori_loop(0, rows // 8, body, acc))
+        parts.extend(lax.fori_loop(0, rows // 8, body, acc, unroll=16))
 
     out = jnp.zeros((1, LANES), jnp.float32)
     for n, acc in enumerate(parts):
@@ -309,7 +311,8 @@
     return x, r, good
 
 
-def combine(every, labels, field, labeling, residual, flag):
+def combine(every, labels, *refs):
+    field, (labeling, residual, flag) = refs[: ITERS + 1], refs[ITERS + 1 :]
     rows, cols = labels.shape[1], labels.shape[2]
     inner = cols // LANES
     top = 2 * HALO
@@ -325,7 +328,7 @@
             sol = jnp.where(labels[0, pl.ds(s, 8), lanes] == 1, 1.0, 0.0)
             res = None
             for k in range(ITERS + 1):
-                t = field[k, j, pl.ds(s + top, 8), :]
+                t = field[k][j, pl.ds(s + top, 8), :]
                 res = r[k] * t if res is None else res + r[k] * t
                 if k < ITERS:
                     sol = sol + x[k] * t
@@ -333,7 +336,7 @@
             residual[0, pl.ds(s, 8), lanes] = res
         return 0
 
-    lax.fori_loop(0, rows // 8, body, 0)
+    lax.fori_loop(0, rows // 8, body, 0, unroll=8)
 
 
 def fixed(shape, at):
@@ -378,14 +381,12 @@
 
     group = lax.axis_size(("row", "col"))
     grid_s = lambda dtype: pltpu.VMEM((tiles, deep, LANES), dtype)
-    field, sums = pl.pallas_call(
+    *field, sums = pl.pallas_call(
         basis,
         in_specs=[ANY] * 4 + [VMEM] * 4,
-        out_specs=[VMEM, VMEM],
-        out_shape=[
-            jax.ShapeDtypeStruct((ITERS + 1, tiles, deep, LANES), f32),
-            jax.ShapeDtypeStruct((group, 1, LANES), f32),
-        ],
+        out_specs=[VMEM] * (ITERS + 2),
+        out_shape=[jax.ShapeDtypeStruct((tiles, deep, LANES), f32)] * (ITERS + 1)
+        + [jax.ShapeDtypeStruct((group, 1, LANES), f32)],
         scratch_shapes=[grid_s(jnp.int32), grid_s(jnp.int32)]
         + [grid_s(f32)] * 6
         + [pltpu.SemaphoreType.DMA((4 * (tiles - 1),))],
@@ -396,12 +397,12 @@
 
     labeling, residual, flag = pl.pallas_call(
         combine,
-        in_specs=[VMEM] * 3,
+        in_specs=[VMEM] * (ITERS + 3),
         out_specs=[VMEM] * 3,
         out_shape=[jax.ShapeDtypeStruct(edges.shape, f32)] * 2
         + [jax.ShapeDtypeStruct((8, LANES), jnp.int32)],
         compiler_params=pltpu.CompilerParams(vmem_limit_bytes=32 * 1024 * 1024),
-    )(every, labels, field)
+    )(every, labels, *field)
 
     def again(carry):
         return (jnp.int32(1), *plain(edges, labels, prior, data_weight))

time: 115 us -> 63.7 us (0.55)
  Pallas kernels: 74.1 us -> 23 us
    pallas_call x2, Pallas kernels: 69.3 us -> 18.1 us  [the longest x1 15.1 us: per_device(): pl.pallas_call(basis, in_specs=[ANY] * 4 + [VMEM] * 4, out_specs=[VMEM] *...]
    unnamed x8 -> x12, local copies, waits for them, and re-layouts: 2.39 us -> 2.42 us
where the time goes in v2:
time: 63.7 us; the launch traced here: 63.3 us
  Pallas kernels  23 us (36%)
  blocking collectives  17.7 us (28%)
  starting transfers between devices  14.3 us (22%)
  waiting for transfers between devices  3.75 us (6%)
  local copies, waits for them, and re-layouts  2.9 us (5%)
  between operations  0.85 us (1%)
  loops' own time  0.73 us (1%)
    all_to_all x1, blocking collectives, per_device(): every = lax.all_to_all(sums, ('row', 'col'), 0, 0, tiled=True)  17.7 us
    pallas_call x1, Pallas kernels, per_device(): pl.pallas_call(basis, in_specs=[ANY] * 4 + [VMEM] * 4, out_specs=[VMEM] *...  15.1 us
    ppermute x1, starting transfers between devices, per_device(): from_upper = lax.ppermute(to_lower, 'row', up)  4.66 us
    ppermute x1, starting transfers between devices, per_device(): from_left = lax.ppermute(to_right, 'col', up)  4.65 us
    ppermute x1, starting transfers between devices, per_device(): from_lower = lax.ppermute(to_upper, 'row', back)  3.75 us
    pallas_call x1, Pallas kernels, per_device(): pl.pallas_call(combine, in_specs=[VMEM] * (ITERS + 3), out_specs=[VMEM] *...  3.06 us
    pallas_call x1, Pallas kernels, per_device(): pl.pallas_call(col_pack, grid=(1,), in_specs=[fixed((1, rows, LANES), (0,...  2.99 us
    unnamed x12, local copies, waits for them, and re-layouts  2.42 us
  transfers between devices with their start and end apart: 4, of which 4 were waited for; matrix products, arithmetic and copies ran while one was open for 0% of the time, Pallas kernels for 0%

profile of v2, /device:TPU:1, one launch (start us, length us, event | category | flops | bytes accessed | tf_op | source)
XLA Modules:
  0.0 63.3 jit_solution(8266369929267069018)
XLA Ops:
  0.6 0.0 copy-start.5
  0.6 0.0 copy-start.7
  0.7 3.0 %shard_map.59 = (f32[40,512]{1,0:T(8,128)}, f32[40,512]{1,0:T(8,128)}) custom-call(s32[1,512,512]{2,1,0:T(8,128)} %edges.1, s32[1,512,512]{2,1,0:T(8,128)} %labels.3, f32[1,512,512]{2,1,0:T(8,128)} %prior.1, f32[1,512,512]{2,1,0:T(8,128)} %weight.1, s32[1,512,512]{2,1,0:T(8,128)} %edges.1, s32[1,512,512]{2,1,0:T(8,128)} %labels.3, f32[1,512,512]{2,1,0:T(8,128)} %prior.1, ...), custom_call_target="tpu_custom_call" | custom-call | tf_op jit(solution)/shard_map/pallas_call | solution.py:353
  3.6 1.3 %collective-permute-start.8 = (f32[40,512]{1,0:T(8,128)}, f32[40,512]{1,0:T(8,128)S(1)}, u32[]{:S(2)}, u32[]{:S(2)}) collective-permute-start(f32[40,512]{1,0:T(8,128)} %get-tuple-element.219), channel_id=1, source_target_pairs={{1,0},{2,1},{3,2},{4,3},{5,4},{6,5},{7,6},{9,8},{10,9},{11,10},{12... | collective-permute-start | bytes 245768 | tf_op jit(solution)/shard_map/ppermute | solution.py:364
  4.9 4.7 %collective-permute-start.9 = (f32[40,512]{1,0:T(8,128)}, f32[40,512]{1,0:T(8,128)S(1)}, u32[]{:S(2)}, u32[]{:S(2)}) collective-permute-start(f32[40,512]{1,0:T(8,128)} %get-tuple-element.220), channel_id=1, source_target_pairs={{0,1},{1,2},{2,3},{3,4},{4,5},{5,6},{6,7},{8,9},{9,10},{10,11},{11... | collective-permute-start | bytes 245768 | tf_op jit(solution)/shard_map/ppermute | solution.py:365
  9.6 0.1 collective-permute-done.8.refs_8_.from_right
  9.7 0.0 copy-start
  9.7 1.7 %collective-permute-done.9.refs_9_.from_left = f32[40,512]{1,0:T(8,128)S(1)} collective-permute-done((f32[40,512]{1,0:T(8,128)}, f32[40,512]{1,0:T(8,128)S(1)}, u32[]{:S(2)}, u32[]{:S(2)}) %collective-permute-start.9) | collective-permute-done | bytes 81952 | tf_op jit(solution)/shard_map/ppermute | solution.py:365
  11.4 0.0 copy-done
  11.4 0.0 copy-start.2
  11.4 0.6 copy-done.2
  12.0 0.0 copy-done.5
  12.0 0.0 copy-done.7
  12.0 1.9 %shard_map.60 = (f32[40,640]{1,0:T(8,128)}, f32[40,640]{1,0:T(8,128)}) custom-call(s32[1,512,512]{2,1,0:T(8,128)S(1)} %copy-done.7, s32[1,512,512]{2,1,0:T(8,128)S(1)} %copy-done.5, f32[1,512,512]{2,1,0:T(8,128)} %prior.1, f32[1,512,512]{2,1,0:T(8,128)} %weight.1, s32[1,512,512]{2,1,0:T(8,128)S(1)} %copy-done.7, s32[1,512,512]{2,1,0:T(8,128)S(1)} %copy-done.5, ...), custom_call_target="tpu_custom_call" | custom-call | tf_op jit(solution)/shard_map/pallas_call | solution.py:367
  13.9 3.8 %collective-permute-start.10 = (f32[40,640]{1,0:T(8,128)}, f32[40,640]{1,0:T(8,128)S(1)}, u32[]{:S(2)}, u32[]{:S(2)}) collective-permute-start(f32[40,640]{1,0:T(8,128)} %get-tuple-element.221), channel_id=1, source_target_pairs={{8,0},{16,8},{24,16},{9,1},{17,9},{25,17},{10,2},{18,10},{26,18},{... | collective-permute-start | bytes 307208 | tf_op jit(solution)/shard_map/ppermute | solution.py:379
  17.6 4.7 %collective-permute-start.11 = (f32[40,640]{1,0:T(8,128)}, f32[40,640]{1,0:T(8,128)S(1)}, u32[]{:S(2)}, u32[]{:S(2)}) collective-permute-start(f32[40,640]{1,0:T(8,128)} %get-tuple-element.222), channel_id=1, source_target_pairs={{0,8},{8,16},{16,24},{1,9},{9,17},{17,25},{2,10},{10,18},{18,26},{... | collective-permute-start | bytes 307208 | tf_op jit(solution)/shard_map/ppermute | solution.py:380
  22.3 0.6 collective-permute-done.10.from_lower
  22.9 1.4 %collective-permute-done.11.from_upper = f32[40,640]{1,0:T(8,128)S(1)} collective-permute-done((f32[40,640]{1,0:T(8,128)}, f32[40,640]{1,0:T(8,128)S(1)}, u32[]{:S(2)}, u32[]{:S(2)}) %collective-permute-start.11) | collective-permute-done | bytes 102432 | tf_op jit(solution)/shard_map/ppermute | solution.py:380
  24.3 0.0 copy-start.1
  24.3 0.9 %copy-done.1 = f32[40,512]{1,0:T(8,128)S(1)} copy-done((f32[40,512]{1,0:T(8,128)S(1)}, f32[40,512]{1,0:T(8,128)}, u32[]{:S(2)}) %copy-start.1) | copy-done | bytes 81944
  25.2 0.0 copy-start.3
  25.2 0.9 %copy-done.3 = f32[40,512]{1,0:T(8,128)S(1)} copy-done((f32[40,512]{1,0:T(8,128)S(1)}, f32[40,512]{1,0:T(8,128)}, u32[]{:S(2)}) %copy-start.3) | copy-done | bytes 81944
  26.1 15.1 %shard_map.61 = (f32[5,544,128]{2,1,0:T(8,128)S(1)}, f32[5,544,128]{2,1,0:T(8,128)S(1)}, f32[5,544,128]{2,1,0:T(8,128)S(1)}, f32[5,544,128]{2,1,0:T(8,128)S(1)},...) custom-call(s32[1,512,512]{2,1,0:T(8,128)S(1)} %copy-done.7, ...), custom_call_target="tpu_custom_call" | custom-call | tf_op jit(solution)/shard_map/pallas_call | solution.py:384
  41.2 17.7 %all_to_all.31.every = f32[32,1,128]{2,1,0:T(1,128)S(1)} all-to-all(f32[32,1,128]{2,1,0:T(1,128)S(1)} %get-tuple-element.223), channel_id=1, replica_groups=mesh['img'=4,'row'=4,'col'=8] {'row','col'}, dimensions={0} | all-to-all | bytes 32768 | tf_op jit(solution)/shard_map/all_to_all | solution.py:396
  58.9 3.1 %shard_map.62 = (f32[1,512,512]{2,1,0:T(8,128)}, f32[1,512,512]{2,1,0:T(8,128)}, s32[8,128]{1,0:T(8,128)S(1)}) custom-call(f32[32,1,128]{2,1,0:T(1,128)S(1)} %all_to_all.31.every, s32[1,512,512]{2,1,0:T(8,128)S(1)} %copy-done.5, f32[5,544,128]{2,1,0:T(8,128)S(1)} %get-tuple-element.224.refs_0_, f32[5,544,128]{2,1,0:T(8,128)S(1)} %get-tuple-element.225.refs_1_, ...), custom_call_target="tpu_custom_call" | custom-call | tf_op jit(solution)/shard_map/pallas_call | solution.py:398
  61.9 0.5 slice.91
  62.4 0.7 %while.30 = (s32[]{:T(128)}, f32[1,512,512]{2,1,0:T(8,128)}, f32[1,512,512]{2,1,0:T(8,128)}, s32[1,512,512]{2,1,0:T(8,128)S(1)}, f32[1,512,512]{2,1,0:T(8,128)},...) while((s32[]{:T(128)}, f32[1,512,512]{2,1,0:T(8,128)}, ...), condition=%region_9.10_spmd, body=%region_0.9_spmd | while | flops 58720352 | bytes 58419332 | solution.py:410
Async XLA Ops:
  0.6 11.4 %copy-start.5 = (s32[1,512,512]{2,1,0:T(8,128)S(1)}, s32[1,512,512]{2,1,0:T(8,128)}, u32[]{:S(2)}) copy-start(s32[1,512,512]{2,1,0:T(8,128)} %labels.3) | copy-start | bytes 3145732
  0.6 11.4 %copy-start.7 = (s32[1,512,512]{2,1,0:T(8,128)S(1)}, s32[1,512,512]{2,1,0:T(8,128)}, u32[]{:S(2)}) copy-start(s32[1,512,512]{2,1,0:T(8,128)} %edges.1) | copy-start | bytes 3145732
  3.6 6.0 %collective-permute-start.8 = (f32[40,512]{1,0:T(8,128)}, f32[40,512]{1,0:T(8,128)S(1)}, u32[]{:S(2)}, u32[]{:S(2)}) collective-permute-start(f32[40,512]{1,0:T(8,128)} %get-tuple-element.219), channel_id=1, source_target_pairs={{1,0},{2,1},{3,2},{4,3},{5,4},{6,5},{7,6},{9,8},{10,9},{11,10},{12... | collective-permute-start | bytes 245768 | tf_op jit(solution)/shard_map/ppermute | solution.py:364
  4.9 6.4 %collective-permute-start.9 = (f32[40,512]{1,0:T(8,128)}, f32[40,512]{1,0:T(8,128)S(1)}, u32[]{:S(2)}, u32[]{:S(2)}) collective-permute-start(f32[40,512]{1,0:T(8,128)} %get-tuple-element.220), channel_id=1, source_target_pairs={{0,1},{1,2},{2,3},{3,4},{4,5},{5,6},{6,7},{8,9},{9,10},{10,11},{11... | collective-permute-start | bytes 245768 | tf_op jit(solution)/shard_map/ppermute | solution.py:365
  9.7 1.7 %copy-start = (f32[40,512]{1,0:T(8,128)}, f32[40,512]{1,0:T(8,128)S(1)}, u32[]{:S(2)}) copy-start(f32[40,512]{1,0:T(8,128)S(1)} %collective-permute-done.8.refs_8_.from_right) | copy-start | bytes 245764
  11.4 0.6 copy-start.2
  13.9 9.0 %collective-permute-start.10 = (f32[40,640]{1,0:T(8,128)}, f32[40,640]{1,0:T(8,128)S(1)}, u32[]{:S(2)}, u32[]{:S(2)}) collective-permute-start(f32[40,640]{1,0:T(8,128)} %get-tuple-element.221), channel_id=1, source_target_pairs={{8,0},{16,8},{24,16},{9,1},{17,9},{25,17},{10,2},{18,10},{26,18},{... | collective-permute-start | bytes 307208 | tf_op jit(solution)/shard_map/ppermute | solution.py:379
  17.6 6.6 %collective-permute-start.11 = (f32[40,640]{1,0:T(8,128)}, f32[40,640]{1,0:T(8,128)S(1)}, u32[]{:S(2)}, u32[]{:S(2)}) collective-permute-start(f32[40,640]{1,0:T(8,128)} %get-tuple-element.222), channel_id=1, source_target_pairs={{0,8},{8,16},{16,24},{1,9},{9,17},{17,25},{2,10},{10,18},{18,26},{... | collective-permute-start | bytes 307208 | tf_op jit(solution)/shard_map/ppermute | solution.py:380
  24.3 0.9 %copy-start.1 = (f32[40,512]{1,0:T(8,128)S(1)}, f32[40,512]{1,0:T(8,128)}, u32[]{:S(2)}) copy-start(f32[40,512]{1,0:T(8,128)} %copy-done) | copy-start | bytes 245764
  25.2 0.9 %copy-start.3 = (f32[40,512]{1,0:T(8,128)S(1)}, f32[40,512]{1,0:T(8,128)}, u32[]{:S(2)}) copy-start(f32[40,512]{1,0:T(8,128)} %copy-done.2) | copy-start | bytes 245764

commit v3 on v0

v3 whole, which is shorter than its diff:
```python
import functools
import jax
import jax.numpy as jnp
from jax import lax
from jax.experimental import pallas as pl
from jax.experimental.pallas import tpu as pltpu
from jax.sharding import PartitionSpec as P

ITERS = 8
HALO = 8
LANES = 128
LOW, HIGH = 0.05, 7.5
CENTRE, RADIUS = (HIGH + LOW) / 2, (HIGH - LOW) / 2
AMPLIFICATION = 24.0
VMEM = pl.BlockSpec(memory_space=pltpu.VMEM)
ANY = pl.BlockSpec(memory_space=pl.ANY)


def with_halo(array, sides, width):
    edges = {}
    for axis, dim in sides:
        count, length = (lax.axis_size(axis), array.shape[dim])
        up = [(i, (i + 1) % count) for i in range(count - 1)]
        last = lax.slice_in_dim(array, length - width, length, axis=dim)
        first = lax.slice_in_dim(array, 0, width, axis=dim)
        edges[dim] = (
            lax.ppermute(last, axis, up),
            lax.ppermute(first, axis, [(b, a) for a, b in up]),
        )
    done = []
    for _, dim in sides:
        low, high = edges[dim]
        around = [(width, width) if d in done else (0, 0) for d in range(array.ndim)]
        array = jnp.concatenate([jnp.pad(low, around), array, jnp.pad(high, around)], axis=dim)
        done.append(dim)
    return array


def total(value, axis):
    count = lax.axis_size(axis)
    flat = value.reshape(1, 1, 1)
    every = lax.all_to_all(jnp.broadcast_to(flat, (count, 1, 1)), axis, 0, 0, tiled=True)
    return every.sum()


def neighbours(field, right, left, down, upper):
    padded = with_halo(field, (("row", 1), ("col", 2)), 1)
    return (
        right * padded[:, 1:-1, 2:]
        + left * padded[:, 1:-1, :-2]
        + down * padded[:, 2:, 1:-1]
        + upper * padded[:, :-2, 1:-1]
    )


def plain(edges, labels, prior, data_weight):
    right = (edges % 2).astype(jnp.float32)
    left = (edges // 2 % 2).astype(jnp.float32)
    down = (edges // 4 % 2).astype(jnp.float32)
    upper = (edges // 8 % 2).astype(jnp.float32)
    degree = right + left + down + upper
    free = (labels == 0).astype(jnp.float32)
    anchor = (labels == 1).astype(jnp.float32)
    diag_term = degree + data_weight

    def nearby(field):
        return neighbours(field, right, left, down, upper)

    rhs = free * (data_weight * prior + nearby(anchor))

    def step(_, carry):
        result, residual, direction, norm_now = carry
        image_v = free * (diag_term * direction - nearby(direction))
        alpha = norm_now / total(jnp.sum(direction * image_v), ("row", "col"))
        result = result + alpha * direction
        residual = residual - alpha * image_v
        norm_next = total(jnp.sum(residual * residual), ("row", "col"))
        direction = residual + (norm_next / norm_now) * direction
        return result, residual, direction, norm_next

    start = (jnp.zeros_like(rhs), rhs, rhs, total(jnp.sum(rhs * rhs), ("row", "col")))
    result, residual, _, _ = lax.fori_loop(0, ITERS, step, start)
    return anchor + result, residual


WIDTH = HALO + 1
LINES = 40
TOP_OF = ((0, 0, 8), (2, 8, 8), (3, 16, 8), (1, 24, 16))


def lane_ids(rows):
    return lax.broadcasted_iota(jnp.int32, (rows, LANES), 1)


def turn(x, by):
    return pltpu.roll(x, by % LANES, 1) if by % LANES else x


def col_pack(edges, labels, prior, weight, to_left, to_right, ints, floats, sem):
    arrays = (edges, labels, prior, weight)
    rows, cols = edges.shape[1], edges.shape[2]
    lane = lane_ids(LANES)

    def copy(side, a, chunk):
        at = pl.ds(chunk * LANES, LANES)
        dst = (ints if a < 2 else floats).at[side, a % 2, at, :]
        return pltpu.make_async_copy(
            arrays[a].at[0, at, pl.ds(side * (cols - LANES), LANES)], dst, sem.at[side, a, chunk]
        )

    chunks = rows // LANES
    for chunk in range(chunks):
        for side in range(2):
            for a in range(4):
                copy(side, a, chunk).start()
    for chunk in range(chunks):
        at = slice(chunk * LANES, (chunk + 1) * LANES)
        for side, out, base in ((0, to_left, 0), (1, to_right, LANES - WIDTH)):
            packed = None
            for a in range(4):
                copy(side, a, chunk).wait()
                x = (ints if a < 2 else floats)[side, a % 2, at, :].astype(jnp.float32)
                x = turn(x, a * WIDTH - base)
                packed = x if packed is None else jnp.where(lane < a * WIDTH, packed, x)
            out[:, at] = jnp.swapaxes(packed, 0, 1)[:LINES]


def load(edges, labels, prior, weight, code_t, lab_t, prior_t, weight_t, sem):
    rows = edges.shape[1]
    tiles = code_t.shape[0]
    copies = []
    for a, (src, dst, at) in enumerate(
        ((edges, code_t, 0), (labels, lab_t, HALO), (prior, prior_t, 0), (weight, weight_t, 0))
    ):
        for j in range(tiles):
            copies.append(
                pltpu.make_async_copy(
                    src.at[0, :, pl.ds(j * LANES, LANES)],
                    dst.at[j, pl.ds(at, rows), :],
                    sem.at[a, j],
                )
            )
    for copy in copies:
        copy.start()
    seeds = jnp.full((HALO, LANES), 2, jnp.int32)
    for j in range(tiles):
        lab_t[j, :HALO, :] = seeds
        lab_t[j, HALO + rows :, :] = seeds
    for copy in copies:
        copy.wait()


def side_tiles(from_right, from_left, at):
    pad = jnp.zeros((LANES - LINES, LANES), jnp.float32)
    r = jnp.swapaxes(jnp.concatenate([from_right[:, at : at + LANES], pad], 0), 0, 1)
    l = jnp.swapaxes(jnp.concatenate([from_left[:, at : at + LANES], pad], 0), 0, 1)
    lane = lane_ids(LANES)
    tiles = []
    for a in range(4):
        right = turn(r, -a * WIDTH)
        left = turn(l, LANES - WIDTH - a * WIDTH)
        outside = 2.0 if a == 1 else 0.0
        tiles.append(jnp.where(lane < WIDTH, right, jnp.where(lane >= LANES - WIDTH, left, outside)))
    return tiles


def row_pack(code_t, lab_t, prior_t, weight_t, from_right, from_left, to_upper, to_lower):
    tiles, rows = code_t.shape[0], code_t.shape[1]
    refs = (code_t, lab_t, prior_t, weight_t)
    for out, at in ((to_upper, 0), (to_lower, rows - LANES)):
        side = side_tiles(from_right, from_left, at)
        for a, line, n in TOP_OF:
            first = 0 if at == 0 else rows - n
            skip = HALO if a == 1 else 0
            for j in range(tiles):
                x = refs[a][j, skip + first : skip + first + n, :].astype(jnp.float32)
                out[line : line + n, j * LANES : (j + 1) * LANES] = x
            out[line : line + n, tiles * LANES :] = side[a][first - at : first - at + n]


def shifted(tiles, lane, by):
    count = len(tiles)
    turned = [turn(t, by) for t in tiles]
    if by > 0:
        return [jnp.where(lane == 0, turned[j - 1], turned[j]) for j in range(count)]
    return [jnp.where(lane == LANES - 1, turned[(j + 1) % count], turned[j]) for j in range(count)]


SCALE = 2.0 / RADIUS


def decode(lane, code, lab, lab_d, lab_u, prior, weight):
    lab_r, lab_l = shifted(lab, lane, -1), shifted(lab, lane, 1)
    er, ed, eu, diag, rhs = [], [], [], [], []
    for j in range(len(code)):
        r = (code[j] & 1).astype(jnp.float32)
        l = ((code[j] >> 1) & 1).astype(jnp.float32)
        d = ((code[j] >> 2) & 1).astype(jnp.float32)
        u = ((code[j] >> 3) & 1).astype(jnp.float32)
        free = lab[j] == 0
        one = jnp.where(free, SCALE, 0.0)
        er.append(jnp.where(lab_r[j] == 0, one, 0.0) * r)
        ed.append(one * d)
        eu.append(one * u)
        diag.append(SCALE * ((r + l + d + u) + weight[j] - CENTRE))
        near = (
            jnp.where(lab_r[j] == 1, r, 0.0)
            + jnp.where(lab_l[j] == 1, l, 0.0)
            + jnp.where(lab_d[j] == 1, d, 0.0)
            + jnp.where(lab_u[j] == 1, u, 0.0)
        )
        rhs.append(jnp.where(free, weight[j] * prior[j] + near, 0.0))
    return er, ed, eu, diag, rhs


def recurrence(lane, k, v, v_d, v_u, before, er, ed, eu, diag):
    v_r = shifted(v, lane, -1)
    g = shifted([er[j] * v[j] for j in range(len(v))], lane, 1)
    new = []
    for j in range(len(v)):
        x = diag[j] * v[j] - (er[j] * v_r[j] + g[j])
        x = x - (ed[j] * v_d[j] + eu[j] * v_u[j])
        new.append(0.5 * x if k == 0 else x - before[j])
    return new


def summed(a, b):
    t = [x * y for x, y in zip(a, b)]
    while len(t) > 1:
        t = [t[q] + t[q + 1] for q in range(0, len(t) - 1, 2)] + ([t[-1]] if len(t) % 2 else [])
    return t[0]


def interior(code_t, lab_t, prior_t, weight_t, from_right, from_left, *refs):
    n = ITERS + 1
    field, (er_t, ed_t, eu_t, diag_t, side_lab, sums) = refs[:n], refs[n : n + 6]
    side_code, side_prior, side_weight = refs[n + 6 :]
    inner, rows = code_t.shape[0], code_t.shape[1]
    tiles = inner + 1
    lane = lane_ids(8)
    for at in range(0, rows, LANES):
        side = side_tiles(from_right, from_left, at)
        side_code[at : at + LANES, :] = side[0].astype(jnp.int32)
        side_lab[HALO + at : HALO + at + LANES, :] = side[1].astype(jnp.int32)
        side_prior[at : at + LANES, :] = side[2]
        side_weight[at : at + LANES, :] = side[3]
    seeds = jnp.full((HALO, LANES), 2, jnp.int32)
    side_lab[:HALO, :] = seeds
    side_lab[HALO + rows :, :] = seeds
    zero = jnp.zeros((8, LANES), jnp.float32)
    for k in range(1, ITERS):
        for j in range(tiles):
            field[k][j, :8, :] = zero
            field[k][j, rows - 8 :, :] = zero

    def read(ref, side, s):
        return [ref[j, pl.ds(s, 8), :] for j in range(inner)] + [side[pl.ds(s, 8), :]]

    def prepare(i, _):
        s = pl.multiple_of(8 * i, 8)
        here = pl.ds(s, 8)
        done = decode(
            lane,
            read(code_t, side_code, s),
            read(lab_t, side_lab, pl.multiple_of(s + HALO, 8)),
            read(lab_t, side_lab, s + HALO + 1),
            read(lab_t, side_lab, s + HALO - 1),
            read(prior_t, side_prior, s),
            read(weight_t, side_weight, s),
        )
        for ref, values in zip((er_t, ed_t, eu_t, diag_t, field[0]), done):
            for j in range(tiles):
                ref[j, here, :] = values[j]
        return 0

    lax.fori_loop(0, rows // 8, prepare, 0, unroll=8)

    def at_rows(ref, s):
        return [ref[j, pl.ds(s, 8), :] for j in range(tiles)]

    def advance(k, s):
        v = at_rows(field[k], s)
        new = recurrence(
            lane, k, v, at_rows(field[k], s + 1), at_rows(field[k], s - 1),
            at_rows(field[k - 1], s) if k else None,
            at_rows(er_t, s), at_rows(ed_t, s), at_rows(eu_t, s), at_rows(diag_t, s),
        )
        for j in range(tiles):
            field[k + 1][j, pl.ds(s, 8), :] = new[j]
        return v[:inner], new[:inner]

    count = 0
    for k in range(ITERS):
        last = k == ITERS - 1

        def body(i, carry, k=k, last=last):
            v, new = advance(k, pl.multiple_of(2 * HALO + 8 * i, 8))
            pairs = [(v, v), (v, new)] + ([(new, new)] if last else [])
            return tuple(acc + summed(a, b) for acc, (a, b) in zip(carry, pairs))

        if not last:
            advance(k, 8)
            advance(k, rows - 16)
        acc = (zero,) * (3 if last else 2)
        acc = lax.fori_loop(0, (rows - 4 * HALO) // 8, body, acc, unroll=15)
        for value in acc:
            sums[count] = value
            count += 1


def band(*refs):
    n = ITERS
    field, (er_t, ed_t, eu_t, diag_t, lab_t, side_lab) = refs[:n], refs[n : n + 6]
    sums, from_upper, from_lower = refs[n + 6 : n + 9]
    out, edge, labs, grid = refs[n + 9 :]
    inner, rows = lab_t.shape[0], er_t.shape[1]
    tiles = inner + 1
    lane = lane_ids(8)
    sub = lax.broadcasted_iota(jnp.int32, (8, LANES), 0)
    zero = jnp.zeros((8, LANES), jnp.float32)

    def lab_own(first):
        return [lab_t[j, HALO + first : HALO + first + 8, :] for j in range(inner)] + [
            side_lab[HALO + first : HALO + first + 8, :]
        ]

    def own(ref, first):
        return [ref[j, first : first + 8, :] for j in range(tiles)]

    terms = []
    for end, (message, first) in enumerate(((from_upper, 0), (from_lower, rows - 8))):
        def line(at, count=8, message=message):
            return [message[at : at + count, j * LANES : (j + 1) * LANES] for j in range(tiles)]

        beyond, mine = (0, 16) if end == 0 else (8, 0)
        for j, (x, y) in enumerate(zip(line(24, 16), lab_own(first))):
            labs[end, j, beyond : beyond + 16, :] = x.astype(jnp.int32)
            labs[end, j, mine : mine + 8, :] = y
        near = lambda at: [labs[end, j, at : at + 8, :] for j in range(tiles)]
        *halo, rhs = decode(
            lane, [x.astype(jnp.int32) for x in line(0)], near(8), near(9), near(7), line(8), line(16)
        )
        if end == 0:
            add = [jnp.where((sub == 0) & (x == 1) & (c > 0.0), 1.0, 0.0) for x, c in zip(near(15), own(eu_t, 0))]
        else:
            add = [jnp.where((sub == 7) & (x == 1) & (c > 0.0), 1.0, 0.0) for x, c in zip(near(1), own(ed_t, first))]
        outer = [x + y for x, y in zip(own(field[0], first), add)]
        step = 8 if end == 0 else -8
        next_in = own(field[0], first + step)
        coefficient = [[own(ref, f) for ref in (er_t, ed_t, eu_t, diag_t)] for f in (first, first + step)]
        trio = [(halo, rhs), (coefficient[0], outer), (coefficient[1], next_in)]
        if end == 1:
            trio.reverse()
        terms.append([t[0] for t in trio])
        for q, (_, start) in enumerate(trio):
            for j in range(tiles):
                grid[end, 0, j, 8 + 8 * q : 16 + 8 * q, :] = start[j]
        guard, inside, take = (0, 32, 16) if end == 0 else (32, 0, rows - 24)
        for k in range(ITERS):
            for j in range(tiles):
                grid[end, k, j, guard : guard + 8, :] = zero
                grid[end, k, j, inside : inside + 8, :] = field[k][j, take : take + 8, :]

    parts = [sums[q] for q in range(2 * ITERS + 1)]
    for k in range(ITERS):
        for end in range(2):
            at = lambda kk, s: [grid[end, kk, j, s : s + 8, :] for j in range(tiles)]
            for q in range(3):
                s = 8 + 8 * q
                v = at(k, s)
                new = recurrence(
                    lane, k, v, at(k, s + 1), at(k, s - 1), at(k - 1, s) if k else None, *terms[end][q]
                )
                for j in range(tiles):
                    grid[end, k + 1, j, s : s + 8, :] = new[j]
                mine = q - 1 if end == 0 else q
                if 0 <= mine < 2:
                    v, new = v[:inner], new[:inner]
                    parts[2 * k] = parts[2 * k] + summed(v, v)
                    parts[2 * k + 1] = parts[2 * k + 1] + summed(v, new)
                    for j in range(inner):
                        edge[k, end, j, 8 * mine : 8 * mine + 8, :] = v[j]
                    if k == ITERS - 1:
                        parts[2 * k + 2] = parts[2 * k + 2] + summed(new, new)
                        for j in range(inner):
                            edge[k + 1, end, j, 8 * mine : 8 * mine + 8, :] = new[j]

    every = jnp.zeros((1, LANES), jnp.float32)
    for q, acc in enumerate(parts):
        one = jnp.sum(jnp.sum(acc, axis=0, keepdims=True), axis=1, keepdims=True)
        every = jnp.where(lane_ids(1) == q, one, every)
    out[...] = jnp.broadcast_to(every[None], out.shape)


def coefficients(dots):
    n = ITERS
    inv = 1.0 / dots[0]
    moment = [jnp.ones_like(dots[0]), dots[1] * inv]
    for k in range(1, n + 1):
        moment.append(2.0 * (dots[2 * k] * inv) - moment[0])
        if k < n:
            moment.append(2.0 * (dots[2 * k + 1] * inv) - moment[1])
    gram = [[0.5 * (moment[i + j] + moment[abs(i - j)]) for j in range(n + 1)] for i in range(n + 1)]

    def image(p):
        q = [CENTRE * x for x in p] + [jnp.zeros_like(p[0])]
        for i, x in enumerate(p):
            if i == 0:
                q[1] = q[1] + RADIUS * x
            else:
                q[i + 1] = q[i + 1] + (RADIUS / 2) * x
                q[i - 1] = q[i - 1] + (RADIUS / 2) * x
        return q

    def product(a, b):
        sums = None
        for i, x in enumerate(a):
            t = gram[i][0] * b[0]
            for j in range(1, len(b)):
                t = t + gram[i][j] * b[j]
            sums = x * t if sums is None else sums + x * t
        return sums

    zero = jnp.zeros_like(inv)
    x, r, p = [], [moment[0]], [moment[0]]
    now = moment[0]
    for _ in range(n):
        q = image(p)
        alpha = now / product(p, q)
        x = [(x[i] if i < len(x) else zero) + alpha * p[i] for i in range(len(p))]
        r = [(r[i] if i < len(r) else zero) - alpha * q[i] for i in range(len(q))]
        following = product(r, r)
        beta = following / now
        p = [r[i] + (beta * p[i] if i < len(p) else zero) for i in range(len(r))]
        now = following
    size = zero
    for i in range(n + 1):
        size = size + jnp.abs(r[i]) * jnp.sqrt(jnp.maximum(gram[i][i], 0.0))
    good = (size * size <= (AMPLIFICATION * AMPLIFICATION) * now) & (now > 0.0)
    return x, r, good


def combine(every, lab_t, edge, *refs):
    n = ITERS + 1
    field, (labeling, residual, flag, sol_s, res_s, sem) = refs[:n], refs[n:]
    inner, rows = field[0].shape[0] - 1, field[0].shape[1]
    g = jnp.sum(every[:, 0, :], axis=0, keepdims=True)
    dots = [jnp.broadcast_to(g[:, q : q + 1], (8, LANES)) for q in range(2 * ITERS + 1)]
    x, r, good = coefficients(dots)
    flag[...] = good.astype(jnp.int32)

    def put(s, source):
        for j in range(inner):
            lanes = slice(j * LANES, (j + 1) * LANES)
            sol = jnp.where(lab_t[j, pl.ds(s + HALO, 8), :] == 1, 1.0, 0.0)
            res = None
            for k in range(n):
                t = source(k, j)
                res = r[k] * t if res is None else res + r[k] * t
                if k < ITERS:
                    sol = sol + x[k] * t
            sol_s[pl.ds(s, 8), lanes] = sol
            res_s[pl.ds(s, 8), lanes] = res

    def body(i, _):
        s = pl.multiple_of(8 * i, 8)
        put(s, lambda k, j: field[k][j, pl.ds(s, 8), :])
        return 0

    copies = []
    chunk = 64
    for c in range(rows // chunk):
        first, last = c * chunk // 8, (c + 1) * chunk // 8
        if c == 0:
            for q in range(2):
                put(8 * q, lambda k, j: edge[k, 0, j, 8 * q : 8 * q + 8, :])
            first += 2
        if (c + 1) * chunk == rows:
            last -= 2
        lax.fori_loop(first, last, body, 0, unroll=2)
        if (c + 1) * chunk == rows:
            for q in range(2):
                put(rows - 16 + 8 * q, lambda k, j: edge[k, 1, j, 8 * q : 8 * q + 8, :])
        at = pl.ds(c * chunk, chunk)
        for q, (src, dst) in enumerate(((sol_s, labeling), (res_s, residual))):
            copy = pltpu.make_async_copy(src.at[at, :], dst.at[0, at, :], sem.at[c, q])
            copy.start()
            copies.append(copy)
    for copy in copies:
        copy.wait()


def both_ways(axis, backward, forward):
    up = [(i, i + 1) for i in range(lax.axis_size(axis) - 1)]
    return (
        lax.ppermute(backward, axis, [(b, a) for a, b in up]),
        lax.ppermute(forward, axis, up),
    )


def call(body, in_specs, outs, scratch, mib, flops, operands, out_specs=None):
    return pl.pallas_call(
        body,
        in_specs=in_specs,
        out_specs=out_specs or [VMEM] * len(outs),
        out_shape=outs,
        scratch_shapes=scratch,
        compiler_params=pltpu.CompilerParams(vmem_limit_bytes=mib * 1024 * 1024),
        cost_estimate=pl.CostEstimate(flops=flops, bytes_accessed=1 << 20, transcendentals=0),
    )(*operands)


def per_device(edges, labels, prior, data_weight):
    arrays = (edges, labels, prior, data_weight)
    _, rows, cols = edges.shape
    f32, i32 = jnp.float32, jnp.int32
    shape = jax.ShapeDtypeStruct
    inner = cols // LANES
    tiles = inner + 1
    dma = pltpu.SemaphoreType.DMA

    to_left, to_right = call(
        col_pack, [ANY] * 4, [shape((LINES, rows), f32)] * 2,
        [
            pltpu.VMEM((2, 2, rows, LANES), i32),
            pltpu.VMEM((2, 2, rows, LANES), f32),
            dma((2, 4, rows // LANES)),
        ],
        6, 1 << 20, arrays,
    )
    from_right, from_left = both_ways("col", to_left, to_right)

    block = call(
        load, [ANY] * 4,
        [
            shape((inner, rows, LANES), i32),
            shape((inner, rows + 2 * HALO, LANES), i32),
            shape((inner, rows, LANES), f32),
            shape((inner, rows, LANES), f32),
        ],
        [dma((4, inner))], 6, 1 << 24, arrays,
    )
    to_upper, to_lower = call(
        row_pack, [VMEM] * 6, [shape((LINES, tiles * LANES), f32)] * 2, [],
        4, 1 << 20, (*block, from_right, from_left),
    )
    from_lower, from_upper = both_ways("row", to_upper, to_lower)

    n = ITERS + 1
    out = call(
        interior, [VMEM] * 6,
        [shape((tiles, rows, LANES), f32)] * (n + 4)
        + [shape((rows + 2 * HALO, LANES), i32), shape((2 * ITERS + 1, 8, LANES), f32)],
        [pltpu.VMEM((rows, LANES), i32), pltpu.VMEM((rows, LANES), f32), pltpu.VMEM((rows, LANES), f32)],
        16, 1 << 26, (*block, from_right, from_left),
    )
    field, terms, side_lab, sums = out[:n], out[n : n + 4], out[n + 4], out[n + 5]
    group = lax.axis_size(("row", "col"))
    sums, edge = call(
        band, [VMEM] * (ITERS + 9),
        [shape((group, 1, LANES), f32), shape((n, 2, inner, 2 * HALO, LANES), f32)],
        [pltpu.VMEM((2, tiles, 24, LANES), i32), pltpu.VMEM((2, n, tiles, 40, LANES), f32)],
        6, 1 << 20, (*field[:ITERS], *terms, block[1], side_lab, sums, from_upper, from_lower),
    )
    every = lax.all_to_all(sums, ("row", "col"), 0, 0, tiled=True)

    labeling, residual, flag = call(
        combine, [VMEM] * (n + 3),
        [shape(edges.shape, f32)] * 2 + [shape((8, LANES), i32)],
        [pltpu.VMEM((rows, cols), f32)] * 2 + [dma((rows // 64, 2))],
        4, 1 << 20, (every, block[1], edge, *field), out_specs=[ANY, ANY, VMEM],
    )

    def again(carry):
        return (jnp.int32(1), *plain(edges, labels, prior, data_weight))

    _, labeling, residual = lax.while_loop(
        lambda carry: carry[0] == 0, again, (flag[0, 0], labeling, residual)
    )
    return labeling, residual


def solution(mesh):
    spec = P("img", "row", "col")
    return jax.shard_map(
        per_device, mesh=mesh, in_specs=(spec,) * 4, out_specs=(spec,) * 2, check_vma=False
    )
```

time: 410 us -> 56.7 us (0.14); the launches traced: 404 us -> 56.5 us
  starting transfers between devices: 122 us -> 14.4 us
  other arithmetic: 94.7 us -> 0 us
  blocking collectives: 110 us -> 17.3 us
  waiting for transfers between devices: 41.4 us -> 0.68 us
  between operations: 29.8 us -> 0.96 us
  Pallas kernels: 0 us -> 21.9 us
  local copies, waits for them, and re-layouts: 6.29 us -> 0.56 us
    ppermute x36 -> x4, starting transfers between devices: 122 us -> 14.4 us  [the longest x2 11.2 us: both_ways(): lax.ppermute(forward, axis, up)]
    all_to_all x8 -> x1, blocking collectives: 110 us -> 17.3 us  [per_device(): every = lax.all_to_all(sums, ('row', 'col'), 0, 0, tiled=True)]
    reduce_sum x16 -> x0, other arithmetic: 50.8 us -> none  [the longest x8 50.4 us: paired_sums(): jnp.sum(residual * residual, axis=(1, 2))]
    ppermute x36 -> x4, waiting for transfers between devices: 41.4 us -> 0.68 us  [the longest x2 0.67 us: both_ways(): lax.ppermute(forward, axis, up)]
    pallas_call x0 -> x6, Pallas kernels: none -> 21.9 us  [call(): pl.pallas_call(body, in_specs=in_specs, out_specs=out_specs or [VMEM] * l...]
    sub x8 -> x0, other arithmetic: 20.4 us -> none  [per_device(): residual = residual - alpha[:, None, None] * along]
    concatenate x8 -> x0, other arithmetic: 10.5 us -> none  [together(): jnp.concatenate([a.reshape(-1) for a in arrays])]
    add x1 -> x0, other arithmetic: 5.75 us -> none  [per_device(): return (anchor + solution, residual)]
  transfers between devices with their start and end apart: 36 -> 4, of which waited for: 18 -> 1; matrix products, arithmetic and copies ran while one was open for 0% -> 0% of each run, Pallas kernels for 0% -> 24%
where the time goes in v3:
time: 56.7 us; the launch traced here: 56.5 us
  Pallas kernels  21.9 us (39%)
  blocking collectives  17.3 us (31%)
  starting transfers between devices  14.4 us (25%)
  between operations  0.96 us (2%)
  loops' own time  0.82 us (1%)
  waiting for transfers between devices  0.68 us (1%)
    pallas_call x6, Pallas kernels, call(): pl.pallas_call(body, in_specs=in_specs, out_specs=out_specs or [VMEM] * l...  21.9 us
    all_to_all x1, blocking collectives, per_device(): every = lax.all_to_all(sums, ('row', 'col'), 0, 0, tiled=True)  17.3 us
    ppermute x2, starting transfers between devices, both_ways(): lax.ppermute(forward, axis, up)  11.2 us
    ppermute x2, starting transfers between devices, both_ways(): lax.ppermute(backward, axis, [(b, a) for a, b in up])  3.21 us
  transfers between devices with their start and end apart: 4, of which 1 were waited for; matrix products, arithmetic and copies ran while one was open for 0% of the time, Pallas kernels for 24%

profile of v3, /device:TPU:1, one launch (start us, length us, event | category | flops | bytes accessed | tf_op | source)
XLA Modules:
  0.0 56.5 jit_solution(6288298995798855487)
XLA Ops:
  0.6 0.0 copy-start.6
  0.6 0.0 copy-start.5
  0.7 0.0 copy-start.4
  0.7 0.0 copy-start.2
  0.7 4.2 %shard_map.60 = (f32[40,512]{1,0:T(8,128)S(1)}, f32[40,512]{1,0:T(8,128)S(1)}) custom-call(s32[1,512,512]{2,1,0:T(8,128)} %edges.3, s32[1,512,512]{2,1,0:T(8,128)} %labels.3, f32[1,512,512]{2,1,0:T(8,128)} %prior.3, f32[1,512,512]{2,1,0:T(8,128)} %weight.3), custom_call_target="tpu_custom_call" | custom-call | flops 1048576 | bytes 1048576 | tf_op jit(solution)/shard_map/pallas_call | solution.py:502
  4.9 1.3 %collective-permute-start.8 = (f32[40,512]{1,0:T(8,128)S(1)}, f32[40,512]{1,0:T(8,128)S(1)}, u32[]{:S(2)}, u32[]{:S(2)}) collective-permute-start(f32[40,512]{1,0:T(8,128)S(1)} %get-tuple-element.234), channel_id=1, source_target_pairs={{1,0},{2,1},{3,2},{4,3},{5,4},{6,5},{7,6},{9,8},{10,9},{11,10},{12... | collective-permute-start | bytes 245768 | tf_op jit(solution)/shard_map/ppermute | solution.py:496
  6.2 4.7 %collective-permute-start.9 = (f32[40,512]{1,0:T(8,128)S(1)}, f32[40,512]{1,0:T(8,128)S(1)}, u32[]{:S(2)}, u32[]{:S(2)}) collective-permute-start(f32[40,512]{1,0:T(8,128)S(1)} %get-tuple-element.235), channel_id=1, source_target_pairs={{0,1},{1,2},{2,3},{3,4},{4,5},{5,6},{6,7},{8,9},{9,10},{10,11},{11... | collective-permute-start | bytes 245768 | tf_op jit(solution)/shard_map/ppermute | solution.py:497
  10.8 0.0 copy-done.6
  10.8 0.0 copy-done.5
  10.8 0.0 copy-done.4
  10.9 0.0 copy-done.2
  10.9 0.7 %shard_map.59 = (s32[4,512,128]{2,1,0:T(8,128)S(1)}, s32[4,528,128]{2,1,0:T(8,128)S(1)}, f32[4,512,128]{2,1,0:T(8,128)S(1)}, f32[4,512,128]{2,1,0:T(8,128)S(1)}) custom-call(s32[1,512,512]{2,1,0:T(8,128)S(1)} %copy-done.2, s32[1,512,512]{2,1,0:T(8,128)S(1)} %copy-done.4, f32[1,512,512]{2,1,0:T(8,128)S(1)} %copy-done.5, f32[1,512,512]{2,1,0:T(8,128)S(1)} %copy-done.6), custom_call_target="tpu_custom_call" | custom-call | flops 16777216 | bytes 1048576 | tf_op jit(solution)/shard_map/pallas_call | solution.py:502
  11.6 0.0 collective-permute-done.8.from_right
  11.6 0.7 %collective-permute-done.9.from_left = f32[40,512]{1,0:T(8,128)S(1)} collective-permute-done((f32[40,512]{1,0:T(8,128)S(1)}, f32[40,512]{1,0:T(8,128)S(1)}, u32[]{:S(2)}, u32[]{:S(2)}) %collective-permute-start.9) | collective-permute-done | bytes 81952 | tf_op jit(solution)/shard_map/ppermute | solution.py:497
  12.3 0.2 shard_map.62
  12.5 6.5 %collective-permute-start.10 = (f32[40,640]{1,0:T(8,128)S(1)}, f32[40,640]{1,0:T(8,128)S(1)}, u32[]{:S(2)}, u32[]{:S(2)}) collective-permute-start(f32[40,640]{1,0:T(8,128)S(1)} %get-tuple-element.250), channel_id=1, source_target_pairs={{0,8},{8,16},{16,24},{1,9},{9,17},{17,25},{2,10},{10,18},{18,26},{... | collective-permute-start | bytes 307208 | tf_op jit(solution)/shard_map/ppermute | solution.py:497
  19.0 1.9 %collective-permute-start.11 = (f32[40,640]{1,0:T(8,128)S(1)}, f32[40,640]{1,0:T(8,128)S(1)}, u32[]{:S(2)}, u32[]{:S(2)}) collective-permute-start(f32[40,640]{1,0:T(8,128)S(1)} %get-tuple-element.251), channel_id=1, source_target_pairs={{8,0},{16,8},{24,16},{9,1},{17,9},{25,17},{10,2},{18,10},{26,18},{... | collective-permute-start | bytes 307208 | tf_op jit(solution)/shard_map/ppermute | solution.py:496
  21.0 13.0 %shard_map.61 = (f32[5,512,128]{2,1,0:T(8,128)S(1)}, f32[5,512,128]{2,1,0:T(8,128)S(1)}, f32[5,512,128]{2,1,0:T(8,128)S(1)}, f32[5,512,128]{2,1,0:T(8,128)S(1)},...) custom-call(s32[4,512,128]{2,1,0:T(8,128)S(1)} %get-tuple-element.23, ...), custom_call_target="tpu_custom_call" | custom-call | flops 67108864 | bytes 1048576 | tf_op jit(solution)/shard_map/pallas_call | solution.py:502
  33.9 0.0 collective-permute-done.10.refs_15_
  34.0 0.0 collective-permute-done.11.refs_16_
  34.0 1.0 %shard_map.63 = (f32[32,1,128]{2,1,0:T(1,128)S(1)}, f32[9,2,4,16,128]{4,3,2,1,0:T(8,128)S(1)}) custom-call(f32[5,512,128]{2,1,0:T(8,128)S(1)} %get-tuple-element.236.refs_0_, f32[5,512,128]{2,1,0:T(8,128)S(1)} %get-tuple-element.237.refs_1_, f32[5,512,128]{2,1,0:T(8,128)S(1)} %get-tuple-element.238.refs_2_, f32[5,512,128]{2,1,0:T(8,128)S(1)} %get-tuple-element.239.refs_3_, ...), custom_call_target="tpu_custom_call" | custom-call | flops 1048576 | bytes 1048576 | tf_op jit(solution)/shard_map/pallas_call | solution.py:502
  35.0 17.3 %all_to_all.31.every = f32[32,1,128]{2,1,0:T(1,128)S(1)} all-to-all(f32[32,1,128]{2,1,0:T(1,128)S(1)} %get-tuple-element.252), channel_id=1, replica_groups=mesh['img'=4,'row'=4,'col'=8] {'row','col'}, dimensions={0} | all-to-all | bytes 32768 | tf_op jit(solution)/shard_map/all_to_all | solution.py:565
  52.2 2.7 %shard_map.64 = (f32[1,512,512]{2,1,0:T(8,128)}, f32[1,512,512]{2,1,0:T(8,128)}, s32[8,128]{1,0:T(8,128)S(1)}) custom-call(f32[32,1,128]{2,1,0:T(1,128)S(1)} %all_to_all.31.every, s32[4,528,128]{2,1,0:T(8,128)S(1)} %get-tuple-element.231.lab_t.refs_12_, f32[9,2,4,16,128]{4,3,2,1,0:T(8,128)S(1)} %get-tuple-element.253.edge, ...), custom_call_target="tpu_custom_call" | custom-call | flops 1048576 | bytes 1048576 | tf_op jit(solution)/shard_map/pallas_call | solution.py:502
  55.0 0.5 slice.91
  55.5 0.8 %while.30 = (s32[]{:T(128)}, f32[1,512,512]{2,1,0:T(8,128)}, f32[1,512,512]{2,1,0:T(8,128)}, s32[1,512,512]{2,1,0:T(8,128)}, f32[1,512,512]{2,1,0:T(8,128)}, /*i...) while((s32[]{:T(128)}, f32[1,512,512]{2,1,0:T(8,128)}, f32[1,512,512]{2,1,0:T(8,128)}, ...), condition=%region_9.10_spmd, body=%region_0.9_spmd | while | flops 58720352 | bytes 45852768 | solution.py:577
Async XLA Ops:
  0.6 10.2 %copy-start.6 = (f32[1,512,512]{2,1,0:T(8,128)S(1)}, f32[1,512,512]{2,1,0:T(8,128)}, u32[]{:S(2)}) copy-start(f32[1,512,512]{2,1,0:T(8,128)} %weight.3) | copy-start | bytes 3145732
  0.6 10.2 %copy-start.5 = (f32[1,512,512]{2,1,0:T(8,128)S(1)}, f32[1,512,512]{2,1,0:T(8,128)}, u32[]{:S(2)}) copy-start(f32[1,512,512]{2,1,0:T(8,128)} %prior.3) | copy-start | bytes 3145732
  0.7 10.2 %copy-start.4 = (s32[1,512,512]{2,1,0:T(8,128)S(1)}, s32[1,512,512]{2,1,0:T(8,128)}, u32[]{:S(2)}) copy-start(s32[1,512,512]{2,1,0:T(8,128)} %labels.3) | copy-start | bytes 3145732
  0.7 10.2 %copy-start.2 = (s32[1,512,512]{2,1,0:T(8,128)S(1)}, s32[1,512,512]{2,1,0:T(8,128)}, u32[]{:S(2)}) copy-start(s32[1,512,512]{2,1,0:T(8,128)} %edges.3) | copy-start | bytes 3145732
  4.9 6.7 %collective-permute-start.8 = (f32[40,512]{1,0:T(8,128)S(1)}, f32[40,512]{1,0:T(8,128)S(1)}, u32[]{:S(2)}, u32[]{:S(2)}) collective-permute-start(f32[40,512]{1,0:T(8,128)S(1)} %get-tuple-element.234), channel_id=1, source_target_pairs={{1,0},{2,1},{3,2},{4,3},{5,4},{6,5},{7,6},{9,8},{10,9},{11,10},{12... | collective-permute-start | bytes 245768 | tf_op jit(solution)/shard_map/ppermute | solution.py:496
  6.2 6.1 %collective-permute-start.9 = (f32[40,512]{1,0:T(8,128)S(1)}, f32[40,512]{1,0:T(8,128)S(1)}, u32[]{:S(2)}, u32[]{:S(2)}) collective-permute-start(f32[40,512]{1,0:T(8,128)S(1)} %get-tuple-element.235), channel_id=1, source_target_pairs={{0,1},{1,2},{2,3},{3,4},{4,5},{5,6},{6,7},{8,9},{9,10},{10,11},{11... | collective-permute-start | bytes 245768 | tf_op jit(solution)/shard_map/ppermute | solution.py:497
  12.5 21.4 %collective-permute-start.10 = (f32[40,640]{1,0:T(8,128)S(1)}, f32[40,640]{1,0:T(8,128)S(1)}, u32[]{:S(2)}, u32[]{:S(2)}) collective-permute-start(f32[40,640]{1,0:T(8,128)S(1)} %get-tuple-element.250), channel_id=1, source_target_pairs={{0,8},{8,16},{16,24},{1,9},{9,17},{17,25},{2,10},{10,18},{18,26},{... | collective-permute-start | bytes 307208 | tf_op jit(solution)/shard_map/ppermute | solution.py:497
  19.0 14.9 %collective-permute-start.11 = (f32[40,640]{1,0:T(8,128)S(1)}, f32[40,640]{1,0:T(8,128)S(1)}, u32[]{:S(2)}, u32[]{:S(2)}) collective-permute-start(f32[40,640]{1,0:T(8,128)S(1)} %get-tuple-element.251), channel_id=1, source_target_pairs={{8,0},{16,8},{24,16},{9,1},{17,9},{25,17},{10,2},{18,10},{26,18},{... | collective-permute-start | bytes 307208 | tf_op jit(solution)/shard_map/ppermute | solution.py:496

commit v4 on v3

--- a/solution.py
+++ b/solution.py
@@ -14,6 +14,7 @@
 AMPLIFICATION = 24.0
 VMEM = pl.BlockSpec(memory_space=pltpu.VMEM)
 ANY = pl.BlockSpec(memory_space=pl.ANY)
+HBM = pl.BlockSpec(memory_space=pltpu.HBM)
 
 
 def with_halo(array, sides, width):
@@ -96,7 +97,7 @@
     return pltpu.roll(x, by % LANES, 1) if by % LANES else x
 
 
-def col_pack(edges, labels, prior, weight, to_left, to_right, ints, floats, sem):
+def col_pack(edges, labels, prior, weight, first, second, ints, floats, sem):
     arrays = (edges, labels, prior, weight)
     rows, cols = edges.shape[1], edges.shape[2]
     lane = lane_ids(LANES)
@@ -115,14 +116,21 @@
                 copy(side, a, chunk).start()
     for chunk in range(chunks):
         at = slice(chunk * LANES, (chunk + 1) * LANES)
-        for side, out, base in ((0, to_left, 0), (1, to_right, LANES - WIDTH)):
+        lines = []
+        for side, base in ((0, 0), (1, LANES - WIDTH)):
             packed = None
             for a in range(4):
                 copy(side, a, chunk).wait()
                 x = (ints if a < 2 else floats)[side, a % 2, at, :].astype(jnp.float32)
                 x = turn(x, a * WIDTH - base)
                 packed = x if packed is None else jnp.where(lane < a * WIDTH, packed, x)
-            out[:, at] = jnp.swapaxes(packed, 0, 1)[:LINES]
+            lines.append(jnp.swapaxes(packed, 0, 1)[:LINES])
+        first[:, at], second[:, at] = ordered("col", *lines)
+
+
+def ordered(axis, before, after):
+    even = lax.axis_index(axis) % 2 == 0
+    return jnp.where(even, after, before), jnp.where(even, before, after)
 
 
 def load(edges, labels, prior, weight, code_t, lab_t, prior_t, weight_t, sem):
@@ -150,10 +158,11 @@
         copy.wait()
 
 
-def side_tiles(from_right, from_left, at):
+def side_tiles(first, second, at):
     pad = jnp.zeros((LANES - LINES, LANES), jnp.float32)
-    r = jnp.swapaxes(jnp.concatenate([from_right[:, at : at + LANES], pad], 0), 0, 1)
-    l = jnp.swapaxes(jnp.concatenate([from_left[:, at : at + LANES], pad], 0), 0, 1)
+    r, l = ordered("col", second[:, at : at + LANES], first[:, at : at + LANES])
+    r = jnp.swapaxes(jnp.concatenate([r, pad], 0), 0, 1)
+    l = jnp.swapaxes(jnp.concatenate([l, pad], 0), 0, 1)
     lane = lane_ids(LANES)
     tiles = []
     for a in range(4):
@@ -164,18 +173,21 @@
     return tiles
 
 
-def row_pack(code_t, lab_t, prior_t, weight_t, from_right, from_left, to_upper, to_lower):
+def row_pack(code_t, lab_t, prior_t, weight_t, col_first, col_second, first, second):
     tiles, rows = code_t.shape[0], code_t.shape[1]
     refs = (code_t, lab_t, prior_t, weight_t)
-    for out, at in ((to_upper, 0), (to_lower, rows - LANES)):
-        side = side_tiles(from_right, from_left, at)
-        for a, line, n in TOP_OF:
-            first = 0 if at == 0 else rows - n
-            skip = HALO if a == 1 else 0
-            for j in range(tiles):
-                x = refs[a][j, skip + first : skip + first + n, :].astype(jnp.float32)
-                out[line : line + n, j * LANES : (j + 1) * LANES] = x
-            out[line : line + n, tiles * LANES :] = side[a][first - at : first - at + n]
+    top = side_tiles(col_first, col_second, 0)
+    bottom = side_tiles(col_first, col_second, rows - LANES)
+    for a, line, n in TOP_OF:
+        skip = HALO if a == 1 else 0
+        here = slice(line, line + n)
+        for j in range(tiles):
+            lanes = slice(j * LANES, (j + 1) * LANES)
+            up = refs[a][j, skip : skip + n, :].astype(jnp.float32)
+            low = refs[a][j, skip + rows - n : skip + rows, :].astype(jnp.float32)
+            first[here, lanes], second[here, lanes] = ordered("row", up, low)
+        lanes = slice(tiles * LANES, (tiles + 1) * LANES)
+        first[here, lanes], second[here, lanes] = ordered("row", top[a][:n], bottom[a][LANES - n :])
 
 
 def shifted(tiles, lane, by):
@@ -231,7 +243,7 @@
     return t[0]
 
 
-def interior(code_t, lab_t, prior_t, weight_t, from_right, from_left, *refs):
+def interior(code_t, lab_t, prior_t, weight_t, col_first, col_second, *refs):
     n = ITERS + 1
     field, (er_t, ed_t, eu_t, diag_t, side_lab, sums) = refs[:n], refs[n : n + 6]
     side_code, side_prior, side_weight = refs[n + 6 :]
@@ -239,7 +251,7 @@
     tiles = inner + 1
     lane = lane_ids(8)
     for at in range(0, rows, LANES):
-        side = side_tiles(from_right, from_left, at)
+        side = side_tiles(col_first, col_second, at)
         side_code[at : at + LANES, :] = side[0].astype(jnp.int32)
         side_lab[HALO + at : HALO + at + LANES, :] = side[1].astype(jnp.int32)
         side_prior[at : at + LANES, :] = side[2]
@@ -311,7 +323,7 @@
 def band(*refs):
     n = ITERS
     field, (er_t, ed_t, eu_t, diag_t, lab_t, side_lab) = refs[:n], refs[n : n + 6]
-    sums, from_upper, from_lower = refs[n + 6 : n + 9]
+    sums, row_first, row_second = refs[n + 6 : n + 9]
     out, edge, labs, grid = refs[n + 9 :]
     inner, rows = lab_t.shape[0], er_t.shape[1]
     tiles = inner + 1
@@ -328,9 +340,13 @@
         return [ref[j, first : first + 8, :] for j in range(tiles)]
 
     terms = []
-    for end, (message, first) in enumerate(((from_upper, 0), (from_lower, rows - 8))):
-        def line(at, count=8, message=message):
-            return [message[at : at + count, j * LANES : (j + 1) * LANES] for j in range(tiles)]
+    for end, first in enumerate((0, rows - 8)):
+        def line(at, count=8, end=end):
+            both = [
+                ordered("row", row_second[at : at + count, lanes], row_first[at : at + count, lanes])
+                for lanes in (slice(j * LANES, (j + 1) * LANES) for j in range(tiles))
+            ]
+            return [pair[1 - end] for pair in both]
 
         beyond, mine = (0, 16) if end == 0 else (8, 0)
         for j, (x, y) in enumerate(zip(line(24, 16), lab_own(first))):
@@ -490,12 +506,12 @@
         copy.wait()
 
 
-def both_ways(axis, backward, forward):
-    up = [(i, i + 1) for i in range(lax.axis_size(axis) - 1)]
-    return (
-        lax.ppermute(backward, axis, [(b, a) for a, b in up]),
-        lax.ppermute(forward, axis, up),
-    )
+def swaps(axis, first, second, around):
+    count = lax.axis_size(axis)
+    pairs = [(i, i + 1) for i in range(0, count - 1, 2)]
+    others = [(i, i + 1) for i in range(1, count - 1, 2)] + ([(count - 1, 0)] if around else [])
+    both = lambda p: [(a, b) for a, b in p] + [(b, a) for a, b in p]
+    return lax.ppermute(first, axis, both(pairs)), lax.ppermute(second, axis, both(others))
 
 
 def call(body, in_specs, outs, scratch, mib, flops, operands, out_specs=None):
@@ -519,8 +535,8 @@
     tiles = inner + 1
     dma = pltpu.SemaphoreType.DMA
 
-    to_left, to_right = call(
-        col_pack, [ANY] * 4, [shape((LINES, rows), f32)] * 2,
+    col_messages = call(
+        col_pack, [HBM] * 4, [shape((LINES, rows), f32)] * 2,
         [
             pltpu.VMEM((2, 2, rows, LANES), i32),
             pltpu.VMEM((2, 2, rows, LANES), f32),
@@ -528,10 +544,10 @@
         ],
         6, 1 << 20, arrays,
     )
-    from_right, from_left = both_ways("col", to_left, to_right)
+    col_first, col_second = swaps("col", *col_messages, True)
 
     block = call(
-        load, [ANY] * 4,
+        load, [HBM] * 4,
         [
             shape((inner, rows, LANES), i32),
             shape((inner, rows + 2 * HALO, LANES), i32),
@@ -540,11 +556,11 @@
         ],
         [dma((4, inner))], 6, 1 << 24, arrays,
     )
-    to_upper, to_lower = call(
+    row_messages = call(
         row_pack, [VMEM] * 6, [shape((LINES, tiles * LANES), f32)] * 2, [],
-        4, 1 << 20, (*block, from_right, from_left),
-    )
-    from_lower, from_upper = both_ways("row", to_upper, to_lower)
+        4, 1 << 20, (*block, col_first, col_second),
+    )
+    row_first, row_second = swaps("row", *row_messages, False)
 
     n = ITERS + 1
     out = call(
@@ -552,7 +568,7 @@
         [shape((tiles, rows, LANES), f32)] * (n + 4)
         + [shape((rows + 2 * HALO, LANES), i32), shape((2 * ITERS + 1, 8, LANES), f32)],
         [pltpu.VMEM((rows, LANES), i32), pltpu.VMEM((rows, LANES), f32), pltpu.VMEM((rows, LANES), f32)],
-        16, 1 << 26, (*block, from_right, from_left),
+        16, 1 << 26, (*block, col_first, col_second),
     )
     field, terms, side_lab, sums = out[:n], out[n : n + 4], out[n + 4], out[n + 5]
     group = lax.axis_size(("row", "col"))
@@ -560,7 +576,7 @@
         band, [VMEM] * (ITERS + 9),
         [shape((group, 1, LANES), f32), shape((n, 2, inner, 2 * HALO, LANES), f32)],
         [pltpu.VMEM((2, tiles, 24, LANES), i32), pltpu.VMEM((2, n, tiles, 40, LANES), f32)],
-        6, 1 << 20, (*field[:ITERS], *terms, block[1], side_lab, sums, from_upper, from_lower),
+        6, 1 << 20, (*field[:ITERS], *terms, block[1], side_lab, sums, row_first, row_second),
     )
     every = lax.all_to_all(sums, ("row", "col"), 0, 0, tiled=True)
 

time: 56.7 us -> 49.2 us (0.87)
  blocking collectives: 17.3 us -> 11.4 us
  starting transfers between devices: 14.4 us -> 11.8 us
  waiting for transfers between devices: 0.68 us -> 1.81 us
    all_to_all x1, blocking collectives: 17.3 us -> 11.4 us  [per_device(): every = lax.all_to_all(sums, ('row', 'col'), 0, 0, tiled=True)]
    ppermute x4, starting transfers between devices: 14.4 us -> 11.8 us  [the longest x2 7.38 us: swaps(): lax.ppermute(second, axis, both(others))]
    ppermute x4, waiting for transfers between devices: 0.68 us -> 1.81 us  [the longest x2 1.8 us: swaps(): lax.ppermute(second, axis, both(others))]
  transfers between devices with their start and end apart: 4 -> 4, of which waited for: 1 -> 1; matrix products, arithmetic and copies ran while one was open for 0% -> 0% of each run, Pallas kernels for 24% -> 28%
where the time goes in v4:
time: 49.2 us; the launch traced here: 49.1 us
  Pallas kernels  21.8 us (44%)
  starting transfers between devices  11.8 us (24%)
  blocking collectives  11.4 us (23%)
  waiting for transfers between devices  1.81 us (4%)
  between operations  0.91 us (2%)
  loops' own time  0.82 us (2%)
  local copies, waits for them, and re-layouts  0.56 us (1%)
    pallas_call x6, Pallas kernels, call(): pl.pallas_call(body, in_specs=in_specs, out_specs=out_specs or [VMEM] * l...  21.8 us
    all_to_all x1, blocking collectives, per_device(): every = lax.all_to_all(sums, ('row', 'col'), 0, 0, tiled=True)  11.4 us
    ppermute x2, starting transfers between devices, swaps(): lax.ppermute(second, axis, both(others))  7.38 us
    ppermute x2, starting transfers between devices, swaps(): lax.ppermute(first, axis, both(pairs))  4.38 us
    ppermute x2, waiting for transfers between devices, swaps(): lax.ppermute(second, axis, both(others))  1.8 us
  transfers between devices with their start and end apart: 4, of which 1 were waited for; matrix products, arithmetic and copies ran while one was open for 0% of the time, Pallas kernels for 28%

profile of v4, /device:TPU:1, one launch (start us, length us, event | category | flops | bytes accessed | tf_op | source)
XLA Modules:
  0.0 49.1 jit_solution(10783430885432858779)
XLA Ops:
  0.6 0.0 copy-start.6
  0.6 0.0 copy-start.5
  0.7 0.0 copy-start.4
  0.7 0.0 copy-start.2
  0.7 4.2 %shard_map.60 = (f32[40,512]{1,0:T(8,128)S(1)}, f32[40,512]{1,0:T(8,128)S(1)}) custom-call(s32[1,512,512]{2,1,0:T(8,128)} %edges.3, s32[1,512,512]{2,1,0:T(8,128)} %labels.3, f32[1,512,512]{2,1,0:T(8,128)} %prior.3, f32[1,512,512]{2,1,0:T(8,128)} %weight.3), custom_call_target="tpu_custom_call" | custom-call | flops 1048576 | bytes 1048576 | tf_op jit(solution)/shard_map/pallas_call | solution.py:518
  4.9 2.2 %collective-permute-start.8 = (f32[40,512]{1,0:T(8,128)S(1)}, f32[40,512]{1,0:T(8,128)S(1)}, u32[]{:S(2)}, u32[]{:S(2)}) collective-permute-start(f32[40,512]{1,0:T(8,128)S(1)} %get-tuple-element.234), channel_id=1, source_target_pairs={{0,1},{2,3},{4,5},{6,7},{1,0},{3,2},{5,4},{7,6},{8,9},{10,11},{12,... | collective-permute-start | bytes 245768 | tf_op jit(solution)/shard_map/ppermute | solution.py:514
  7.1 2.8 %collective-permute-start.9 = (f32[40,512]{1,0:T(8,128)S(1)}, f32[40,512]{1,0:T(8,128)S(1)}, u32[]{:S(2)}, u32[]{:S(2)}) collective-permute-start(f32[40,512]{1,0:T(8,128)S(1)} %get-tuple-element.235), channel_id=1, source_target_pairs={{1,2},{3,4},{5,6},{7,0},{2,1},{4,3},{6,5},{0,7},{9,10},{11,12},{13... | collective-permute-start | bytes 245768 | tf_op jit(solution)/shard_map/ppermute | solution.py:514
  9.9 0.0 copy-done.6
  9.9 0.0 copy-done.5
  9.9 0.0 copy-done.4
  9.9 0.0 copy-done.2
  9.9 0.7 %shard_map.59 = (s32[4,512,128]{2,1,0:T(8,128)S(1)}, s32[4,528,128]{2,1,0:T(8,128)S(1)}, f32[4,512,128]{2,1,0:T(8,128)S(1)}, f32[4,512,128]{2,1,0:T(8,128)S(1)}) custom-call(s32[1,512,512]{2,1,0:T(8,128)S(1)} %copy-done.2, s32[1,512,512]{2,1,0:T(8,128)S(1)} %copy-done.4, f32[1,512,512]{2,1,0:T(8,128)S(1)} %copy-done.5, f32[1,512,512]{2,1,0:T(8,128)S(1)} %copy-done.6), custom_call_target="tpu_custom_call" | custom-call | flops 16777216 | bytes 1048576 | tf_op jit(solution)/shard_map/pallas_call | solution.py:518
  10.7 0.0 collective-permute-done.8.col_first
  10.7 1.8 %collective-permute-done.9.col_second = f32[40,512]{1,0:T(8,128)S(1)} collective-permute-done((f32[40,512]{1,0:T(8,128)S(1)}, f32[40,512]{1,0:T(8,128)S(1)}, u32[]{:S(2)}, u32[]{:S(2)}) %collective-permute-start.9) | collective-permute-done | bytes 81952 | tf_op jit(solution)/shard_map/ppermute | solution.py:514
  12.5 0.2 shard_map.62
  12.7 2.2 %collective-permute-start.10 = (f32[40,640]{1,0:T(8,128)S(1)}, f32[40,640]{1,0:T(8,128)S(1)}, u32[]{:S(2)}, u32[]{:S(2)}) collective-permute-start(f32[40,640]{1,0:T(8,128)S(1)} %get-tuple-element.250), channel_id=1, source_target_pairs={{0,8},{16,24},{8,0},{24,16},{1,9},{17,25},{9,1},{25,17},{2,10},{18... | collective-permute-start | bytes 307208 | tf_op jit(solution)/shard_map/ppermute | solution.py:514
  14.9 4.6 %collective-permute-start.11 = (f32[40,640]{1,0:T(8,128)S(1)}, f32[40,640]{1,0:T(8,128)S(1)}, u32[]{:S(2)}, u32[]{:S(2)}) collective-permute-start(f32[40,640]{1,0:T(8,128)S(1)} %get-tuple-element.251), channel_id=1, source_target_pairs={{8,16},{16,8},{9,17},{17,9},{10,18},{18,10},{11,19},{19,11},{12,20... | collective-permute-start | bytes 307208 | tf_op jit(solution)/shard_map/ppermute | solution.py:514
  19.4 13.0 %shard_map.61 = (f32[5,512,128]{2,1,0:T(8,128)S(1)}, f32[5,512,128]{2,1,0:T(8,128)S(1)}, f32[5,512,128]{2,1,0:T(8,128)S(1)}, f32[5,512,128]{2,1,0:T(8,128)S(1)},...) custom-call(s32[4,512,128]{2,1,0:T(8,128)S(1)} %get-tuple-element.23, ...), custom_call_target="tpu_custom_call" | custom-call | flops 67108864 | bytes 1048576 | tf_op jit(solution)/shard_map/pallas_call | solution.py:518
  32.4 0.0 collective-permute-done.10.refs_15_
  32.4 0.0 collective-permute-done.11.refs_16_
  32.5 1.0 %shard_map.63 = (f32[32,1,128]{2,1,0:T(1,128)S(1)}, f32[9,2,4,16,128]{4,3,2,1,0:T(8,128)S(1)}) custom-call(f32[5,512,128]{2,1,0:T(8,128)S(1)} %get-tuple-element.236.refs_0_, f32[5,512,128]{2,1,0:T(8,128)S(1)} %get-tuple-element.237.refs_1_, f32[5,512,128]{2,1,0:T(8,128)S(1)} %get-tuple-element.238.refs_2_, f32[5,512,128]{2,1,0:T(8,128)S(1)} %get-tuple-element.239.refs_3_, ...), custom_call_target="tpu_custom_call" | custom-call | flops 1048576 | bytes 1048576 | tf_op jit(solution)/shard_map/pallas_call | solution.py:518
  33.4 11.4 %all_to_all.31.every = f32[32,1,128]{2,1,0:T(1,128)S(1)} all-to-all(f32[32,1,128]{2,1,0:T(1,128)S(1)} %get-tuple-element.252), channel_id=1, replica_groups=mesh['img'=4,'row'=4,'col'=8] {'row','col'}, dimensions={0} | all-to-all | bytes 32768 | tf_op jit(solution)/shard_map/all_to_all | solution.py:581
  44.8 2.7 %shard_map.64 = (f32[1,512,512]{2,1,0:T(8,128)}, f32[1,512,512]{2,1,0:T(8,128)}, s32[8,128]{1,0:T(8,128)S(1)}) custom-call(f32[32,1,128]{2,1,0:T(1,128)S(1)} %all_to_all.31.every, s32[4,528,128]{2,1,0:T(8,128)S(1)} %get-tuple-element.231.lab_t.refs_12_, f32[9,2,4,16,128]{4,3,2,1,0:T(8,128)S(1)} %get-tuple-element.253.edge, ...), custom_call_target="tpu_custom_call" | custom-call | flops 1048576 | bytes 1048576 | tf_op jit(solution)/shard_map/pallas_call | solution.py:518
  47.6 0.5 %slice.91 = s32[1,1]{1,0:T(1,128)} slice(s32[8,128]{1,0:T(8,128)S(1)} %get-tuple-element.255), slice={[0:1], [0:1]} | slice | bytes 8 | tf_op jit(solution)/shard_map/slice | solution.py:594
  48.1 0.8 %while.30 = (s32[]{:T(128)}, f32[1,512,512]{2,1,0:T(8,128)}, f32[1,512,512]{2,1,0:T(8,128)}, s32[1,512,512]{2,1,0:T(8,128)}, f32[1,512,512]{2,1,0:T(8,128)}, /*i...) while((s32[]{:T(128)}, f32[1,512,512]{2,1,0:T(8,128)}, f32[1,512,512]{2,1,0:T(8,128)}, ...), condition=%region_9.10_spmd, body=%region_0.9_spmd | while | flops 58720352 | bytes 45852768 | solution.py:593
Async XLA Ops:
  0.6 9.3 %copy-start.6 = (f32[1,512,512]{2,1,0:T(8,128)S(1)}, f32[1,512,512]{2,1,0:T(8,128)}, u32[]{:S(2)}) copy-start(f32[1,512,512]{2,1,0:T(8,128)} %weight.3) | copy-start | bytes 3145732
  0.6 9.3 %copy-start.5 = (f32[1,512,512]{2,1,0:T(8,128)S(1)}, f32[1,512,512]{2,1,0:T(8,128)}, u32[]{:S(2)}) copy-start(f32[1,512,512]{2,1,0:T(8,128)} %prior.3) | copy-start | bytes 3145732
  0.7 9.2 %copy-start.4 = (s32[1,512,512]{2,1,0:T(8,128)S(1)}, s32[1,512,512]{2,1,0:T(8,128)}, u32[]{:S(2)}) copy-start(s32[1,512,512]{2,1,0:T(8,128)} %labels.3) | copy-start | bytes 3145732
  0.7 9.2 %copy-start.2 = (s32[1,512,512]{2,1,0:T(8,128)S(1)}, s32[1,512,512]{2,1,0:T(8,128)}, u32[]{:S(2)}) copy-start(s32[1,512,512]{2,1,0:T(8,128)} %edges.3) | copy-start | bytes 3145732
  4.9 5.8 %collective-permute-start.8 = (f32[40,512]{1,0:T(8,128)S(1)}, f32[40,512]{1,0:T(8,128)S(1)}, u32[]{:S(2)}, u32[]{:S(2)}) collective-permute-start(f32[40,512]{1,0:T(8,128)S(1)} %get-tuple-element.234), channel_id=1, source_target_pairs={{0,1},{2,3},{4,5},{6,7},{1,0},{3,2},{5,4},{7,6},{8,9},{10,11},{12,... | collective-permute-start | bytes 245768 | tf_op jit(solution)/shard_map/ppermute | solution.py:514
  7.1 5.4 %collective-permute-start.9 = (f32[40,512]{1,0:T(8,128)S(1)}, f32[40,512]{1,0:T(8,128)S(1)}, u32[]{:S(2)}, u32[]{:S(2)}) collective-permute-start(f32[40,512]{1,0:T(8,128)S(1)} %get-tuple-element.235), channel_id=1, source_target_pairs={{1,2},{3,4},{5,6},{7,0},{2,1},{4,3},{6,5},{0,7},{9,10},{11,12},{13... | collective-permute-start | bytes 245768 | tf_op jit(solution)/shard_map/ppermute | solution.py:514
  12.7 19.7 %collective-permute-start.10 = (f32[40,640]{1,0:T(8,128)S(1)}, f32[40,640]{1,0:T(8,128)S(1)}, u32[]{:S(2)}, u32[]{:S(2)}) collective-permute-start(f32[40,640]{1,0:T(8,128)S(1)} %get-tuple-element.250), channel_id=1, source_target_pairs={{0,8},{16,24},{8,0},{24,16},{1,9},{17,25},{9,1},{25,17},{2,10},{18... | collective-permute-start | bytes 307208 | tf_op jit(solution)/shard_map/ppermute | solution.py:514
  14.9 17.6 %collective-permute-start.11 = (f32[40,640]{1,0:T(8,128)S(1)}, f32[40,640]{1,0:T(8,128)S(1)}, u32[]{:S(2)}, u32[]{:S(2)}) collective-permute-start(f32[40,640]{1,0:T(8,128)S(1)} %get-tuple-element.251), channel_id=1, source_target_pairs={{8,16},{16,8},{9,17},{17,9},{10,18},{18,10},{11,19},{19,11},{12,20... | collective-permute-start | bytes 307208 | tf_op jit(solution)/shard_map/ppermute | solution.py:514

commit v5 on v4

--- a/solution.py
+++ b/solution.py
@@ -101,28 +101,23 @@
     arrays = (edges, labels, prior, weight)
     rows, cols = edges.shape[1], edges.shape[2]
     lane = lane_ids(LANES)
-
-    def copy(side, a, chunk):
-        at = pl.ds(chunk * LANES, LANES)
-        dst = (ints if a < 2 else floats).at[side, a % 2, at, :]
-        return pltpu.make_async_copy(
-            arrays[a].at[0, at, pl.ds(side * (cols - LANES), LANES)], dst, sem.at[side, a, chunk]
-        )
-
-    chunks = rows // LANES
-    for chunk in range(chunks):
-        for side in range(2):
-            for a in range(4):
-                copy(side, a, chunk).start()
-    for chunk in range(chunks):
+    held = [(ints if a < 2 else floats).at[:, a % 2] for a in range(4)]
+    copies = []
+    for side in range(2):
+        for a, ref in enumerate(arrays):
+            src = ref.at[0, :, pl.ds(side * (cols - LANES), LANES)]
+            copies.append(pltpu.make_async_copy(src, held[a].at[side], sem.at[side, a]))
+    for copy in copies:
+        copy.start()
+    for copy in copies:
+        copy.wait()
+    for chunk in range(rows // LANES):
         at = slice(chunk * LANES, (chunk + 1) * LANES)
         lines = []
         for side, base in ((0, 0), (1, LANES - WIDTH)):
             packed = None
             for a in range(4):
-                copy(side, a, chunk).wait()
-                x = (ints if a < 2 else floats)[side, a % 2, at, :].astype(jnp.float32)
-                x = turn(x, a * WIDTH - base)
+                x = turn(held[a][side, at, :].astype(jnp.float32), a * WIDTH - base)
                 packed = x if packed is None else jnp.where(lane < a * WIDTH, packed, x)
             lines.append(jnp.swapaxes(packed, 0, 1)[:LINES])
         first[:, at], second[:, at] = ordered("col", *lines)
@@ -131,31 +126,6 @@
 def ordered(axis, before, after):
     even = lax.axis_index(axis) % 2 == 0
     return jnp.where(even, after, before), jnp.where(even, before, after)
-
-
-def load(edges, labels, prior, weight, code_t, lab_t, prior_t, weight_t, sem):
-    rows = edges.shape[1]
-    tiles = code_t.shape[0]
-    copies = []
-    for a, (src, dst, at) in enumerate(
-        ((edges, code_t, 0), (labels, lab_t, HALO), (prior, prior_t, 0), (weight, weight_t, 0))
-    ):
-        for j in range(tiles):
-            copies.append(
-                pltpu.make_async_copy(
-                    src.at[0, :, pl.ds(j * LANES, LANES)],
-                    dst.at[j, pl.ds(at, rows), :],
-                    sem.at[a, j],
-                )
-            )
-    for copy in copies:
-        copy.start()
-    seeds = jnp.full((HALO, LANES), 2, jnp.int32)
-    for j in range(tiles):
-        lab_t[j, :HALO, :] = seeds
-        lab_t[j, HALO + rows :, :] = seeds
-    for copy in copies:
-        copy.wait()
 
 
 def side_tiles(first, second, at):
@@ -173,18 +143,21 @@
     return tiles
 
 
-def row_pack(code_t, lab_t, prior_t, weight_t, col_first, col_second, first, second):
-    tiles, rows = code_t.shape[0], code_t.shape[1]
-    refs = (code_t, lab_t, prior_t, weight_t)
+def row_pack(edges, lab_t, prior, weight, col_first, col_second, first, second):
+    rows, cols = edges.shape[1], edges.shape[2]
+    tiles = cols // LANES
+    refs = (edges, None, prior, weight)
     top = side_tiles(col_first, col_second, 0)
     bottom = side_tiles(col_first, col_second, rows - LANES)
     for a, line, n in TOP_OF:
-        skip = HALO if a == 1 else 0
         here = slice(line, line + n)
         for j in range(tiles):
             lanes = slice(j * LANES, (j + 1) * LANES)
-            up = refs[a][j, skip : skip + n, :].astype(jnp.float32)
-            low = refs[a][j, skip + rows - n : skip + rows, :].astype(jnp.float32)
+            if a == 1:
+                up, low = lab_t[j, HALO : HALO + n, :], lab_t[j, HALO + rows - n : HALO + rows, :]
+            else:
+                up, low = refs[a][0, :n, lanes], refs[a][0, rows - n :, lanes]
+            up, low = up.astype(jnp.float32), low.astype(jnp.float32)
             first[here, lanes], second[here, lanes] = ordered("row", up, low)
         lanes = slice(tiles * LANES, (tiles + 1) * LANES)
         first[here, lanes], second[here, lanes] = ordered("row", top[a][:n], bottom[a][LANES - n :])
@@ -201,28 +174,66 @@
 SCALE = 2.0 / RADIUS
 
 
-def decode(lane, code, lab, lab_d, lab_u, prior, weight):
+def decode(code, lab, lab_r, lab_l, lab_d, lab_u, prior, weight):
+    r = (code & 1).astype(jnp.float32)
+    l = ((code >> 1) & 1).astype(jnp.float32)
+    d = ((code >> 2) & 1).astype(jnp.float32)
+    u = ((code >> 3) & 1).astype(jnp.float32)
+    free = lab == 0
+    one = jnp.where(free, SCALE, 0.0)
+    near = (
+        jnp.where(lab_r == 1, r, 0.0)
+        + jnp.where(lab_l == 1, l, 0.0)
+        + jnp.where(lab_d == 1, d, 0.0)
+        + jnp.where(lab_u == 1, u, 0.0)
+    )
+    return (
+        jnp.where(lab_r == 0, one, 0.0) * r,
+        one * d,
+        one * u,
+        SCALE * ((r + l + d + u) + weight - CENTRE),
+        jnp.where(free, weight * prior + near, 0.0),
+    )
+
+
+def decode_row(lane, code, lab, lab_d, lab_u, prior, weight):
     lab_r, lab_l = shifted(lab, lane, -1), shifted(lab, lane, 1)
-    er, ed, eu, diag, rhs = [], [], [], [], []
-    for j in range(len(code)):
-        r = (code[j] & 1).astype(jnp.float32)
-        l = ((code[j] >> 1) & 1).astype(jnp.float32)
-        d = ((code[j] >> 2) & 1).astype(jnp.float32)
-        u = ((code[j] >> 3) & 1).astype(jnp.float32)
-        free = lab[j] == 0
-        one = jnp.where(free, SCALE, 0.0)
-        er.append(jnp.where(lab_r[j] == 0, one, 0.0) * r)
-        ed.append(one * d)
-        eu.append(one * u)
-        diag.append(SCALE * ((r + l + d + u) + weight[j] - CENTRE))
-        near = (
-            jnp.where(lab_r[j] == 1, r, 0.0)
-            + jnp.where(lab_l[j] == 1, l, 0.0)
-            + jnp.where(lab_d[j] == 1, d, 0.0)
-            + jnp.where(lab_u[j] == 1, u, 0.0)
+    return list(zip(*map(decode, code, lab, lab_r, lab_l, lab_d, lab_u, prior, weight)))
+
+
+def prepare(edges, labels, prior, weight, lab_t, *terms):
+    rows, cols = edges.shape[1], edges.shape[2]
+    tiles = cols // LANES
+    lane = lane_ids(8)
+    seeds = jnp.full((8, LANES), 2, jnp.int32)
+    for j in range(tiles):
+        lab_t[j, :HALO, :] = seeds
+        lab_t[j, HALO + rows :, :] = seeds
+
+    def lay(i, _):
+        s = pl.multiple_of(8 * i, 8)
+        for j in range(tiles):
+            lab_t[j, pl.ds(s + HALO, 8), :] = labels[0, pl.ds(s, 8), j * LANES : (j + 1) * LANES]
+        return 0
+
+    lax.fori_loop(0, rows // 8, lay, 0, unroll=16)
+
+    def body(i, _):
+        s = pl.multiple_of(8 * i, 8)
+        read = lambda ref: [ref[0, pl.ds(s, 8), j * LANES : (j + 1) * LANES] for j in range(tiles)]
+        near = lambda at: [lab_t[j, pl.ds(at, 8), :] for j in range(tiles)]
+        lab = near(pl.multiple_of(s + HALO, 8))
+        lab_r, lab_l = (shifted(lab + [seeds], lane, by)[:tiles] for by in (-1, 1))
+        done = map(
+            decode, read(edges), lab, lab_r, lab_l, near(s + HALO + 1), near(s + HALO - 1),
+            read(prior), read(weight),
         )
-        rhs.append(jnp.where(free, weight[j] * prior[j] + near, 0.0))
-    return er, ed, eu, diag, rhs
+        for j, values in enumerate(done):
+            for ref, value in zip(terms, values):
+                ref[j, pl.ds(s, 8), :] = value
+        return 0
+
+    lax.fori_loop(0, rows // 8, body, 0, unroll=8)
 
 
 def recurrence(lane, k, v, v_d, v_u, before, er, ed, eu, diag):
@@ -243,11 +254,12 @@
     return t[0]
 
 
-def interior(code_t, lab_t, prior_t, weight_t, col_first, col_second, *refs):
-    n = ITERS + 1
-    field, (er_t, ed_t, eu_t, diag_t, side_lab, sums) = refs[:n], refs[n : n + 6]
-    side_code, side_prior, side_weight = refs[n + 6 :]
-    inner, rows = code_t.shape[0], code_t.shape[1]
+def interior(edges, lab_t, col_first, col_second, *refs):
+    refs = refs[5:]
+    (er_t, ed_t, eu_t, diag_t), field, side_lab, sums = refs[:4], refs[4:13], refs[13], refs[14]
+    side_code, side_prior, side_weight = refs[15:]
+    rows = edges.shape[1]
+    inner = lab_t.shape[0]
     tiles = inner + 1
     lane = lane_ids(8)
     for at in range(0, rows, LANES):
@@ -264,28 +276,30 @@
         for j in range(tiles):
             field[k][j, :8, :] = zero
             field[k][j, rows - 8 :, :] = zero
-
-    def read(ref, side, s):
-        return [ref[j, pl.ds(s, 8), :] for j in range(inner)] + [side[pl.ds(s, 8), :]]
-
-    def prepare(i, _):
+    end = inner - 1
+
+    def sides(i, _):
         s = pl.multiple_of(8 * i, 8)
-        here = pl.ds(s, 8)
-        done = decode(
-            lane,
-            read(code_t, side_code, s),
-            read(lab_t, side_lab, pl.multiple_of(s + HALO, 8)),
-            read(lab_t, side_lab, s + HALO + 1),
-            read(lab_t, side_lab, s + HALO - 1),
-            read(prior_t, side_prior, s),
-            read(weight_t, side_weight, s),
+        here, there = pl.ds(s, 8), pl.ds(pl.multiple_of(s + HALO, 8), 8)
+        lab, lab_0, lab_end = side_lab[there, :], lab_t[0, there, :], lab_t[end, there, :]
+        lab_r, lab_l = turn(lab, -1), turn(lab, 1)
+        values = decode(
+            side_code[here, :], lab,
+            jnp.where(lane == LANES - 1, turn(lab_0, -1), lab_r),
+            jnp.where(lane == 0, turn(lab_end, 1), lab_l),
+            side_lab[pl.ds(s + HALO + 1, 8), :], side_lab[pl.ds(s + HALO - 1, 8), :],
+            side_prior[here, :], side_weight[here, :],
         )
-        for ref, values in zip((er_t, ed_t, eu_t, diag_t, field[0]), done):
-            for j in range(tiles):
-                ref[j, here, :] = values[j]
+        for ref, value in zip((er_t, ed_t, eu_t, diag_t, field[0]), values):
+            ref[inner, here, :] = value
+        left = (lane == 0) & (lab_0 == 0) & ((edges[0, here, :LANES] & 2) != 0)
+        field[0][0, here, :] += jnp.where(left & (lab_l == 1), 1.0, 0.0)
+        right = (lane == LANES - 1) & (lab_end == 0) & ((edges[0, here, end * LANES :] & 1) != 0)
+        field[0][end, here, :] += jnp.where(right & (lab_r == 1), 1.0, 0.0)
+        er_t[end, here, :] += jnp.where(right & (lab_r == 0), SCALE, 0.0)
         return 0
 
-    lax.fori_loop(0, rows // 8, prepare, 0, unroll=8)
+    lax.fori_loop(0, rows // 8, sides, 0, unroll=16)
 
     def at_rows(ref, s):
         return [ref[j, pl.ds(s, 8), :] for j in range(tiles)]
@@ -314,7 +328,7 @@
             advance(k, 8)
             advance(k, rows - 16)
         acc = (zero,) * (3 if last else 2)
-        acc = lax.fori_loop(0, (rows - 4 * HALO) // 8, body, acc, unroll=15)
+        acc = lax.fori_loop(0, (rows - 4 * HALO) // 8, body, acc, unroll=60)
         for value in acc:
             sums[count] = value
             count += 1
@@ -353,7 +367,7 @@
             labs[end, j, beyond : beyond + 16, :] = x.astype(jnp.int32)
             labs[end, j, mine : mine + 8, :] = y
         near = lambda at: [labs[end, j, at : at + 8, :] for j in range(tiles)]
-        *halo, rhs = decode(
+        *halo, rhs = decode_row(
             lane, [x.astype(jnp.int32) for x in line(0)], near(8), near(9), near(7), line(8), line(16)
         )
         if end == 0:
@@ -463,7 +477,7 @@
     g = jnp.sum(every[:, 0, :], axis=0, keepdims=True)
     dots = [jnp.broadcast_to(g[:, q : q + 1], (8, LANES)) for q in range(2 * ITERS + 1)]
     x, r, good = coefficients(dots)
-    flag[...] = good.astype(jnp.int32)
+    flag[0, 0] = jnp.min(good.astype(jnp.int32))
 
     def put(s, source):
         for j in range(inner):
@@ -484,7 +498,7 @@
         return 0
 
     copies = []
-    chunk = 64
+    chunk = 128
     for c in range(rows // chunk):
         first, last = c * chunk // 8, (c + 1) * chunk // 8
         if c == 0:
@@ -493,7 +507,7 @@
             first += 2
         if (c + 1) * chunk == rows:
             last -= 2
-        lax.fori_loop(first, last, body, 0, unroll=2)
+        lax.fori_loop(first, last, body, 0, unroll=(last - first) // 2)
         if (c + 1) * chunk == rows:
             for q in range(2):
                 put(rows - 16 + 8 * q, lambda k, j: edge[k, 1, j, 8 * q : 8 * q + 8, :])
@@ -514,13 +528,14 @@
     return lax.ppermute(first, axis, both(pairs)), lax.ppermute(second, axis, both(others))
 
 
-def call(body, in_specs, outs, scratch, mib, flops, operands, out_specs=None):
+def call(body, in_specs, outs, scratch, mib, flops, operands, out_specs=None, aliases={}):
     return pl.pallas_call(
         body,
         in_specs=in_specs,
         out_specs=out_specs or [VMEM] * len(outs),
         out_shape=outs,
         scratch_shapes=scratch,
+        input_output_aliases=aliases,
         compiler_params=pltpu.CompilerParams(vmem_limit_bytes=mib * 1024 * 1024),
         cost_estimate=pl.CostEstimate(flops=flops, bytes_accessed=1 << 20, transcendentals=0),
     )(*operands)
@@ -540,51 +555,47 @@
         [
             pltpu.VMEM((2, 2, rows, LANES), i32),
             pltpu.VMEM((2, 2, rows, LANES), f32),
-            dma((2, 4, rows // LANES)),
+            dma((2, 4)),
         ],
         6, 1 << 20, arrays,
     )
     col_first, col_second = swaps("col", *col_messages, True)
 
-    block = call(
-        load, [HBM] * 4,
-        [
-            shape((inner, rows, LANES), i32),
-            shape((inner, rows + 2 * HALO, LANES), i32),
-            shape((inner, rows, LANES), f32),
-            shape((inner, rows, LANES), f32),
-        ],
-        [dma((4, inner))], 6, 1 << 24, arrays,
+    n = ITERS + 1
+    whole = shape((tiles, rows, LANES), f32)
+    lab_t, *terms = call(
+        prepare, [VMEM] * 4, [shape((inner, rows + 2 * HALO, LANES), i32)] + [whole] * 5, [],
+        6, 1 << 24, arrays,
     )
     row_messages = call(
         row_pack, [VMEM] * 6, [shape((LINES, tiles * LANES), f32)] * 2, [],
-        4, 1 << 20, (*block, col_first, col_second),
+        4, 1 << 20, (edges, lab_t, prior, data_weight, col_first, col_second),
     )
     row_first, row_second = swaps("row", *row_messages, False)
 
-    n = ITERS + 1
     out = call(
-        interior, [VMEM] * 6,
-        [shape((tiles, rows, LANES), f32)] * (n + 4)
+        interior, [VMEM] * 9,
+        [whole] * (4 + n)
         + [shape((rows + 2 * HALO, LANES), i32), shape((2 * ITERS + 1, 8, LANES), f32)],
         [pltpu.VMEM((rows, LANES), i32), pltpu.VMEM((rows, LANES), f32), pltpu.VMEM((rows, LANES), f32)],
-        16, 1 << 26, (*block, col_first, col_second),
-    )
-    field, terms, side_lab, sums = out[:n], out[n : n + 4], out[n + 4], out[n + 5]
+        16, 1 << 26, (edges, lab_t, col_first, col_second, *terms),
+        aliases={4 + q: q for q in range(5)},
+    )
+    terms, field, side_lab, sums = out[:4], out[4 : 4 + n], out[4 + n], out[5 + n]
     group = lax.axis_size(("row", "col"))
     sums, edge = call(
         band, [VMEM] * (ITERS + 9),
         [shape((group, 1, LANES), f32), shape((n, 2, inner, 2 * HALO, LANES), f32)],
         [pltpu.VMEM((2, tiles, 24, LANES), i32), pltpu.VMEM((2, n, tiles, 40, LANES), f32)],
-        6, 1 << 20, (*field[:ITERS], *terms, block[1], side_lab, sums, row_first, row_second),
+        6, 1 << 20, (*field[:ITERS], *terms, lab_t, side_lab, sums, row_first, row_second),
     )
     every = lax.all_to_all(sums, ("row", "col"), 0, 0, tiled=True)
 
     labeling, residual, flag = call(
         combine, [VMEM] * (n + 3),
-        [shape(edges.shape, f32)] * 2 + [shape((8, LANES), i32)],
-        [pltpu.VMEM((rows, cols), f32)] * 2 + [dma((rows // 64, 2))],
-        4, 1 << 20, (every, block[1], edge, *field), out_specs=[ANY, ANY, VMEM],
+        [shape(edges.shape, f32)] * 2 + [shape((1, 1), i32)],
+        [pltpu.VMEM((rows, cols), f32)] * 2 + [dma((rows // 128, 2))],
+        4, 1 << 20, (every, lab_t, edge, *field), out_specs=[ANY, ANY, pl.BlockSpec(memory_space=pltpu.SMEM)],
     )
 
     def again(carry):

time: 49.2 us -> 45.5 us (0.925)
  waiting for transfers between devices: 1.81 us -> 0.01 us
  Pallas kernels: 21.8 us -> 20.7 us
  local copies, waits for them, and re-layouts: 0.56 us -> 0.02 us
    ppermute x2, waiting for transfers between devices: 1.8 us -> 0.01 us  [swaps(): lax.ppermute(second, axis, both(others))]
    pallas_call x6, Pallas kernels: 21.8 us -> 20.7 us  [call(): pl.pallas_call(body, in_specs=in_specs, out_specs=out_specs or [VMEM] * l...]
    slice x1 -> x0, local copies, waits for them, and re-layouts: 0.54 us -> none  [per_device(): flag[0, 0]]
  transfers between devices with their start and end apart: 4 -> 4, of which waited for: 1 -> 0; matrix products, arithmetic and copies ran while one was open for 0% -> 0% of each run, Pallas kernels for 28% -> 31%
where the time goes in v5:
time: 45.5 us; the launch traced here: 45.3 us
  Pallas kernels  20.7 us (45%)
  blocking collectives  11.6 us (25%)
  starting transfers between devices  11.5 us (25%)
  between operations  0.9 us (2%)
  loops' own time  0.64 us (1%)
    pallas_call x6, Pallas kernels, call(): pl.pallas_call(body, in_specs=in_specs, out_specs=out_specs or [VMEM] * l...  20.7 us
    all_to_all x1, blocking collectives, per_device(): every = lax.all_to_all(sums, ('row', 'col'), 0, 0, tiled=True)  11.6 us
    ppermute x2, starting transfers between devices, swaps(): lax.ppermute(second, axis, both(others))  7.38 us
    ppermute x2, starting transfers between devices, swaps(): lax.ppermute(first, axis, both(pairs))  4.11 us
  transfers between devices with their start and end apart: 4, of which 0 were waited for; matrix products, arithmetic and copies ran while one was open for 0% of the time, Pallas kernels for 31%

profile of v5, /device:TPU:1, one launch (start us, length us, event | category | flops | bytes accessed | tf_op | source)
XLA Modules:
  0.0 45.3 jit_solution(4655265985407479592)
XLA Ops:
  0.6 0.0 copy-start.4
  0.6 0.0 copy-start.5
  0.7 0.0 copy-start.1
  0.7 2.5 %shard_map.60 = (f32[40,512]{1,0:T(8,128)S(1)}, f32[40,512]{1,0:T(8,128)S(1)}) custom-call(s32[1,512,512]{2,1,0:T(8,128)} %edges.7, s32[1,512,512]{2,1,0:T(8,128)} %labels.3, f32[1,512,512]{2,1,0:T(8,128)} %prior.5, f32[1,512,512]{2,1,0:T(8,128)} %weight.5), custom_call_target="tpu_custom_call" | custom-call | flops 1048576 | bytes 1048576 | tf_op jit(solution)/shard_map/pallas_call | solution.py:532
  3.2 2.2 %collective-permute-start.8 = (f32[40,512]{1,0:T(8,128)S(1)}, f32[40,512]{1,0:T(8,128)S(1)}, u32[]{:S(2)}, u32[]{:S(2)}) collective-permute-start(f32[40,512]{1,0:T(8,128)S(1)} %get-tuple-element.233), channel_id=1, source_target_pairs={{0,1},{2,3},{4,5},{6,7},{1,0},{3,2},{5,4},{7,6},{8,9},{10,11},{12,... | collective-permute-start | bytes 245768 | tf_op jit(solution)/shard_map/ppermute | solution.py:528
  5.4 2.8 %collective-permute-start.9 = (f32[40,512]{1,0:T(8,128)S(1)}, f32[40,512]{1,0:T(8,128)S(1)}, u32[]{:S(2)}, u32[]{:S(2)}) collective-permute-start(f32[40,512]{1,0:T(8,128)S(1)} %get-tuple-element.234), channel_id=1, source_target_pairs={{1,2},{3,4},{5,6},{7,0},{2,1},{4,3},{6,5},{0,7},{9,10},{11,12},{13... | collective-permute-start | bytes 245768 | tf_op jit(solution)/shard_map/ppermute | solution.py:528
  8.2 0.0 copy-done.4
  8.2 0.0 copy-done.5
  8.2 0.0 copy-done.1
  8.2 2.8 %shard_map.59 = (s32[4,528,128]{2,1,0:T(8,128)S(1)}, f32[5,512,128]{2,1,0:T(8,128)S(1)}, f32[5,512,128]{2,1,0:T(8,128)S(1)}, f32[5,512,128]{2,1,0:T(8,128)S(1)},...) custom-call(s32[1,512,512]{2,1,0:T(8,128)S(1)} %copy-done.1, s32[1,512,512]{2,1,0:T(8,128)} %labels.3, ...), custom_call_target="tpu_custom_call" | custom-call | flops 16777216 | bytes 1048576 | tf_op jit(solution)/shard_map/pallas_call | solution.py:532
  11.0 0.0 collective-permute-done.8.col_first
  11.1 0.0 collective-permute-done.9.col_second
  11.1 0.2 shard_map.62
  11.3 1.9 %collective-permute-start.10 = (f32[40,640]{1,0:T(8,128)S(1)}, f32[40,640]{1,0:T(8,128)S(1)}, u32[]{:S(2)}, u32[]{:S(2)}) collective-permute-start(f32[40,640]{1,0:T(8,128)S(1)} %get-tuple-element.254), channel_id=1, source_target_pairs={{0,8},{16,24},{8,0},{24,16},{1,9},{17,25},{9,1},{25,17},{2,10},{18... | collective-permute-start | bytes 307208 | tf_op jit(solution)/shard_map/ppermute | solution.py:528
  13.2 4.6 %collective-permute-start.11 = (f32[40,640]{1,0:T(8,128)S(1)}, f32[40,640]{1,0:T(8,128)S(1)}, u32[]{:S(2)}, u32[]{:S(2)}) collective-permute-start(f32[40,640]{1,0:T(8,128)S(1)} %get-tuple-element.255), channel_id=1, source_target_pairs={{8,16},{16,8},{9,17},{17,9},{10,18},{18,10},{11,19},{19,11},{12,20... | collective-permute-start | bytes 307208 | tf_op jit(solution)/shard_map/ppermute | solution.py:528
  17.8 11.0 %shard_map.61 = (f32[5,512,128]{2,1,0:T(8,128)S(1)}, f32[5,512,128]{2,1,0:T(8,128)S(1)}, f32[5,512,128]{2,1,0:T(8,128)S(1)}, f32[5,512,128]{2,1,0:T(8,128)S(1)},...) custom-call(s32[1,512,512]{2,1,0:T(8,128)S(1)} %copy-done.1, ...), custom_call_target="tpu_custom_call", output_to_operand_aliasing={{0}: (4, {}), {1}: (5, {}), {2}: (6, {}), {3}: (7, {}), {4}... | custom-call | flops 67108864 | bytes 1048576 | tf_op jit(solution)/shard_map/pallas_call | solution.py:532
  28.8 0.0 collective-permute-done.10.refs_15_
  28.8 0.0 collective-permute-done.11.refs_16_
  28.8 1.0 %shard_map.63 = (f32[32,1,128]{2,1,0:T(1,128)S(1)}, f32[9,2,4,16,128]{4,3,2,1,0:T(8,128)S(1)}) custom-call(f32[5,512,128]{2,1,0:T(8,128)S(1)} %get-tuple-element.240.refs_0_, f32[5,512,128]{2,1,0:T(8,128)S(1)} %get-tuple-element.241.refs_1_, f32[5,512,128]{2,1,0:T(8,128)S(1)} %get-tuple-element.242.refs_2_, f32[5,512,128]{2,1,0:T(8,128)S(1)} %get-tuple-element.243.refs_3_, ...), custom_call_target="tpu_custom_call" | custom-call | flops 1048576 | bytes 1048576 | tf_op jit(solution)/shard_map/pallas_call | solution.py:532
  29.8 11.6 %all_to_all.31.every = f32[32,1,128]{2,1,0:T(1,128)S(1)} all-to-all(f32[32,1,128]{2,1,0:T(1,128)S(1)} %get-tuple-element.256), channel_id=1, replica_groups=mesh['img'=4,'row'=4,'col'=8] {'row','col'}, dimensions={0} | all-to-all | bytes 32768 | tf_op jit(solution)/shard_map/all_to_all | solution.py:592
  41.4 3.1 %shard_map.64 = (f32[1,512,512]{2,1,0:T(8,128)}, f32[1,512,512]{2,1,0:T(8,128)}, s32[1,1]{1,0:T(1,128)}) custom-call(f32[32,1,128]{2,1,0:T(1,128)S(1)} %all_to_all.31.every, s32[4,528,128]{2,1,0:T(8,128)S(1)} %get-tuple-element.232.lab_t.refs_12_, f32[9,2,4,16,128]{4,3,2,1,0:T(8,128)S(1)} %get-tuple-element.257.edge, ...), custom_call_target="tpu_custom_call" | custom-call | flops 1048576 | bytes 1048576 | tf_op jit(solution)/shard_map/pallas_call | solution.py:532
  44.5 0.6 %while.30 = (s32[]{:T(128)}, f32[1,512,512]{2,1,0:T(8,128)}, f32[1,512,512]{2,1,0:T(8,128)}, s32[1,512,512]{2,1,0:T(8,128)}, f32[1,512,512]{2,1,0:T(8,128)}, /*i...) while((s32[]{:T(128)}, f32[1,512,512]{2,1,0:T(8,128)}, f32[1,512,512]{2,1,0:T(8,128)}, ...), condition=%region_9.10_spmd, body=%region_0.9_spmd | while | flops 58720352 | bytes 45852768 | solution.py:604
Async XLA Ops:
  0.6 7.6 %copy-start.4 = (f32[1,512,512]{2,1,0:T(8,128)S(1)}, f32[1,512,512]{2,1,0:T(8,128)}, u32[]{:S(2)}) copy-start(f32[1,512,512]{2,1,0:T(8,128)} %prior.5) | copy-start | bytes 3145732
  0.6 7.6 %copy-start.5 = (f32[1,512,512]{2,1,0:T(8,128)S(1)}, f32[1,512,512]{2,1,0:T(8,128)}, u32[]{:S(2)}) copy-start(f32[1,512,512]{2,1,0:T(8,128)} %weight.5) | copy-start | bytes 3145732
  0.7 7.6 %copy-start.1 = (s32[1,512,512]{2,1,0:T(8,128)S(1)}, s32[1,512,512]{2,1,0:T(8,128)}, u32[]{:S(2)}) copy-start(s32[1,512,512]{2,1,0:T(8,128)} %edges.7) | copy-start | bytes 3145732
  3.2 7.8 %collective-permute-start.8 = (f32[40,512]{1,0:T(8,128)S(1)}, f32[40,512]{1,0:T(8,128)S(1)}, u32[]{:S(2)}, u32[]{:S(2)}) collective-permute-start(f32[40,512]{1,0:T(8,128)S(1)} %get-tuple-element.233), channel_id=1, source_target_pairs={{0,1},{2,3},{4,5},{6,7},{1,0},{3,2},{5,4},{7,6},{8,9},{10,11},{12,... | collective-permute-start | bytes 245768 | tf_op jit(solution)/shard_map/ppermute | solution.py:528
  5.4 5.7 %collective-permute-start.9 = (f32[40,512]{1,0:T(8,128)S(1)}, f32[40,512]{1,0:T(8,128)S(1)}, u32[]{:S(2)}, u32[]{:S(2)}) collective-permute-start(f32[40,512]{1,0:T(8,128)S(1)} %get-tuple-element.234), channel_id=1, source_target_pairs={{1,2},{3,4},{5,6},{7,0},{2,1},{4,3},{6,5},{0,7},{9,10},{11,12},{13... | collective-permute-start | bytes 245768 | tf_op jit(solution)/shard_map/ppermute | solution.py:528
  11.3 17.5 %collective-permute-start.10 = (f32[40,640]{1,0:T(8,128)S(1)}, f32[40,640]{1,0:T(8,128)S(1)}, u32[]{:S(2)}, u32[]{:S(2)}) collective-permute-start(f32[40,640]{1,0:T(8,128)S(1)} %get-tuple-element.254), channel_id=1, source_target_pairs={{0,8},{16,24},{8,0},{24,16},{1,9},{17,25},{9,1},{25,17},{2,10},{18... | collective-permute-start | bytes 307208 | tf_op jit(solution)/shard_map/ppermute | solution.py:528
  13.2 15.6 %collective-permute-start.11 = (f32[40,640]{1,0:T(8,128)S(1)}, f32[40,640]{1,0:T(8,128)S(1)}, u32[]{:S(2)}, u32[]{:S(2)}) collective-permute-start(f32[40,640]{1,0:T(8,128)S(1)} %get-tuple-element.255), channel_id=1, source_target_pairs={{8,16},{16,8},{9,17},{17,9},{10,18},{18,10},{11,19},{19,11},{12,20... | collective-permute-start | bytes 307208 | tf_op jit(solution)/shard_map/ppermute | solution.py:528

commit v6 on v5

--- a/solution.py
+++ b/solution.py
@@ -86,7 +86,7 @@
 
 WIDTH = HALO + 1
 LINES = 40
-TOP_OF = ((0, 0, 8), (2, 8, 8), (3, 16, 8), (1, 24, 16))
+SLOTS = ((0, 0, 8), (2, 8, 8), (3, 16, 8), (1, 24, 16))
 
 
 def lane_ids(rows):
@@ -97,30 +97,40 @@
     return pltpu.roll(x, by % LANES, 1) if by % LANES else x
 
 
-def col_pack(edges, labels, prior, weight, first, second, ints, floats, sem):
-    arrays = (edges, labels, prior, weight)
+def col_pack(edges, labels, prior, weight, first, second, lab_t, ints, floats, sem):
     rows, cols = edges.shape[1], edges.shape[2]
+    tiles = cols // LANES
     lane = lane_ids(LANES)
-    held = [(ints if a < 2 else floats).at[:, a % 2] for a in range(4)]
-    copies = []
+    pairs = []
     for side in range(2):
-        for a, ref in enumerate(arrays):
-            src = ref.at[0, :, pl.ds(side * (cols - LANES), LANES)]
-            copies.append(pltpu.make_async_copy(src, held[a].at[side], sem.at[side, a]))
+        at = pl.ds(side * (cols - LANES), LANES)
+        pairs.append((edges.at[0, :, at], ints.at[side]))
+        pairs.append((prior.at[0, :, at], floats.at[side, 0]))
+        pairs.append((weight.at[0, :, at], floats.at[side, 1]))
+    for j in (0, tiles - 1, *range(1, tiles - 1)):
+        pairs.append((labels.at[0, :, pl.ds(j * LANES, LANES)], lab_t.at[j, pl.ds(HALO, rows), :]))
+    copies = [pltpu.make_async_copy(*pair, sem.at[q]) for q, pair in enumerate(pairs)]
     for copy in copies:
         copy.start()
-    for copy in copies:
+    seeds = jnp.full((HALO, LANES), 2, jnp.int32)
+    for j in range(tiles):
+        lab_t[j, :HALO, :] = seeds
+        lab_t[j, HALO + rows :, :] = seeds
+    for copy in copies[:8]:
         copy.wait()
     for chunk in range(rows // LANES):
         at = slice(chunk * LANES, (chunk + 1) * LANES)
         lines = []
-        for side, base in ((0, 0), (1, LANES - WIDTH)):
+        for side in range(2):
+            labs = lab_t[side * (tiles - 1), HALO + chunk * LANES : HALO + (chunk + 1) * LANES, :]
             packed = None
-            for a in range(4):
-                x = turn(held[a][side, at, :].astype(jnp.float32), a * WIDTH - base)
-                packed = x if packed is None else jnp.where(lane < a * WIDTH, packed, x)
+            for x, (_, line, n) in zip((ints[side, at, :], floats[side, 0, at, :], floats[side, 1, at, :], labs), SLOTS):
+                x = turn(x.astype(jnp.float32), line + side * n)
+                packed = x if packed is None else jnp.where(lane < line, packed, x)
             lines.append(jnp.swapaxes(packed, 0, 1)[:LINES])
         first[:, at], second[:, at] = ordered("col", *lines)
+    for copy in copies[8:]:
+        copy.wait()
 
 
 def ordered(axis, before, after):
@@ -129,27 +139,29 @@
 
 
 def side_tiles(first, second, at):
-    pad = jnp.zeros((LANES - LINES, LANES), jnp.float32)
-    r, l = ordered("col", second[:, at : at + LANES], first[:, at : at + LANES])
-    r = jnp.swapaxes(jnp.concatenate([r, pad], 0), 0, 1)
-    l = jnp.swapaxes(jnp.concatenate([l, pad], 0), 0, 1)
+    right, left = ordered("col", second[:, at : at + LANES], first[:, at : at + LANES])
+    both = []
+    for _, line, n in SLOTS:
+        both += [left[line : line + n], right[line : line + n]]
+    both.append(jnp.zeros((LANES - 2 * LINES, LANES), jnp.float32))
+    both = jnp.swapaxes(jnp.concatenate(both, 0), 0, 1)
     lane = lane_ids(LANES)
-    tiles = []
-    for a in range(4):
-        right = turn(r, -a * WIDTH)
-        left = turn(l, LANES - WIDTH - a * WIDTH)
-        outside = 2.0 if a == 1 else 0.0
-        tiles.append(jnp.where(lane < WIDTH, right, jnp.where(lane >= LANES - WIDTH, left, outside)))
+    tiles = {}
+    for a, line, n in SLOTS:
+        width, outside = (WIDTH, 2.0) if a == 1 else (HALO, 0.0)
+        inside = (lane < width) | (lane >= LANES - width)
+        tiles[a] = jnp.where(inside, turn(both, -(2 * line + n)), outside)
     return tiles
 
 
-def row_pack(edges, lab_t, prior, weight, col_first, col_second, first, second):
+def row_pack(edges, lab_t, prior, weight, col_first, col_second, after, first, second):
+    del after
     rows, cols = edges.shape[1], edges.shape[2]
     tiles = cols // LANES
     refs = (edges, None, prior, weight)
     top = side_tiles(col_first, col_second, 0)
     bottom = side_tiles(col_first, col_second, rows - LANES)
-    for a, line, n in TOP_OF:
+    for a, line, n in SLOTS:
         here = slice(line, line + n)
         for j in range(tiles):
             lanes = slice(j * LANES, (j + 1) * LANES)
@@ -201,22 +213,11 @@
     return list(zip(*map(decode, code, lab, lab_r, lab_l, lab_d, lab_u, prior, weight)))
 
 
-def prepare(edges, labels, prior, weight, lab_t, *terms):
+def prepare(edges, lab_t, prior, weight, *terms):
     rows, cols = edges.shape[1], edges.shape[2]
     tiles = cols // LANES
     lane = lane_ids(8)
     seeds = jnp.full((8, LANES), 2, jnp.int32)
-    for j in range(tiles):
-        lab_t[j, :HALO, :] = seeds
-        lab_t[j, HALO + rows :, :] = seeds
-
-    def lay(i, _):
-        s = pl.multiple_of(8 * i, 8)
-        for j in range(tiles):
-            lab_t[j, pl.ds(s + HALO, 8), :] = labels[0, pl.ds(s, 8), j * LANES : (j + 1) * LANES]
-        return 0
-
-    lax.fori_loop(0, rows // 8, lay, 0, unroll=16)
 
     def body(i, _):
         s = pl.multiple_of(8 * i, 8)
@@ -550,12 +551,13 @@
     tiles = inner + 1
     dma = pltpu.SemaphoreType.DMA
 
-    col_messages = call(
-        col_pack, [HBM] * 4, [shape((LINES, rows), f32)] * 2,
+    *col_messages, lab_t = call(
+        col_pack, [HBM] * 4,
+        [shape((LINES, rows), f32)] * 2 + [shape((inner, rows + 2 * HALO, LANES), i32)],
         [
-            pltpu.VMEM((2, 2, rows, LANES), i32),
+            pltpu.VMEM((2, rows, LANES), i32),
             pltpu.VMEM((2, 2, rows, LANES), f32),
-            dma((2, 4)),
+            dma((6 + inner,)),
         ],
         6, 1 << 20, arrays,
     )
@@ -563,13 +565,12 @@
 
     n = ITERS + 1
     whole = shape((tiles, rows, LANES), f32)
-    lab_t, *terms = call(
-        prepare, [VMEM] * 4, [shape((inner, rows + 2 * HALO, LANES), i32)] + [whole] * 5, [],
-        6, 1 << 24, arrays,
+    terms = call(
+        prepare, [VMEM] * 4, [whole] * 5, [], 6, 1 << 24, (edges, lab_t, prior, data_weight),
     )
     row_messages = call(
-        row_pack, [VMEM] * 6, [shape((LINES, tiles * LANES), f32)] * 2, [],
-        4, 1 << 20, (edges, lab_t, prior, data_weight, col_first, col_second),
+        row_pack, [VMEM] * 7, [shape((LINES, tiles * LANES), f32)] * 2, [],
+        4, 1 << 20, (edges, lab_t, prior, data_weight, col_first, col_second, terms[1]),
     )
     row_first, row_second = swaps("row", *row_messages, False)
 

time: 45.5 us -> 45.5 us (level)
  Pallas kernels: 20.7 us -> 19.6 us
  waiting for transfers between devices: 0.01 us -> 1.06 us
    pallas_call x6, Pallas kernels: 20.7 us -> 19.6 us  [call(): pl.pallas_call(body, in_specs=in_specs, out_specs=out_specs or [VMEM] * l...]
    ppermute x2, waiting for transfers between devices: 0.01 us -> 1.06 us  [swaps(): lax.ppermute(second, axis, both(others))]
  transfers between devices with their start and end apart: 4 -> 4, of which waited for: 0 -> 1; matrix products, arithmetic and copies ran while one was open for 0% -> 0% of each run, Pallas kernels for 31% -> 28%
where the time goes in v6:
time: 45.5 us; the launch traced here: 45.3 us
  Pallas kernels  19.6 us (43%)
  starting transfers between devices  11.8 us (26%)
  blocking collectives  11.4 us (25%)
  waiting for transfers between devices  1.06 us (2%)
  between operations  0.89 us (2%)
  loops' own time  0.64 us (1%)
    pallas_call x6, Pallas kernels, call(): pl.pallas_call(body, in_specs=in_specs, out_specs=out_specs or [VMEM] * l...  19.6 us
    all_to_all x1, blocking collectives, per_device(): every = lax.all_to_all(sums, ('row', 'col'), 0, 0, tiled=True)  11.4 us
    ppermute x2, starting transfers between devices, swaps(): lax.ppermute(second, axis, both(others))  7.38 us
    ppermute x2, starting transfers between devices, swaps(): lax.ppermute(first, axis, both(pairs))  4.38 us
    ppermute x2, waiting for transfers between devices, swaps(): lax.ppermute(second, axis, both(others))  1.06 us
  transfers between devices with their start and end apart: 4, of which 1 were waited for; matrix products, arithmetic and copies ran while one was open for 0% of the time, Pallas kernels for 28%

profile of v6, /device:TPU:1, one launch (start us, length us, event | category | flops | bytes accessed | tf_op | source)
XLA Modules:
  0.0 45.3 jit_solution(8760851444883245460)
XLA Ops:
  0.6 0.0 copy-start.1
  0.6 0.0 copy-start.5
  0.7 0.0 copy-start.4
  0.7 2.6 %shard_map.59 = (f32[40,512]{1,0:T(8,128)S(1)}, f32[40,512]{1,0:T(8,128)S(1)}, s32[4,528,128]{2,1,0:T(8,128)S(1)}) custom-call(s32[1,512,512]{2,1,0:T(8,128)} %edges.7, s32[1,512,512]{2,1,0:T(8,128)} %labels.1, f32[1,512,512]{2,1,0:T(8,128)} %prior.5, f32[1,512,512]{2,1,0:T(8,128)} %weight.5), custom_call_target="tpu_custom_call" | custom-call | flops 1048576 | bytes 1048576 | tf_op jit(solution)/shard_map/pallas_call | solution.py:533
  3.2 2.2 %collective-permute-start.8 = (f32[40,512]{1,0:T(8,128)S(1)}, f32[40,512]{1,0:T(8,128)S(1)}, u32[]{:S(2)}, u32[]{:S(2)}) collective-permute-start(f32[40,512]{1,0:T(8,128)S(1)} %get-tuple-element.233), channel_id=1, source_target_pairs={{0,1},{2,3},{4,5},{6,7},{1,0},{3,2},{5,4},{7,6},{8,9},{10,11},{12,... | collective-permute-start | bytes 245768 | tf_op jit(solution)/shard_map/ppermute | solution.py:529
  5.4 2.8 %collective-permute-start.9 = (f32[40,512]{1,0:T(8,128)S(1)}, f32[40,512]{1,0:T(8,128)S(1)}, u32[]{:S(2)}, u32[]{:S(2)}) collective-permute-start(f32[40,512]{1,0:T(8,128)S(1)} %get-tuple-element.234), channel_id=1, source_target_pairs={{1,2},{3,4},{5,6},{7,0},{2,1},{4,3},{6,5},{0,7},{9,10},{11,12},{13... | collective-permute-start | bytes 245768 | tf_op jit(solution)/shard_map/ppermute | solution.py:529
  8.3 0.0 copy-done.1
  8.3 0.0 copy-done.5
  8.3 0.0 copy-done.4
  8.3 1.5 %shard_map.60 = (f32[5,512,128]{2,1,0:T(8,128)S(1)}, f32[5,512,128]{2,1,0:T(8,128)S(1)}, f32[5,512,128]{2,1,0:T(8,128)S(1)}, f32[5,512,128]{2,1,0:T(8,128)S(1)}, f32[5,512,128]{2,1,0:T(8,128)S(1)}) custom-call(s32[1,512,512]{2,1,0:T(8,128)S(1)} %copy-done.1, s32[4,528,128]{2,1,0:T(8,128)S(1)} %get-tuple-element.232.lab_t.refs_12_, ...), custom_call_target="tpu_custom_call" | custom-call | flops 16777216 | bytes 1048576 | tf_op jit(solution)/shard_map/pallas_call | solution.py:533
  9.8 0.0 collective-permute-done.8.col_first
  9.8 1.1 %collective-permute-done.9.col_second = f32[40,512]{1,0:T(8,128)S(1)} collective-permute-done((f32[40,512]{1,0:T(8,128)S(1)}, f32[40,512]{1,0:T(8,128)S(1)}, u32[]{:S(2)}, u32[]{:S(2)}) %collective-permute-start.9) | collective-permute-done | bytes 81952 | tf_op jit(solution)/shard_map/ppermute | solution.py:529
  10.8 0.2 shard_map.62
  11.0 2.2 %collective-permute-start.10 = (f32[40,640]{1,0:T(8,128)S(1)}, f32[40,640]{1,0:T(8,128)S(1)}, u32[]{:S(2)}, u32[]{:S(2)}) collective-permute-start(f32[40,640]{1,0:T(8,128)S(1)} %get-tuple-element.254), channel_id=1, source_target_pairs={{0,8},{16,24},{8,0},{24,16},{1,9},{17,25},{9,1},{25,17},{2,10},{18... | collective-permute-start | bytes 307208 | tf_op jit(solution)/shard_map/ppermute | solution.py:529
  13.2 4.6 %collective-permute-start.11 = (f32[40,640]{1,0:T(8,128)S(1)}, f32[40,640]{1,0:T(8,128)S(1)}, u32[]{:S(2)}, u32[]{:S(2)}) collective-permute-start(f32[40,640]{1,0:T(8,128)S(1)} %get-tuple-element.255), channel_id=1, source_target_pairs={{8,16},{16,8},{9,17},{17,9},{10,18},{18,10},{11,19},{19,11},{12,20... | collective-permute-start | bytes 307208 | tf_op jit(solution)/shard_map/ppermute | solution.py:529
  17.8 11.2 %shard_map.61 = (f32[5,512,128]{2,1,0:T(8,128)S(1)}, f32[5,512,128]{2,1,0:T(8,128)S(1)}, f32[5,512,128]{2,1,0:T(8,128)S(1)}, f32[5,512,128]{2,1,0:T(8,128)S(1)},...) custom-call(s32[1,512,512]{2,1,0:T(8,128)S(1)} %copy-done.1, ...), custom_call_target="tpu_custom_call", output_to_operand_aliasing={{0}: (4, {}), {1}: (5, {}), {2}: (6, {}), {3}: (7, {}), {4}... | custom-call | flops 67108864 | bytes 1048576 | tf_op jit(solution)/shard_map/pallas_call | solution.py:533
  29.0 0.0 collective-permute-done.10.refs_15_
  29.0 0.0 collective-permute-done.11.refs_16_
  29.0 1.0 %shard_map.63 = (f32[32,1,128]{2,1,0:T(1,128)S(1)}, f32[9,2,4,16,128]{4,3,2,1,0:T(8,128)S(1)}) custom-call(f32[5,512,128]{2,1,0:T(8,128)S(1)} %get-tuple-element.240.refs_0_, f32[5,512,128]{2,1,0:T(8,128)S(1)} %get-tuple-element.241.refs_1_, f32[5,512,128]{2,1,0:T(8,128)S(1)} %get-tuple-element.242.refs_2_, f32[5,512,128]{2,1,0:T(8,128)S(1)} %get-tuple-element.243.refs_3_, ...), custom_call_target="tpu_custom_call" | custom-call | flops 1048576 | bytes 1048576 | tf_op jit(solution)/shard_map/pallas_call | solution.py:533
  30.0 11.4 %all_to_all.31.every = f32[32,1,128]{2,1,0:T(1,128)S(1)} all-to-all(f32[32,1,128]{2,1,0:T(1,128)S(1)} %get-tuple-element.256), channel_id=1, replica_groups=mesh['img'=4,'row'=4,'col'=8] {'row','col'}, dimensions={0} | all-to-all | bytes 32768 | tf_op jit(solution)/shard_map/all_to_all | solution.py:593
  41.4 3.2 %shard_map.64 = (f32[1,512,512]{2,1,0:T(8,128)}, f32[1,512,512]{2,1,0:T(8,128)}, s32[1,1]{1,0:T(1,128)}) custom-call(f32[32,1,128]{2,1,0:T(1,128)S(1)} %all_to_all.31.every, s32[4,528,128]{2,1,0:T(8,128)S(1)} %get-tuple-element.232.lab_t.refs_12_, f32[9,2,4,16,128]{4,3,2,1,0:T(8,128)S(1)} %get-tuple-element.257.edge, ...), custom_call_target="tpu_custom_call" | custom-call | flops 1048576 | bytes 1048576 | tf_op jit(solution)/shard_map/pallas_call | solution.py:533
  44.5 0.6 %while.30 = (s32[]{:T(128)}, f32[1,512,512]{2,1,0:T(8,128)}, f32[1,512,512]{2,1,0:T(8,128)}, s32[1,512,512]{2,1,0:T(8,128)}, f32[1,512,512]{2,1,0:T(8,128)}, /*i...) while((s32[]{:T(128)}, f32[1,512,512]{2,1,0:T(8,128)}, f32[1,512,512]{2,1,0:T(8,128)}, ...), condition=%region_9.10_spmd, body=%region_0.9_spmd | while | flops 58720352 | bytes 45852768 | solution.py:605
Async XLA Ops:
  0.6 7.6 %copy-start.1 = (s32[1,512,512]{2,1,0:T(8,128)S(1)}, s32[1,512,512]{2,1,0:T(8,128)}, u32[]{:S(2)}) copy-start(s32[1,512,512]{2,1,0:T(8,128)} %edges.7) | copy-start | bytes 3145732
  0.6 7.6 %copy-start.5 = (f32[1,512,512]{2,1,0:T(8,128)S(1)}, f32[1,512,512]{2,1,0:T(8,128)}, u32[]{:S(2)}) copy-start(f32[1,512,512]{2,1,0:T(8,128)} %weight.5) | copy-start | bytes 3145732
  0.7 7.6 %copy-start.4 = (f32[1,512,512]{2,1,0:T(8,128)S(1)}, f32[1,512,512]{2,1,0:T(8,128)}, u32[]{:S(2)}) copy-start(f32[1,512,512]{2,1,0:T(8,128)} %prior.5) | copy-start | bytes 3145732
  3.2 6.5 %collective-permute-start.8 = (f32[40,512]{1,0:T(8,128)S(1)}, f32[40,512]{1,0:T(8,128)S(1)}, u32[]{:S(2)}, u32[]{:S(2)}) collective-permute-start(f32[40,512]{1,0:T(8,128)S(1)} %get-tuple-element.233), channel_id=1, source_target_pairs={{0,1},{2,3},{4,5},{6,7},{1,0},{3,2},{5,4},{7,6},{8,9},{10,11},{12,... | collective-permute-start | bytes 245768 | tf_op jit(solution)/shard_map/ppermute | solution.py:529
  5.4 5.4 %collective-permute-start.9 = (f32[40,512]{1,0:T(8,128)S(1)}, f32[40,512]{1,0:T(8,128)S(1)}, u32[]{:S(2)}, u32[]{:S(2)}) collective-permute-start(f32[40,512]{1,0:T(8,128)S(1)} %get-tuple-element.234), channel_id=1, source_target_pairs={{1,2},{3,4},{5,6},{7,0},{2,1},{4,3},{6,5},{0,7},{9,10},{11,12},{13... | collective-permute-start | bytes 245768 | tf_op jit(solution)/shard_map/ppermute | solution.py:529
  11.0 18.0 %collective-permute-start.10 = (f32[40,640]{1,0:T(8,128)S(1)}, f32[40,640]{1,0:T(8,128)S(1)}, u32[]{:S(2)}, u32[]{:S(2)}) collective-permute-start(f32[40,640]{1,0:T(8,128)S(1)} %get-tuple-element.254), channel_id=1, source_target_pairs={{0,8},{16,24},{8,0},{24,16},{1,9},{17,25},{9,1},{25,17},{2,10},{18... | collective-permute-start | bytes 307208 | tf_op jit(solution)/shard_map/ppermute | solution.py:529
  13.2 15.8 %collective-permute-start.11 = (f32[40,640]{1,0:T(8,128)S(1)}, f32[40,640]{1,0:T(8,128)S(1)}, u32[]{:S(2)}, u32[]{:S(2)}) collective-permute-start(f32[40,640]{1,0:T(8,128)S(1)} %get-tuple-element.255), channel_id=1, source_target_pairs={{8,16},{16,8},{9,17},{17,9},{10,18},{18,10},{11,19},{19,11},{12,20... | collective-permute-start | bytes 307208 | tf_op jit(solution)/shard_map/ppermute | solution.py:529

commit v7 on v6

--- a/solution.py
+++ b/solution.py
@@ -184,6 +184,7 @@
 
 
 SCALE = 2.0 / RADIUS
+SPARE = 24
 
 
 def decode(code, lab, lab_r, lab_l, lab_d, lab_u, prior, weight):
@@ -276,7 +277,7 @@
     for k in range(1, ITERS):
         for j in range(tiles):
             field[k][j, :8, :] = zero
-            field[k][j, rows - 8 :, :] = zero
+            field[k][j, rows - 8 : rows, :] = zero
     end = inner - 1
 
     def sides(i, _):
@@ -340,7 +341,7 @@
     field, (er_t, ed_t, eu_t, diag_t, lab_t, side_lab) = refs[:n], refs[n : n + 6]
     sums, row_first, row_second = refs[n + 6 : n + 9]
     out, edge, labs, grid = refs[n + 9 :]
-    inner, rows = lab_t.shape[0], er_t.shape[1]
+    inner, rows = lab_t.shape[0], lab_t.shape[1] - 2 * HALO
     tiles = inner + 1
     lane = lane_ids(8)
     sub = lax.broadcasted_iota(jnp.int32, (8, LANES), 0)
@@ -474,7 +475,7 @@
 def combine(every, lab_t, edge, *refs):
     n = ITERS + 1
     field, (labeling, residual, flag, sol_s, res_s, sem) = refs[:n], refs[n:]
-    inner, rows = field[0].shape[0] - 1, field[0].shape[1]
+    inner, rows = lab_t.shape[0], lab_t.shape[1] - 2 * HALO
     g = jnp.sum(every[:, 0, :], axis=0, keepdims=True)
     dots = [jnp.broadcast_to(g[:, q : q + 1], (8, LANES)) for q in range(2 * ITERS + 1)]
     x, r, good = coefficients(dots)
@@ -564,7 +565,7 @@
     col_first, col_second = swaps("col", *col_messages, True)
 
     n = ITERS + 1
-    whole = shape((tiles, rows, LANES), f32)
+    whole = shape((tiles, rows + SPARE, LANES), f32)
     terms = call(
         prepare, [VMEM] * 4, [whole] * 5, [], 6, 1 << 24, (edges, lab_t, prior, data_weight),
     )

time: 45.5 us -> 45.1 us (level)
  Pallas kernels: 19.6 us -> 19 us
    pallas_call x6, Pallas kernels: 19.6 us -> 19 us  [call(): pl.pallas_call(body, in_specs=in_specs, out_specs=out_specs or [VMEM] * l...]
  transfers between devices with their start and end apart: 4 -> 4, of which waited for: 1 -> 1; matrix products, arithmetic and copies ran while one was open for 0% -> 0% of each run, Pallas kernels for 28% -> 27%
where the time goes in v7:
time: 45.1 us; the launch traced here: 44.9 us
  Pallas kernels  19 us (42%)
  starting transfers between devices  11.8 us (26%)
  blocking collectives  11.4 us (25%)
  waiting for transfers between devices  1.06 us (2%)
  between operations  0.89 us (2%)
  loops' own time  0.82 us (2%)
    pallas_call x6, Pallas kernels, call(): pl.pallas_call(body, in_specs=in_specs, out_specs=out_specs or [VMEM] * l...  19 us
    all_to_all x1, blocking collectives, per_device(): every = lax.all_to_all(sums, ('row', 'col'), 0, 0, tiled=True)  11.4 us
    ppermute x2, starting transfers between devices, swaps(): lax.ppermute(second, axis, both(others))  7.38 us
    ppermute x2, starting transfers between devices, swaps(): lax.ppermute(first, axis, both(pairs))  4.38 us
    ppermute x2, waiting for transfers between devices, swaps(): lax.ppermute(second, axis, both(others))  1.06 us
  transfers between devices with their start and end apart: 4, of which 1 were waited for; matrix products, arithmetic and copies ran while one was open for 0% of the time, Pallas kernels for 27%

profile of v7, /device:TPU:1, one launch (start us, length us, event | category | flops | bytes accessed | tf_op | source)
XLA Modules:
  0.0 44.9 jit_solution(13479305243373889052)
XLA Ops:
  0.6 0.0 copy-start.1
  0.6 0.0 copy-start.5
  0.7 0.0 copy-start.4
  0.7 2.6 %shard_map.59 = (f32[40,512]{1,0:T(8,128)S(1)}, f32[40,512]{1,0:T(8,128)S(1)}, s32[4,528,128]{2,1,0:T(8,128)S(1)}) custom-call(s32[1,512,512]{2,1,0:T(8,128)} %edges.7, s32[1,512,512]{2,1,0:T(8,128)} %labels.1, f32[1,512,512]{2,1,0:T(8,128)} %prior.5, f32[1,512,512]{2,1,0:T(8,128)} %weight.5), custom_call_target="tpu_custom_call" | custom-call | flops 1048576 | bytes 1048576 | tf_op jit(solution)/shard_map/pallas_call | solution.py:534
  3.2 2.2 %collective-permute-start.8 = (f32[40,512]{1,0:T(8,128)S(1)}, f32[40,512]{1,0:T(8,128)S(1)}, u32[]{:S(2)}, u32[]{:S(2)}) collective-permute-start(f32[40,512]{1,0:T(8,128)S(1)} %get-tuple-element.233), channel_id=1, source_target_pairs={{0,1},{2,3},{4,5},{6,7},{1,0},{3,2},{5,4},{7,6},{8,9},{10,11},{12,... | collective-permute-start | bytes 245768 | tf_op jit(solution)/shard_map/ppermute | solution.py:530
  5.4 2.8 %collective-permute-start.9 = (f32[40,512]{1,0:T(8,128)S(1)}, f32[40,512]{1,0:T(8,128)S(1)}, u32[]{:S(2)}, u32[]{:S(2)}) collective-permute-start(f32[40,512]{1,0:T(8,128)S(1)} %get-tuple-element.234), channel_id=1, source_target_pairs={{1,2},{3,4},{5,6},{7,0},{2,1},{4,3},{6,5},{0,7},{9,10},{11,12},{13... | collective-permute-start | bytes 245768 | tf_op jit(solution)/shard_map/ppermute | solution.py:530
  8.3 0.0 copy-done.1
  8.3 0.0 copy-done.5
  8.3 0.0 copy-done.4
  8.3 1.5 %shard_map.60 = (f32[5,536,128]{2,1,0:T(8,128)S(1)}, f32[5,536,128]{2,1,0:T(8,128)S(1)}, f32[5,536,128]{2,1,0:T(8,128)S(1)}, f32[5,536,128]{2,1,0:T(8,128)S(1)}, f32[5,536,128]{2,1,0:T(8,128)S(1)}) custom-call(s32[1,512,512]{2,1,0:T(8,128)S(1)} %copy-done.1, s32[4,528,128]{2,1,0:T(8,128)S(1)} %get-tuple-element.232.lab_t.refs_12_, ...), custom_call_target="tpu_custom_call" | custom-call | flops 16777216 | bytes 1048576 | tf_op jit(solution)/shard_map/pallas_call | solution.py:534
  9.8 0.0 collective-permute-done.8.col_first
  9.8 1.1 %collective-permute-done.9.col_second = f32[40,512]{1,0:T(8,128)S(1)} collective-permute-done((f32[40,512]{1,0:T(8,128)S(1)}, f32[40,512]{1,0:T(8,128)S(1)}, u32[]{:S(2)}, u32[]{:S(2)}) %collective-permute-start.9) | collective-permute-done | bytes 81952 | tf_op jit(solution)/shard_map/ppermute | solution.py:530
  10.8 0.2 shard_map.62
  11.0 2.2 %collective-permute-start.10 = (f32[40,640]{1,0:T(8,128)S(1)}, f32[40,640]{1,0:T(8,128)S(1)}, u32[]{:S(2)}, u32[]{:S(2)}) collective-permute-start(f32[40,640]{1,0:T(8,128)S(1)} %get-tuple-element.254), channel_id=1, source_target_pairs={{0,8},{16,24},{8,0},{24,16},{1,9},{17,25},{9,1},{25,17},{2,10},{18... | collective-permute-start | bytes 307208 | tf_op jit(solution)/shard_map/ppermute | solution.py:530
  13.2 4.6 %collective-permute-start.11 = (f32[40,640]{1,0:T(8,128)S(1)}, f32[40,640]{1,0:T(8,128)S(1)}, u32[]{:S(2)}, u32[]{:S(2)}) collective-permute-start(f32[40,640]{1,0:T(8,128)S(1)} %get-tuple-element.255), channel_id=1, source_target_pairs={{8,16},{16,8},{9,17},{17,9},{10,18},{18,10},{11,19},{19,11},{12,20... | collective-permute-start | bytes 307208 | tf_op jit(solution)/shard_map/ppermute | solution.py:530
  17.8 10.5 %shard_map.61 = (f32[5,536,128]{2,1,0:T(8,128)S(1)}, f32[5,536,128]{2,1,0:T(8,128)S(1)}, f32[5,536,128]{2,1,0:T(8,128)S(1)}, f32[5,536,128]{2,1,0:T(8,128)S(1)},...) custom-call(s32[1,512,512]{2,1,0:T(8,128)S(1)} %copy-done.1, ...), custom_call_target="tpu_custom_call", output_to_operand_aliasing={{0}: (4, {}), {1}: (5, {}), {2}: (6, {}), {3}: (7, {}), {4}... | custom-call | flops 67108864 | bytes 1048576 | tf_op jit(solution)/shard_map/pallas_call | solution.py:534
  28.3 0.0 collective-permute-done.10.refs_15_
  28.3 0.0 collective-permute-done.11.refs_16_
  28.3 1.0 %shard_map.63 = (f32[32,1,128]{2,1,0:T(1,128)S(1)}, f32[9,2,4,16,128]{4,3,2,1,0:T(8,128)S(1)}) custom-call(f32[5,536,128]{2,1,0:T(8,128)S(1)} %get-tuple-element.240.refs_0_, f32[5,536,128]{2,1,0:T(8,128)S(1)} %get-tuple-element.241.refs_1_, f32[5,536,128]{2,1,0:T(8,128)S(1)} %get-tuple-element.242.refs_2_, f32[5,536,128]{2,1,0:T(8,128)S(1)} %get-tuple-element.243.refs_3_, ...), custom_call_target="tpu_custom_call" | custom-call | flops 1048576 | bytes 1048576 | tf_op jit(solution)/shard_map/pallas_call | solution.py:534
  29.3 11.4 %all_to_all.31.every = f32[32,1,128]{2,1,0:T(1,128)S(1)} all-to-all(f32[32,1,128]{2,1,0:T(1,128)S(1)} %get-tuple-element.256), channel_id=1, replica_groups=mesh['img'=4,'row'=4,'col'=8] {'row','col'}, dimensions={0} | all-to-all | bytes 32768 | tf_op jit(solution)/shard_map/all_to_all | solution.py:594
  40.7 3.2 %shard_map.64 = (f32[1,512,512]{2,1,0:T(8,128)}, f32[1,512,512]{2,1,0:T(8,128)}, s32[1,1]{1,0:T(1,128)}) custom-call(f32[32,1,128]{2,1,0:T(1,128)S(1)} %all_to_all.31.every, s32[4,528,128]{2,1,0:T(8,128)S(1)} %get-tuple-element.232.lab_t.refs_12_, f32[9,2,4,16,128]{4,3,2,1,0:T(8,128)S(1)} %get-tuple-element.257.edge, ...), custom_call_target="tpu_custom_call" | custom-call | flops 1048576 | bytes 1048576 | tf_op jit(solution)/shard_map/pallas_call | solution.py:534
  43.9 0.8 %while.30 = (s32[]{:T(128)}, f32[1,512,512]{2,1,0:T(8,128)}, f32[1,512,512]{2,1,0:T(8,128)}, s32[1,512,512]{2,1,0:T(8,128)}, f32[1,512,512]{2,1,0:T(8,128)}, /*i...) while((s32[]{:T(128)}, f32[1,512,512]{2,1,0:T(8,128)}, f32[1,512,512]{2,1,0:T(8,128)}, ...), condition=%region_9.10_spmd, body=%region_0.9_spmd | while | flops 58720352 | bytes 45852768 | solution.py:606
Async XLA Ops:
  0.6 7.6 %copy-start.1 = (s32[1,512,512]{2,1,0:T(8,128)S(1)}, s32[1,512,512]{2,1,0:T(8,128)}, u32[]{:S(2)}) copy-start(s32[1,512,512]{2,1,0:T(8,128)} %edges.7) | copy-start | bytes 3145732
  0.6 7.6 %copy-start.5 = (f32[1,512,512]{2,1,0:T(8,128)S(1)}, f32[1,512,512]{2,1,0:T(8,128)}, u32[]{:S(2)}) copy-start(f32[1,512,512]{2,1,0:T(8,128)} %weight.5) | copy-start | bytes 3145732
  0.7 7.6 %copy-start.4 = (f32[1,512,512]{2,1,0:T(8,128)S(1)}, f32[1,512,512]{2,1,0:T(8,128)}, u32[]{:S(2)}) copy-start(f32[1,512,512]{2,1,0:T(8,128)} %prior.5) | copy-start | bytes 3145732
  3.2 6.5 %collective-permute-start.8 = (f32[40,512]{1,0:T(8,128)S(1)}, f32[40,512]{1,0:T(8,128)S(1)}, u32[]{:S(2)}, u32[]{:S(2)}) collective-permute-start(f32[40,512]{1,0:T(8,128)S(1)} %get-tuple-element.233), channel_id=1, source_target_pairs={{0,1},{2,3},{4,5},{6,7},{1,0},{3,2},{5,4},{7,6},{8,9},{10,11},{12,... | collective-permute-start | bytes 245768 | tf_op jit(solution)/shard_map/ppermute | solution.py:530
  5.4 5.4 %collective-permute-start.9 = (f32[40,512]{1,0:T(8,128)S(1)}, f32[40,512]{1,0:T(8,128)S(1)}, u32[]{:S(2)}, u32[]{:S(2)}) collective-permute-start(f32[40,512]{1,0:T(8,128)S(1)} %get-tuple-element.234), channel_id=1, source_target_pairs={{1,2},{3,4},{5,6},{7,0},{2,1},{4,3},{6,5},{0,7},{9,10},{11,12},{13... | collective-permute-start | bytes 245768 | tf_op jit(solution)/shard_map/ppermute | solution.py:530
  11.0 17.3 %collective-permute-start.10 = (f32[40,640]{1,0:T(8,128)S(1)}, f32[40,640]{1,0:T(8,128)S(1)}, u32[]{:S(2)}, u32[]{:S(2)}) collective-permute-start(f32[40,640]{1,0:T(8,128)S(1)} %get-tuple-element.254), channel_id=1, source_target_pairs={{0,8},{16,24},{8,0},{24,16},{1,9},{17,25},{9,1},{25,17},{2,10},{18... | collective-permute-start | bytes 307208 | tf_op jit(solution)/shard_map/ppermute | solution.py:530
  13.2 15.1 %collective-permute-start.11 = (f32[40,640]{1,0:T(8,128)S(1)}, f32[40,640]{1,0:T(8,128)S(1)}, u32[]{:S(2)}, u32[]{:S(2)}) collective-permute-start(f32[40,640]{1,0:T(8,128)S(1)} %get-tuple-element.255), channel_id=1, source_target_pairs={{8,16},{16,8},{9,17},{17,9},{10,18},{18,10},{11,19},{19,11},{12,20... | collective-permute-start | bytes 307208 | tf_op jit(solution)/shard_map/ppermute | solution.py:530

commit v8 on v7

--- a/solution.py
+++ b/solution.py
@@ -313,7 +313,7 @@
             at_rows(field[k - 1], s) if k else None,
             at_rows(er_t, s), at_rows(ed_t, s), at_rows(eu_t, s), at_rows(diag_t, s),
         )
-        for j in range(tiles):
+        for j in range(tiles if k + 1 < ITERS else inner):
             field[k + 1][j, pl.ds(s, 8), :] = new[j]
         return v[:inner], new[:inner]
 

time: 45.1 us -> 44.8 us (level)
  transfers between devices with their start and end apart: 4 -> 4, of which waited for: 1 -> 1; matrix products, arithmetic and copies ran while one was open for 0% -> 0% of each run, Pallas kernels for 27% -> 26%
where the time goes in v8:
time: 44.8 us; the launch traced here: 44.6 us
  Pallas kernels  18.7 us (42%)
  starting transfers between devices  11.8 us (26%)
  blocking collectives  11.4 us (25%)
  waiting for transfers between devices  1.06 us (2%)
  between operations  0.89 us (2%)
  loops' own time  0.82 us (2%)
    pallas_call x6, Pallas kernels, call(): pl.pallas_call(body, in_specs=in_specs, out_specs=out_specs or [VMEM] * l...  18.7 us
    all_to_all x1, blocking collectives, per_device(): every = lax.all_to_all(sums, ('row', 'col'), 0, 0, tiled=True)  11.4 us
    ppermute x2, starting transfers between devices, swaps(): lax.ppermute(second, axis, both(others))  7.38 us
    ppermute x2, starting transfers between devices, swaps(): lax.ppermute(first, axis, both(pairs))  4.38 us
    ppermute x2, waiting for transfers between devices, swaps(): lax.ppermute(second, axis, both(others))  1.06 us
  transfers between devices with their start and end apart: 4, of which 1 were waited for; matrix products, arithmetic and copies ran while one was open for 0% of the time, Pallas kernels for 26%

profile of v8, /device:TPU:1, one launch (start us, length us, event | category | flops | bytes accessed | tf_op | source)
XLA Modules:
  0.0 44.6 jit_solution(6291707764491795472)
XLA Ops:
  0.6 0.0 copy-start.1
  0.6 0.0 copy-start.5
  0.7 0.0 copy-start.4
  0.7 2.6 %shard_map.59 = (f32[40,512]{1,0:T(8,128)S(1)}, f32[40,512]{1,0:T(8,128)S(1)}, s32[4,528,128]{2,1,0:T(8,128)S(1)}) custom-call(s32[1,512,512]{2,1,0:T(8,128)} %edges.7, s32[1,512,512]{2,1,0:T(8,128)} %labels.1, f32[1,512,512]{2,1,0:T(8,128)} %prior.5, f32[1,512,512]{2,1,0:T(8,128)} %weight.5), custom_call_target="tpu_custom_call" | custom-call | flops 1048576 | bytes 1048576 | tf_op jit(solution)/shard_map/pallas_call | solution.py:534
  3.2 2.2 %collective-permute-start.8 = (f32[40,512]{1,0:T(8,128)S(1)}, f32[40,512]{1,0:T(8,128)S(1)}, u32[]{:S(2)}, u32[]{:S(2)}) collective-permute-start(f32[40,512]{1,0:T(8,128)S(1)} %get-tuple-element.233), channel_id=1, source_target_pairs={{0,1},{2,3},{4,5},{6,7},{1,0},{3,2},{5,4},{7,6},{8,9},{10,11},{12,... | collective-permute-start | bytes 245768 | tf_op jit(solution)/shard_map/ppermute | solution.py:530
  5.4 2.8 %collective-permute-start.9 = (f32[40,512]{1,0:T(8,128)S(1)}, f32[40,512]{1,0:T(8,128)S(1)}, u32[]{:S(2)}, u32[]{:S(2)}) collective-permute-start(f32[40,512]{1,0:T(8,128)S(1)} %get-tuple-element.234), channel_id=1, source_target_pairs={{1,2},{3,4},{5,6},{7,0},{2,1},{4,3},{6,5},{0,7},{9,10},{11,12},{13... | collective-permute-start | bytes 245768 | tf_op jit(solution)/shard_map/ppermute | solution.py:530
  8.3 0.0 copy-done.1
  8.3 0.0 copy-done.5
  8.3 0.0 copy-done.4
  8.3 1.5 %shard_map.60 = (f32[5,536,128]{2,1,0:T(8,128)S(1)}, f32[5,536,128]{2,1,0:T(8,128)S(1)}, f32[5,536,128]{2,1,0:T(8,128)S(1)}, f32[5,536,128]{2,1,0:T(8,128)S(1)}, f32[5,536,128]{2,1,0:T(8,128)S(1)}) custom-call(s32[1,512,512]{2,1,0:T(8,128)S(1)} %copy-done.1, s32[4,528,128]{2,1,0:T(8,128)S(1)} %get-tuple-element.232.lab_t.refs_12_, ...), custom_call_target="tpu_custom_call" | custom-call | flops 16777216 | bytes 1048576 | tf_op jit(solution)/shard_map/pallas_call | solution.py:534
  9.8 0.0 collective-permute-done.8.col_first
  9.8 1.1 %collective-permute-done.9.col_second = f32[40,512]{1,0:T(8,128)S(1)} collective-permute-done((f32[40,512]{1,0:T(8,128)S(1)}, f32[40,512]{1,0:T(8,128)S(1)}, u32[]{:S(2)}, u32[]{:S(2)}) %collective-permute-start.9) | collective-permute-done | bytes 81952 | tf_op jit(solution)/shard_map/ppermute | solution.py:530
  10.8 0.2 shard_map.62
  11.0 2.2 %collective-permute-start.10 = (f32[40,640]{1,0:T(8,128)S(1)}, f32[40,640]{1,0:T(8,128)S(1)}, u32[]{:S(2)}, u32[]{:S(2)}) collective-permute-start(f32[40,640]{1,0:T(8,128)S(1)} %get-tuple-element.254), channel_id=1, source_target_pairs={{0,8},{16,24},{8,0},{24,16},{1,9},{17,25},{9,1},{25,17},{2,10},{18... | collective-permute-start | bytes 307208 | tf_op jit(solution)/shard_map/ppermute | solution.py:530
  13.2 4.6 %collective-permute-start.11 = (f32[40,640]{1,0:T(8,128)S(1)}, f32[40,640]{1,0:T(8,128)S(1)}, u32[]{:S(2)}, u32[]{:S(2)}) collective-permute-start(f32[40,640]{1,0:T(8,128)S(1)} %get-tuple-element.255), channel_id=1, source_target_pairs={{8,16},{16,8},{9,17},{17,9},{10,18},{18,10},{11,19},{19,11},{12,20... | collective-permute-start | bytes 307208 | tf_op jit(solution)/shard_map/ppermute | solution.py:530
  17.8 10.2 %shard_map.61 = (f32[5,536,128]{2,1,0:T(8,128)S(1)}, f32[5,536,128]{2,1,0:T(8,128)S(1)}, f32[5,536,128]{2,1,0:T(8,128)S(1)}, f32[5,536,128]{2,1,0:T(8,128)S(1)},...) custom-call(s32[1,512,512]{2,1,0:T(8,128)S(1)} %copy-done.1, ...), custom_call_target="tpu_custom_call", output_to_operand_aliasing={{0}: (4, {}), {1}: (5, {}), {2}: (6, {}), {3}: (7, {}), {4}... | custom-call | flops 67108864 | bytes 1048576 | tf_op jit(solution)/shard_map/pallas_call | solution.py:534
  28.0 0.0 collective-permute-done.10.refs_15_
  28.0 0.0 collective-permute-done.11.refs_16_
  28.0 1.0 %shard_map.63 = (f32[32,1,128]{2,1,0:T(1,128)S(1)}, f32[9,2,4,16,128]{4,3,2,1,0:T(8,128)S(1)}) custom-call(f32[5,536,128]{2,1,0:T(8,128)S(1)} %get-tuple-element.240.refs_0_, f32[5,536,128]{2,1,0:T(8,128)S(1)} %get-tuple-element.241.refs_1_, f32[5,536,128]{2,1,0:T(8,128)S(1)} %get-tuple-element.242.refs_2_, f32[5,536,128]{2,1,0:T(8,128)S(1)} %get-tuple-element.243.refs_3_, ...), custom_call_target="tpu_custom_call" | custom-call | flops 1048576 | bytes 1048576 | tf_op jit(solution)/shard_map/pallas_call | solution.py:534
  29.0 11.4 %all_to_all.31.every = f32[32,1,128]{2,1,0:T(1,128)S(1)} all-to-all(f32[32,1,128]{2,1,0:T(1,128)S(1)} %get-tuple-element.256), channel_id=1, replica_groups=mesh['img'=4,'row'=4,'col'=8] {'row','col'}, dimensions={0} | all-to-all | bytes 32768 | tf_op jit(solution)/shard_map/all_to_all | solution.py:594
  40.4 3.2 %shard_map.64 = (f32[1,512,512]{2,1,0:T(8,128)}, f32[1,512,512]{2,1,0:T(8,128)}, s32[1,1]{1,0:T(1,128)}) custom-call(f32[32,1,128]{2,1,0:T(1,128)S(1)} %all_to_all.31.every, s32[4,528,128]{2,1,0:T(8,128)S(1)} %get-tuple-element.232.lab_t.refs_12_, f32[9,2,4,16,128]{4,3,2,1,0:T(8,128)S(1)} %get-tuple-element.257.edge, ...), custom_call_target="tpu_custom_call" | custom-call | flops 1048576 | bytes 1048576 | tf_op jit(solution)/shard_map/pallas_call | solution.py:534
  43.7 0.8 %while.30 = (s32[]{:T(128)}, f32[1,512,512]{2,1,0:T(8,128)}, f32[1,512,512]{2,1,0:T(8,128)}, s32[1,512,512]{2,1,0:T(8,128)}, f32[1,512,512]{2,1,0:T(8,128)}, /*i...) while((s32[]{:T(128)}, f32[1,512,512]{2,1,0:T(8,128)}, f32[1,512,512]{2,1,0:T(8,128)}, ...), condition=%region_9.10_spmd, body=%region_0.9_spmd | while | flops 58720352 | bytes 45852768 | solution.py:606
Async XLA Ops:
  0.6 7.6 %copy-start.1 = (s32[1,512,512]{2,1,0:T(8,128)S(1)}, s32[1,512,512]{2,1,0:T(8,128)}, u32[]{:S(2)}) copy-start(s32[1,512,512]{2,1,0:T(8,128)} %edges.7) | copy-start | bytes 3145732
  0.6 7.6 %copy-start.5 = (f32[1,512,512]{2,1,0:T(8,128)S(1)}, f32[1,512,512]{2,1,0:T(8,128)}, u32[]{:S(2)}) copy-start(f32[1,512,512]{2,1,0:T(8,128)} %weight.5) | copy-start | bytes 3145732
  0.7 7.6 %copy-start.4 = (f32[1,512,512]{2,1,0:T(8,128)S(1)}, f32[1,512,512]{2,1,0:T(8,128)}, u32[]{:S(2)}) copy-start(f32[1,512,512]{2,1,0:T(8,128)} %prior.5) | copy-start | bytes 3145732
  3.2 6.5 %collective-permute-start.8 = (f32[40,512]{1,0:T(8,128)S(1)}, f32[40,512]{1,0:T(8,128)S(1)}, u32[]{:S(2)}, u32[]{:S(2)}) collective-permute-start(f32[40,512]{1,0:T(8,128)S(1)} %get-tuple-element.233), channel_id=1, source_target_pairs={{0,1},{2,3},{4,5},{6,7},{1,0},{3,2},{5,4},{7,6},{8,9},{10,11},{12,... | collective-permute-start | bytes 245768 | tf_op jit(solution)/shard_map/ppermute | solution.py:530
  5.4 5.4 %collective-permute-start.9 = (f32[40,512]{1,0:T(8,128)S(1)}, f32[40,512]{1,0:T(8,128)S(1)}, u32[]{:S(2)}, u32[]{:S(2)}) collective-permute-start(f32[40,512]{1,0:T(8,128)S(1)} %get-tuple-element.234), channel_id=1, source_target_pairs={{1,2},{3,4},{5,6},{7,0},{2,1},{4,3},{6,5},{0,7},{9,10},{11,12},{13... | collective-permute-start | bytes 245768 | tf_op jit(solution)/shard_map/ppermute | solution.py:530
  11.0 17.0 %collective-permute-start.10 = (f32[40,640]{1,0:T(8,128)S(1)}, f32[40,640]{1,0:T(8,128)S(1)}, u32[]{:S(2)}, u32[]{:S(2)}) collective-permute-start(f32[40,640]{1,0:T(8,128)S(1)} %get-tuple-element.254), channel_id=1, source_target_pairs={{0,8},{16,24},{8,0},{24,16},{1,9},{17,25},{9,1},{25,17},{2,10},{18... | collective-permute-start | bytes 307208 | tf_op jit(solution)/shard_map/ppermute | solution.py:530
  13.2 14.8 %collective-permute-start.11 = (f32[40,640]{1,0:T(8,128)S(1)}, f32[40,640]{1,0:T(8,128)S(1)}, u32[]{:S(2)}, u32[]{:S(2)}) collective-permute-start(f32[40,640]{1,0:T(8,128)S(1)} %get-tuple-element.255), channel_id=1, source_target_pairs={{8,16},{16,8},{9,17},{17,9},{10,18},{18,10},{11,19},{19,11},{12,20... | collective-permute-start | bytes 307208 | tf_op jit(solution)/shard_map/ppermute | solution.py:530
